TPU v7x, 128 devices: a whole 4x4x4 slice. The times are simulated.
128 devices in a mesh: py: 8 (over z, x_hi), px: 4 (over y_hi, core), pz: 4 (over y_lo, x_lo).
Axes of the slice: x: 4 (x_hi: 2, x_lo: 2; x = x_hi * 2 + x_lo), y: 4 (y_hi: 2, y_lo: 2; y = y_hi * 2 + y_lo), z: 4, core: 2. Of those that a mesh axis runs over, the one named last changes fastest.
Arguments:
- initial_density: float32 [32, 256, 384, 128], P('py', 'px', 'pz'), may hold values from 0.2 to 1.8
- inverse_limit: float32 [32, 256, 384, 128], P('py', 'px', 'pz'), may hold values from 0.5 to 2
Outputs:
- temperature_end: float32 [32, 256, 384, 128], P('py', 'px', 'pz')
All inputs are finite; a program needn't handle non-finite values.
Results may differ from a plain program's by a relative error of at most 0.00002.
Values sent between devices are 32-bit elements; how exact they have to be, the bound alone decides.
No kernel may reach another device: no remote copies, remote signals or barrier semaphores. Data moves between devices by JAX's collectives and lax.ppermute only.
A program may use at most 384 MiB of HBM per device.

v0:
```python
import jax
import jax.numpy as jnp
from jax import lax
from jax.sharding import PartitionSpec as P

STEPS = 3


def extended(x, sides, width):
    edges = {}
    for axis, dim in sides:
        peers, length = (lax.axis_size(axis), x.shape[dim])
        up = [(i, (i + 1) % peers) for i in range(peers - 1)]
        last = lax.slice_in_dim(x, length - width, length, axis=dim)
        leading = lax.slice_in_dim(x, 0, width, axis=dim)
        edges[dim] = (
            lax.ppermute(last, axis, up),
            lax.ppermute(leading, axis, [(b, a) for a, b in up]),
        )
    done = []
    for _, dim in sides:
        low, high = edges[dim]
        around = [(width, width) if d in done else (0, 0) for d in range(x.ndim)]
        x = jnp.concatenate([jnp.pad(low, around), x, jnp.pad(high, around)], axis=dim)
        done.append(dim)
    return x


def inner_cells(values, dims):
    for dim in dims:
        values = lax.slice_in_dim(values, 1, values.shape[dim] - 1, axis=dim)
    return values


def boundary_cells(values, dim, start, dims):
    remaining_parts = [other for other in dims if other != dim]
    values = inner_cells(values, remaining_parts)
    return lax.slice_in_dim(values, start, start + values.shape[dim] - 2, axis=dim)


def advance_population(haloed_population, inverse_limit):
    middle = inner_cells(haloed_population, (0, 1, 2))
    lower = [boundary_cells(haloed_population, dim, 0, (0, 1, 2)) for dim in (0, 1, 2)]
    upper = [boundary_cells(haloed_population, dim, 2, (0, 1, 2)) for dim in (0, 1, 2)]
    spread = lower[0] + upper[0] + lower[1] + upper[1] + lower[2] + upper[2] - 6.0 * middle
    return middle + 0.1 * spread + 0.2 * middle * (1.0 - middle * inverse_limit)


def local(initial_density, inverse_limit):
    for step in range(STEPS):
        haloed_population = extended(initial_density, (("py", 0), ("px", 1), ("pz", 2)), 1)
        initial_density = advance_population(haloed_population, inverse_limit)
    return initial_density


def solution(mesh):
    in_specs = (P("py", "px", "pz", None), P("py", "px", "pz", None))
    out_specs = P("py", "px", "pz", None)
    return jax.shard_map(local, mesh=mesh, in_specs=in_specs, out_specs=out_specs, check_vma=False)
```

profile of v0, /device:TPU:20, one launch (start us, length us, event | category | flops | bytes accessed | tf_op | source)
XLA Modules:
  0.0 584.3 jit_solution(3034799448884535832)
XLA Ops:
  0.0 5.0 fusion.41
  5.0 3.8 collective-permute-start
  8.7 3.8 collective-permute-start.1
  13.6 1.9 collective-permute-start.2
  15.5 5.1 collective-permute-start.3
  20.6 2.4 fusion.39
  24.4 5.2 collective-permute-start.4
  30.4 48.9 %collective-permute-done = f32[1,64,96,128]{3,2,1,0:T(8,128)S(1)} collective-permute-done((f32[1,64,96,128]{3,2,1,0:T(8,128)S(1)}, f32[1,64,96,128]{3,2,1,0:T(8,128)S(1)}, u32[]{:S(2)}, u32[]{:S(2)}) %collective-permute-start) | collective-permute-done | bytes 3145760 | tf_op jit(solution)/shard_map/ppermute | solution.py:17
  79.3 1.8 constant_dynamic-update-slice_fusion.2
  81.1 10.3 %constant_dynamic-update-slice_fusion.1 = f32[6,64,96,128]{3,2,1,0:T(8,128)} fusion(f32[6,64,96,128]{3,2,1,0:T(8,128)} %constant_dynamic-update-slice_fusion.2, f32[4,64,96,128]{3,2,1,0:T(8,128)} %param.2), kind=kLoop, calls=%fused_computation.82 | loop fusion | bytes 25165824
  91.5 56.6 %collective-permute-done.1 = f32[1,64,96,128]{3,2,1,0:T(8,128)S(1)} collective-permute-done((f32[1,64,96,128]{3,2,1,0:T(8,128)}, f32[1,64,96,128]{3,2,1,0:T(8,128)S(1)}, u32[]{:S(2)}, u32[]{:S(2)}) %collective-permute-start.1) | collective-permute-done | bytes 3145760 | tf_op jit(solution)/shard_map/ppermute | solution.py:18
  149.8 1.9 constant_dynamic-update-slice_fusion
  151.7 41.2 %fusion.27 = f32[4,64,96,128]{3,2,1,0:T(8,128)} fusion(f32[4,64,96,128]{3,2,1,0:T(8,128)} %param.2, f32[4,64,1,128]{3,2,1,0:T(1,128)} %bitcast.11, f32[6,1,96,128]{3,2,1,0:T(8,128)} %pad.39, f32[6,64,96,128]{3,2,1,0:T(8,128)} %constant_dynamic-update-slice_fusion, f32[6,1,96,128]{3,2,1,0:T(8,128)S(1)} %pad.38, f32[4,64,1,128]{3,2,1,0:T(1,128)} %bitcast.9, ...), kind=kLoop, calls=%fused_computation.64 | loop fusion | flops 94371840 | bytes 63766528 | tf_op jit(solution)/shard_map/add | solution.py:46
  192.9 3.3 fusion.37
  196.2 3.8 collective-permute-start.6
  199.9 3.8 collective-permute-start.7
  204.8 1.9 collective-permute-start.8
  206.7 5.1 collective-permute-start.9
  211.9 1.7 fusion.36
  213.6 3.1 collective-permute-start.10
  219.0 116.5 %collective-permute-done.10 = f32[4,64,1,128]{3,1,2,0:T(8,128)S(1)} collective-permute-done((f32[4,64,1,128]{3,1,2,0:T(8,128)S(1)}, f32[4,64,1,128]{3,1,2,0:T(8,128)S(1)}, u32[]{:S(2)}, u32[]{:S(2)}) %collective-permute-start.10) | collective-permute-done | bytes 131104 | tf_op jit(solution)/shard_map/ppermute | solution.py:17
  335.5 5.4 collective-permute-done.11
  342.5 45.1 %fusion.16 = f32[4,64,96,128]{3,2,1,0:T(8,128)} fusion(f32[4,64,96,128]{3,2,1,0:T(8,128)} %fusion.27, f32[4,64,1,128]{3,2,1,0:T(1,128)} %bitcast.15, f32[6,1,96,128]{3,2,1,0:T(8,128)} %pad.43, f32[6,1,96,128]{3,2,1,0:T(8,128)S(1)} %pad.42, f32[1,64,96,128]{3,2,1,0:T(8,128)} %copy-done.2, f32[1,64,96,128]{3,2,1,0:T(8,128)S(1)} %collective-permute-done.6, ...), kind=kLoop, calls=%fused_computation.35 | loop fusion | flops 119537664 | bytes 44892160 | tf_op jit(solution)/shard_map/add | solution.py:46
  387.6 3.3 fusion.34
  390.9 3.4 collective-permute-start.12
  394.3 4.1 collective-permute-start.13
  399.5 1.9 collective-permute-start.14
  401.4 5.1 collective-permute-start.15
  408.3 3.9 collective-permute-start.16
  414.3 114.6 %collective-permute-done.16 = f32[4,64,1,128]{3,1,2,0:T(8,128)S(1)} collective-permute-done((f32[4,64,1,128]{3,1,2,0:T(8,128)S(1)}, f32[4,64,1,128]{3,1,2,0:T(8,128)S(1)}, u32[]{:S(2)}, u32[]{:S(2)}) %collective-permute-start.16) | collective-permute-done | bytes 131104 | tf_op jit(solution)/shard_map/ppermute | solution.py:17
  528.9 8.4 %collective-permute-done.17 = f32[4,64,1,128]{3,1,2,0:T(8,128)S(1)} collective-permute-done((f32[4,64,1,128]{3,1,2,0:T(8,128)S(1)}, f32[4,64,1,128]{3,1,2,0:T(8,128)S(1)}, u32[]{:S(2)}, u32[]{:S(2)}) %collective-permute-start.17) | collective-permute-done | bytes 131104 | tf_op jit(solution)/shard_map/ppermute | solution.py:18
  539.0 45.2 %fusion.5 = f32[4,64,96,128]{3,2,1,0:T(8,128)} fusion(f32[4,64,96,128]{3,2,1,0:T(8,128)} %fusion.16, f32[4,64,1,128]{3,2,1,0:T(1,128)} %bitcast.14, f32[6,1,96,128]{3,2,1,0:T(8,128)} %pad.47, f32[6,1,96,128]{3,2,1,0:T(8,128)S(1)} %pad.46, f32[1,64,96,128]{3,2,1,0:T(8,128)} %copy-done.1, f32[1,64,96,128]{3,2,1,0:T(8,128)S(1)} %collective-permute-done.12, ...), kind=kLoop, calls=%fused_computation.6 | loop fusion | flops 119537664 | bytes 44892160 | tf_op jit(solution)/shard_map/add | solution.py:46
  (39 shorter events, 16.3 us)
Async XLA Ops:
  5.0 74.4 %collective-permute-start = (f32[1,64,96,128]{3,2,1,0:T(8,128)S(1)}, f32[1,64,96,128]{3,2,1,0:T(8,128)S(1)}, u32[]{:S(2)}, u32[]{:S(2)}) collective-permute-start(f32[1,64,96,128]{3,2,1,0:T(8,128)S(1)} %get-tuple-element.22), channel_id=1, source_target_pairs={{0,16},{16,32},{32,48},{48,64},{64,80},{80,96},{96,112},{1,17},{17... | collective-permute-start | bytes 9437192 | tf_op jit(solution)/shard_map/ppermute | solution.py:17
  8.7 139.4 %collective-permute-start.1 = (f32[1,64,96,128]{3,2,1,0:T(8,128)}, f32[1,64,96,128]{3,2,1,0:T(8,128)S(1)}, u32[]{:S(2)}, u32[]{:S(2)}) collective-permute-start(f32[1,64,96,128]{3,2,1,0:T(8,128)} %get-tuple-element.21), channel_id=1, source_target_pairs={{16,0},{32,16},{48,32},{64,48},{80,64},{96,80},{112,96},{17,1},{33... | collective-permute-start | bytes 9437192 | tf_op jit(solution)/shard_map/ppermute | solution.py:18
  13.6 10.8 %collective-permute-start.2 = (f32[4,1,96,128]{3,2,1,0:T(8,128)S(1)}, f32[4,1,96,128]{3,2,1,0:T(8,128)S(1)}, u32[]{:S(2)}, u32[]{:S(2)}) collective-permute-start(f32[4,1,96,128]{3,2,1,0:T(8,128)S(1)} %get-tuple-element.19), channel_id=1, source_target_pairs={{0,4},{4,8},{8,12},{1,5},{5,9},{9,13},{2,6},{6,10},{10,14},{3,7},{... | collective-permute-start | bytes 589832 | tf_op jit(solution)/shard_map/ppermute | solution.py:17
  15.5 14.1 %collective-permute-start.3 = (f32[4,1,96,128]{3,2,1,0:T(8,128)S(1)}, f32[4,1,96,128]{3,2,1,0:T(8,128)S(1)}, u32[]{:S(2)}, u32[]{:S(2)}) collective-permute-start(f32[4,1,96,128]{3,2,1,0:T(8,128)S(1)} %get-tuple-element.20), channel_id=1, source_target_pairs={{4,0},{8,4},{12,8},{5,1},{9,5},{13,9},{6,2},{10,6},{14,10},{7,3},{... | collective-permute-start | bytes 589832 | tf_op jit(solution)/shard_map/ppermute | solution.py:18
  23.1 128.6 %collective-permute-start.5 = (f32[4,64,1,128]{3,1,2,0:T(8,128)}, f32[4,64,1,128]{3,1,2,0:T(8,128)}, u32[]{:S(2)}, u32[]{:S(2)}) collective-permute-start(f32[4,64,1,128]{3,1,2,0:T(8,128)} %bitcast.10), channel_id=1, source_target_pairs={{1,0},{2,1},{3,2},{5,4},{6,5},{7,6},{9,8},{10,9},{11,10},{13,12},{... | collective-permute-start | bytes 393224 | tf_op jit(solution)/shard_map/ppermute | solution.py:18
  24.4 127.3 %collective-permute-start.4 = (f32[4,64,1,128]{3,1,2,0:T(8,128)}, f32[4,64,1,128]{3,1,2,0:T(8,128)}, u32[]{:S(2)}, u32[]{:S(2)}) collective-permute-start(f32[4,64,1,128]{3,1,2,0:T(8,128)} %bitcast.8), channel_id=1, source_target_pairs={{0,1},{1,2},{2,3},{4,5},{5,6},{6,7},{8,9},{9,10},{10,11},{12,13},{... | collective-permute-start | bytes 393224 | tf_op jit(solution)/shard_map/ppermute | solution.py:17
  148.1 1.7 copy-start
  196.2 144.7 %collective-permute-start.6 = (f32[1,64,96,128]{3,2,1,0:T(8,128)S(1)}, f32[1,64,96,128]{3,2,1,0:T(8,128)S(1)}, u32[]{:S(2)}, u32[]{:S(2)}) collective-permute-start(f32[1,64,96,128]{3,2,1,0:T(8,128)S(1)} %get-tuple-element.13), channel_id=1, source_target_pairs={{0,16},{16,32},{32,48},{48,64},{64,80},{80,96},{96,112},{1,17},{17... | collective-permute-start | bytes 9437192 | tf_op jit(solution)/shard_map/ppermute | solution.py:17
  199.9 140.9 %collective-permute-start.7 = (f32[1,64,96,128]{3,2,1,0:T(8,128)S(1)}, f32[1,64,96,128]{3,2,1,0:T(8,128)S(1)}, u32[]{:S(2)}, u32[]{:S(2)}) collective-permute-start(f32[1,64,96,128]{3,2,1,0:T(8,128)S(1)} %get-tuple-element.14), channel_id=1, source_target_pairs={{16,0},{32,16},{48,32},{64,48},{80,64},{96,80},{112,96},{17,1},{33... | collective-permute-start | bytes 9437192 | tf_op jit(solution)/shard_map/ppermute | solution.py:18
  204.8 11.9 %collective-permute-start.8 = (f32[4,1,96,128]{3,2,1,0:T(8,128)S(1)}, f32[4,1,96,128]{3,2,1,0:T(8,128)S(1)}, u32[]{:S(2)}, u32[]{:S(2)}) collective-permute-start(f32[4,1,96,128]{3,2,1,0:T(8,128)S(1)} %get-tuple-element.15), channel_id=1, source_target_pairs={{0,4},{4,8},{8,12},{1,5},{5,9},{9,13},{2,6},{6,10},{10,14},{3,7},{... | collective-permute-start | bytes 589832 | tf_op jit(solution)/shard_map/ppermute | solution.py:17
  206.7 11.5 %collective-permute-start.9 = (f32[4,1,96,128]{3,2,1,0:T(8,128)S(1)}, f32[4,1,96,128]{3,2,1,0:T(8,128)S(1)}, u32[]{:S(2)}, u32[]{:S(2)}) collective-permute-start(f32[4,1,96,128]{3,2,1,0:T(8,128)S(1)} %get-tuple-element.16), channel_id=1, source_target_pairs={{4,0},{8,4},{12,8},{5,1},{9,5},{13,9},{6,2},{10,6},{14,10},{7,3},{... | collective-permute-start | bytes 589832 | tf_op jit(solution)/shard_map/ppermute | solution.py:18
  213.6 121.9 %collective-permute-start.10 = (f32[4,64,1,128]{3,1,2,0:T(8,128)S(1)}, f32[4,64,1,128]{3,1,2,0:T(8,128)S(1)}, u32[]{:S(2)}, u32[]{:S(2)}) collective-permute-start(f32[4,64,1,128]{3,1,2,0:T(8,128)S(1)} %bitcast.19), channel_id=1, source_target_pairs={{0,1},{1,2},{2,3},{4,5},{5,6},{6,7},{8,9},{9,10},{10,11},{12,13},{... | collective-permute-start | bytes 393224 | tf_op jit(solution)/shard_map/ppermute | solution.py:17
  216.7 124.1 %collective-permute-start.11 = (f32[4,64,1,128]{3,1,2,0:T(8,128)S(1)}, f32[4,64,1,128]{3,1,2,0:T(8,128)S(1)}, u32[]{:S(2)}, u32[]{:S(2)}) collective-permute-start(f32[4,64,1,128]{3,1,2,0:T(8,128)S(1)} %bitcast.17), channel_id=1, source_target_pairs={{1,0},{2,1},{3,2},{5,4},{6,5},{7,6},{9,8},{10,9},{11,10},{13,12},{... | collective-permute-start | bytes 393224 | tf_op jit(solution)/shard_map/ppermute | solution.py:18
  335.5 7.0 %copy-start.4 = (f32[4,64,1,128]{3,1,2,0:T(8,128)}, f32[4,64,1,128]{3,1,2,0:T(8,128)S(1)}, u32[]{:S(2)}) copy-start(f32[4,64,1,128]{3,1,2,0:T(8,128)S(1)} %collective-permute-done.10) | copy-start | bytes 393220
  340.9 1.7 copy-start.6
  340.9 1.7 copy-start.2
  390.9 146.4 %collective-permute-start.12 = (f32[1,64,96,128]{3,2,1,0:T(8,128)S(1)}, f32[1,64,96,128]{3,2,1,0:T(8,128)S(1)}, u32[]{:S(2)}, u32[]{:S(2)}) collective-permute-start(f32[1,64,96,128]{3,2,1,0:T(8,128)S(1)} %get-tuple-element.7), channel_id=1, source_target_pairs={{0,16},{16,32},{32,48},{48,64},{64,80},{80,96},{96,112},{1,17},{17... | collective-permute-start | bytes 9437192 | tf_op jit(solution)/shard_map/ppermute | solution.py:17
  394.3 143.0 %collective-permute-start.13 = (f32[1,64,96,128]{3,2,1,0:T(8,128)S(1)}, f32[1,64,96,128]{3,2,1,0:T(8,128)S(1)}, u32[]{:S(2)}, u32[]{:S(2)}) collective-permute-start(f32[1,64,96,128]{3,2,1,0:T(8,128)S(1)} %get-tuple-element.8), channel_id=1, source_target_pairs={{16,0},{32,16},{48,32},{64,48},{80,64},{96,80},{112,96},{17,1},{33... | collective-permute-start | bytes 9437192 | tf_op jit(solution)/shard_map/ppermute | solution.py:18
  399.5 12.7 %collective-permute-start.14 = (f32[4,1,96,128]{3,2,1,0:T(8,128)S(1)}, f32[4,1,96,128]{3,2,1,0:T(8,128)S(1)}, u32[]{:S(2)}, u32[]{:S(2)}) collective-permute-start(f32[4,1,96,128]{3,2,1,0:T(8,128)S(1)} %get-tuple-element.9), channel_id=1, source_target_pairs={{0,4},{4,8},{8,12},{1,5},{5,9},{9,13},{2,6},{6,10},{10,14},{3,7},{... | collective-permute-start | bytes 589832 | tf_op jit(solution)/shard_map/ppermute | solution.py:17
  401.4 12.1 %collective-permute-start.15 = (f32[4,1,96,128]{3,2,1,0:T(8,128)S(1)}, f32[4,1,96,128]{3,2,1,0:T(8,128)S(1)}, u32[]{:S(2)}, u32[]{:S(2)}) collective-permute-start(f32[4,1,96,128]{3,2,1,0:T(8,128)S(1)} %get-tuple-element.10), channel_id=1, source_target_pairs={{4,0},{8,4},{12,8},{5,1},{9,5},{13,9},{6,2},{10,6},{14,10},{7,3},{... | collective-permute-start | bytes 589832 | tf_op jit(solution)/shard_map/ppermute | solution.py:18
  408.3 120.6 %collective-permute-start.16 = (f32[4,64,1,128]{3,1,2,0:T(8,128)S(1)}, f32[4,64,1,128]{3,1,2,0:T(8,128)S(1)}, u32[]{:S(2)}, u32[]{:S(2)}) collective-permute-start(f32[4,64,1,128]{3,1,2,0:T(8,128)S(1)} %bitcast.18), channel_id=1, source_target_pairs={{0,1},{1,2},{2,3},{4,5},{5,6},{6,7},{8,9},{9,10},{10,11},{12,13},{... | collective-permute-start | bytes 393224 | tf_op jit(solution)/shard_map/ppermute | solution.py:17
  412.2 125.1 %collective-permute-start.17 = (f32[4,64,1,128]{3,1,2,0:T(8,128)S(1)}, f32[4,64,1,128]{3,1,2,0:T(8,128)S(1)}, u32[]{:S(2)}, u32[]{:S(2)}) collective-permute-start(f32[4,64,1,128]{3,1,2,0:T(8,128)S(1)} %bitcast.16), channel_id=1, source_target_pairs={{1,0},{2,1},{3,2},{5,4},{6,5},{7,6},{9,8},{10,9},{11,10},{13,12},{... | collective-permute-start | bytes 393224 | tf_op jit(solution)/shard_map/ppermute | solution.py:18
  528.9 10.0 %copy-start.3 = (f32[4,64,1,128]{3,1,2,0:T(8,128)}, f32[4,64,1,128]{3,1,2,0:T(8,128)S(1)}, u32[]{:S(2)}) copy-start(f32[4,64,1,128]{3,1,2,0:T(8,128)S(1)} %collective-permute-done.16) | copy-start | bytes 393220
  537.3 1.7 copy-start.5
  537.3 1.7 copy-start.1
where the time goes:
time: 585 us; the launch traced here: 584 us
  waiting for transfers between devices  350 us (60%)
  other arithmetic  131 us (22%)
  starting transfers between devices  60 us (10%)
  local copies, waits for them, and re-layouts  42 us (7%)
    ppermute x9, waiting for transfers between devices, extended(): lax.ppermute(last, axis, up)  280 us
    add x3, other arithmetic, advance_population(): return middle + 0.1 * spread + 0.2 * middle * (1.0 - middle * inverse_limit)  131 us
    ppermute x9, waiting for transfers between devices, extended(): lax.ppermute(leading, axis, [(b, a) for a, b in up])  70.3 us
    ppermute x9, starting transfers between devices, extended(): lax.ppermute(leading, axis, [(b, a) for a, b in up])  31.1 us
    ppermute x9, starting transfers between devices, extended(): lax.ppermute(last, axis, up)  28.9 us
    unnamed x16, local copies, waits for them, and re-layouts  17.2 us
    slice x8, local copies, waits for them, and re-layouts, extended(): last = lax.slice_in_dim(x, length - width, length, axis=dim)  15.7 us
  transfers between devices with their start and end apart: 18, of which 6 were waited for; matrix products, arithmetic and copies ran while one was open for 4% of the time, Pallas kernels for 0%

commit v1 on v0

v1 whole, which is shorter than its diff:
```python
import functools

import jax
import jax.numpy as jnp
from jax import lax
from jax.experimental import pallas as pl
from jax.experimental.pallas import tpu as pltpu
from jax.sharding import PartitionSpec as P


STEPS = 3
ROWS = 8
TILE = 16
DIRECT = 48

EVEN_CUTS = [(0, 1), (1, 0), (2, 3), (3, 2), (4, 5), (5, 4), (6, 7), (7, 6)]
ODD_CUTS = [(1, 2), (2, 1), (3, 4), (4, 3), (5, 6), (6, 5)]
RELAYS = [
    ([(2, 0), (5, 7)], [(0, 1), (7, 6)]),
    ([(4, 0), (3, 7)], [(0, 3), (7, 4)]),
    ([(6, 0), (1, 7)], [(0, 5), (7, 2)]),
]
VMEM = 20 * 1024 * 1024


def struct(*shape):
    return jax.ShapeDtypeStruct(shape, jnp.float32)


def fixed(*shape):
    return pl.BlockSpec(shape, lambda i, *_: (0,) * len(shape))


def partial_kernel(first, last, odd_ref, *refs):
    planes = [refs[3 * s : 3 * s + 3] for s in range(4)]
    inverse, px_low, px_high, pz_low, pz_high = refs[12:17]
    part_o, part_e, kept, mx_low, mx_high, mz_low, mz_high = (refs[17:] + (None,) * 4)[:7]
    i, blocks = pl.program_id(0), pl.num_programs(0)
    odd = odd_ref[0]
    shape = px_low.shape[1:]
    depth = shape[0]
    z = lax.broadcasted_iota(jnp.int32, shape, 0)

    def stored(s):
        return jnp.where(odd == 1, 3 - s, s)

    def edge(s):
        return stored(s) if first else s

    def main(s, r):
        ref = planes[s][0]
        return ref[r] if len(ref.shape) == 3 else ref[0, r]

    def one_row(r, before, after):
        for s in range(4):
            c = main(s, r)
            below = jnp.where(z == 0, pz_low[edge(s), pl.ds(r, 1), :], pltpu.roll(c, 1, 0))
            above = jnp.where(z == depth - 1, pz_high[edge(s), pl.ds(r, 1), :], pltpu.roll(c, depth - 1, 0))
            total = (before(s) + after(s)) + (below + above)
            if s > 0:
                total = total + main(s - 1, r)
            if s < 3:
                total = total + main(s + 1, r)
            value = c * (0.6 - 0.2 * c * inverse[stored(s), r]) + 0.1 * total
            if s == 0:
                part_o[r] = value
            elif s == 3:
                part_e[r] = value
            elif last:
                kept[stored(s), r] = value
            else:
                kept[s - 1, r] = value
                mz_low[s - 1, pl.ds(r, 1), :] = value[0:1, :]
                mz_high[s - 1, pl.ds(r, 1), :] = value[depth - 1 : depth, :]

    def earlier(s):
        return jnp.where(i == 0, px_low[edge(s)], planes[s][1][...].reshape(shape))

    def later(s):
        return jnp.where(i == blocks - 1, px_high[edge(s)], planes[s][2][...].reshape(shape))

    one_row(0, earlier, lambda s: main(s, 1))

    @pl.loop(1, ROWS - 1)
    def _(r):
        one_row(r, lambda s: main(s, r - 1), lambda s: main(s, r + 1))

    one_row(ROWS - 1, lambda s: main(s, ROWS - 2), later)
    if not last:

        @pl.when(i == 0)
        def _():
            mx_low[...] = kept[:, 0]

        @pl.when(i == blocks - 1)
        def _():
            mx_high[...] = kept[:, ROWS - 1]


def partial_step(step, odd, o, mid, e, inverse, px, pz):
    first, last = step == 0, step == STEPS - 1
    rows, depth, levels = o.shape

    def specs(plane):
        if plane is None:
            shape, at = (lambda k: (k, depth, levels)), (lambda j, odd_ref: (j, 0, 0))
        else:
            shape, at = (lambda k: (1, k, depth, levels)), (lambda j, odd_ref: (plane(odd_ref), j, 0, 0))
        return [
            pl.BlockSpec(shape(ROWS), lambda i, odd_ref: at(i, odd_ref)),
            pl.BlockSpec(shape(1), lambda i, odd_ref: at(jnp.maximum(i * ROWS - 1, 0), odd_ref)),
            pl.BlockSpec(shape(1), lambda i, odd_ref: at(jnp.minimum(i * ROWS + ROWS, rows - 1), odd_ref)),
        ]

    def middle(s):
        if first:
            return lambda odd_ref: jnp.where(odd_ref[0] == 1, 3 - s, s)
        return lambda odd_ref: s - 1

    def block(planes):
        return pl.BlockSpec((planes, ROWS, depth, levels), lambda i, odd_ref: (0, i, 0, 0))

    def ends(planes):
        return pl.BlockSpec((planes, ROWS, levels), lambda i, odd_ref: (0, i, 0))

    face = pl.BlockSpec((ROWS, depth, levels), lambda i, odd_ref: (i, 0, 0))
    out_specs = [face, face, block(4 if last else 2)]
    out_shape = [struct(*o.shape), struct(*o.shape), struct(4 if last else 2, *o.shape)]
    if not last:
        out_specs += [fixed(2, depth, levels)] * 2 + [ends(2)] * 2
        out_shape += [struct(2, depth, levels)] * 2 + [struct(2, rows, levels)] * 2
    return pl.pallas_call(
        functools.partial(partial_kernel, first, last),
        grid_spec=pltpu.PrefetchScalarGridSpec(
            num_scalar_prefetch=1,
            grid=(rows // ROWS,),
            in_specs=specs(None)
            + specs(middle(1))
            + specs(middle(2))
            + specs(None)
            + [block(4), fixed(4, depth, levels), fixed(4, depth, levels), ends(4), ends(4)],
            out_specs=out_specs,
        ),
        out_shape=out_shape,
        compiler_params=pltpu.CompilerParams(vmem_limit_bytes=VMEM),
        cost_estimate=pl.CostEstimate(flops=60_000_000, bytes_accessed=40_000_000, transcendentals=0),
        name="partial_step",
    )(odd, *([o] * 3), *([mid] * 6), *([e] * 3), inverse, *px, *pz)


def finish_even_kernel(part, halo, face, x_ends, z_ends):
    i, blocks = pl.program_id(0), pl.num_programs(0)
    depth = face.shape[1]
    face[...] = part[...] + 0.1 * halo[...]
    z_ends[0] = face[:, 0, :]
    z_ends[1] = face[:, depth - 1, :]

    @pl.when(i == 0)
    def _():
        x_ends[0] = face[0]

    @pl.when(i == blocks - 1)
    def _():
        x_ends[1] = face[TILE - 1]


def finish_even(part, halo):
    rows, depth, levels = part.shape
    face = pl.BlockSpec((TILE, depth, levels), lambda i: (i, 0, 0))
    return pl.pallas_call(
        finish_even_kernel,
        grid=(rows // TILE,),
        in_specs=[face, face],
        out_specs=[face, fixed(2, depth, levels), pl.BlockSpec((2, TILE, levels), lambda i: (0, i, 0))],
        out_shape=[struct(*part.shape), struct(2, depth, levels), struct(2, rows, levels)],
        compiler_params=pltpu.CompilerParams(vmem_limit_bytes=VMEM),
        cost_estimate=pl.CostEstimate(flops=6_000_000, bytes_accessed=9_500_000, transcendentals=0),
        name="finish_even",
    )(part, halo)


def odd_halo(i, halo, relayed, store):
    straight = DIRECT // TILE

    @pl.when(i < straight)
    def _():
        store(halo[...])

    @pl.when(i >= straight)
    def _():
        store(relayed[0][...] + relayed[1][...] + relayed[2][...])


def odd_halo_specs(depth, levels):
    straight = DIRECT // TILE
    top = pl.BlockSpec((TILE, depth, levels), lambda i, *_: (jnp.minimum(i, straight - 1), 0, 0))
    rest = pl.BlockSpec((TILE, depth, levels), lambda i, *_: (jnp.maximum(i - straight, 0), 0, 0))
    return top, rest


def finish_odd_kernel(part, halo, r0, r1, r2, mx_low, mx_high, mz_low, mz_high, ex, ez, *outs):
    face, top, rest, x_low, x_high, z_low, z_high = outs
    i, blocks = pl.program_id(0), pl.num_programs(0)
    depth = face.shape[1]

    def store(h):
        face[...] = part[...] + 0.1 * h

    odd_halo(i, halo, (r0, r1, r2), store)

    @pl.when(i < DIRECT // TILE)
    def _():
        top[...] = face[...]

    @pl.when(i >= DIRECT // TILE)
    def _():
        rest[...] = face[...]

    for z_out, z_mid, k, at in ((z_low, mz_low, 0, 0), (z_high, mz_high, 1, depth - 1)):
        z_out[0] = face[:, at, :]
        z_out[1:3] = z_mid[...]
        z_out[3] = ez[k]

    @pl.when(i == 0)
    def _():
        x_low[0] = face[0]
        x_low[1:3] = mx_low[...]
        x_low[3] = ex[0]

    @pl.when(i == blocks - 1)
    def _():
        x_high[0] = face[TILE - 1]
        x_high[1:3] = mx_high[...]
        x_high[3] = ex[1]


def finish_odd(part, halo, relayed, mids, ex, ez):
    rows, depth, levels = part.shape
    face = pl.BlockSpec((TILE, depth, levels), lambda i: (i, 0, 0))
    top, rest = odd_halo_specs(depth, levels)

    def ends(planes):
        return pl.BlockSpec((planes, TILE, levels), lambda i: (0, i, 0))

    x2, x4 = fixed(2, depth, levels), fixed(4, depth, levels)
    return pl.pallas_call(
        finish_odd_kernel,
        grid=(rows // TILE,),
        in_specs=[face, top, rest, rest, rest, x2, x2, ends(2), ends(2), x2, ends(2)],
        out_specs=[face, top, rest, x4, x4, ends(4), ends(4)],
        out_shape=[struct(*part.shape), struct(DIRECT, depth, levels), struct(rows - DIRECT, depth, levels)]
        + [struct(4, depth, levels)] * 2
        + [struct(4, rows, levels)] * 2,
        compiler_params=pltpu.CompilerParams(vmem_limit_bytes=VMEM),
        cost_estimate=pl.CostEstimate(flops=6_000_000, bytes_accessed=12_600_000, transcendentals=0),
        name="finish_odd",
    )(part, halo, *relayed, *mids, ex, ez)


def place_even_kernel(at_ref, part, halo, whole, out):
    out[0] = part[...] + 0.1 * halo[...]


def place_odd_kernel(at_ref, part, halo, r0, r1, r2, whole, out):
    def store(h):
        out[0] = part[...] + 0.1 * h

    odd_halo(pl.program_id(0), halo, (r0, r1, r2), store)


def place(kernel, at, part, halos, whole, specs):
    rows, depth, levels = part.shape
    face = pl.BlockSpec((TILE, depth, levels), lambda i, at_ref: (i, 0, 0))
    return pl.pallas_call(
        kernel,
        grid_spec=pltpu.PrefetchScalarGridSpec(
            num_scalar_prefetch=1,
            grid=(rows // TILE,),
            in_specs=[face, *(specs or [face]), pl.BlockSpec(memory_space=pl.ANY)],
            out_specs=pl.BlockSpec((1, TILE, depth, levels), lambda i, at_ref: (at_ref[0], i, 0, 0)),
        ),
        out_shape=struct(*whole.shape),
        input_output_aliases={2 + len(halos): 0},
        compiler_params=pltpu.CompilerParams(vmem_limit_bytes=VMEM),
        cost_estimate=pl.CostEstimate(flops=6_000_000, bytes_accessed=9_500_000, transcendentals=0),
        name="place",
    )(at.astype(jnp.int32).reshape(1), part, *halos, whole)


def local(density, inverse):
    odd = lax.axis_index("py") % 2
    odd_ref = odd.astype(jnp.int32).reshape(1)
    e_plane, o_plane = 3 * (1 - odd), 3 * odd
    e = lax.dynamic_index_in_dim(density, e_plane, 0, keepdims=False)
    o = lax.dynamic_index_in_dim(density, o_plane, 0, keepdims=False)
    mid = density
    rows, depth, levels = o.shape
    top, rest = o[:DIRECT], o[DIRECT:]
    x_low, x_high = density[:, 0], density[:, rows - 1]
    z_low, z_high = density[:, :, 0], density[:, :, depth - 1]
    up = [(k, k + 1) for k in range(3)]
    down = [(b, a) for a, b in up]
    e_halo = lax.ppermute(e, "py", EVEN_CUTS)
    for step in range(STEPS):
        relayed = []
        for to, _ in RELAYS:
            relayed.append(lax.ppermute(rest, "py", to))
        pz = [lax.ppermute(z_high, "pz", up), lax.ppermute(z_low, "pz", down)]
        px = [lax.ppermute(x_high, "px", up), lax.ppermute(x_low, "px", down)]
        o_halo = lax.ppermute(top, "py", ODD_CUTS)
        for k, (_, on) in enumerate(RELAYS):
            relayed[k] = lax.ppermute(relayed[k], "py", on)
        o_part, e_part, mid, *mids = partial_step(step, odd_ref, o, mid, e, inverse, px, pz)
        if step == STEPS - 1:
            break
        e, ex, ez = finish_even(e_part, e_halo)
        e_halo = lax.ppermute(e, "py", EVEN_CUTS)
        o, top, rest, x_low, x_high, z_low, z_high = finish_odd(o_part, o_halo, relayed, mids, ex, ez)
    out = place(place_even_kernel, e_plane, e_part, (e_halo,), mid, None)
    halo, relay = odd_halo_specs(depth, levels)
    return place(place_odd_kernel, o_plane, o_part, (o_halo, *relayed), out, [halo] + [relay] * 3)


def solution(mesh):
    spec = P("py", "px", "pz", None)
    return jax.shard_map(local, mesh=mesh, in_specs=(spec, spec), out_specs=spec, check_vma=False)
```

time: 585 us -> 566 us (0.968)
  the two profiles are of different devices: /device:TPU:20 before, /device:TPU:70 now
where the time goes in v1:
time: 566 us; the launch traced here: 565 us
  waiting for transfers between devices  398 us (70%)
  starting transfers between devices  92.5 us (16%)
  Pallas kernels  44.7 us (8%)
  local copies, waits for them, and re-layouts  29.3 us (5%)
    ppermute x6, waiting for transfers between devices, local(): pz = [lax.ppermute(z_high, 'pz', up), lax.ppermute(z_low, 'pz', down)]  236 us
    ppermute x9, waiting for transfers between devices, local(): relayed[k] = lax.ppermute(relayed[k], 'py', on)  152 us
    pallas_call x3, Pallas kernels, partial_step(): pl.pallas_call(functools.partial(partial_kernel, first, last), grid_spec=...  31.4 us
    ppermute x3, starting transfers between devices, local(): o_halo = lax.ppermute(top, 'py', ODD_CUTS)  31.3 us
    ppermute x3, starting transfers between devices, local(): e_halo = lax.ppermute(e, 'py', EVEN_CUTS)  21.8 us
    unnamed x14, local copies, waits for them, and re-layouts  16.2 us
    ppermute x6, starting transfers between devices, local(): pz = [lax.ppermute(z_high, 'pz', up), lax.ppermute(z_low, 'pz', down)]  15.3 us
  transfers between devices with their start and end apart: 36, of which 10 were waited for; matrix products, arithmetic and copies ran while one was open for 1% of the time, Pallas kernels for 8%

profile of v1, /device:TPU:70, one launch (start us, length us, event | category | flops | bytes accessed | tf_op | source)
XLA Modules:
  0.0 565.1 jit_solution(5547042397828179020)
XLA Ops:
  0.0 5.9 %dynamic-slice_bitcast_fusion = (f32[64,96,128]{2,1,0:T(8,128)}, f32[64,96,128]{2,1,0:T(8,128)}) fusion(f32[4,64,96,128]{3,2,1,0:T(8,128)} %refs_8_.1, s32[]{:T(128)S(6)} %select_n.16, s32[]{:T(128)S(6)} %select_n.15), kind=kLoop, calls=%fused_computation | loop fusion | bytes 12582920 | tf_op jit(solution)/shard_map/jit(dynamic_index_in_dim)/squeeze | solution.py:294
  7.3 3.2 dynamic-slice_bitcast_fusion.2
  10.6 5.1 collective-permute-start.4
  17.4 3.8 collective-permute-start.2
  24.8 103.9 %collective-permute-done.2.refs_15_ = f32[4,64,128]{2,1,0:T(8,128)S(1)} collective-permute-done((f32[4,64,128]{2,1,0:T(8,128)S(1)}, f32[4,64,128]{2,1,0:T(8,128)S(1)}, u32[]{:S(2)}, u32[]{:S(2)}) %collective-permute-start.2) | collective-permute-done | bytes 131104 | tf_op jit(solution)/shard_map/ppermute | solution.py:308
  128.7 1.9 collective-permute-start.3
  131.8 4.7 collective-permute-done.3.refs_16_
  139.3 4.6 copy-done
  145.8 11.3 %partial_step.3 = (f32[64,96,128]{2,1,0:T(8,128)S(1)}, f32[64,96,128]{2,1,0:T(8,128)S(1)}, f32[2,64,96,128]{3,2,1,0:T(8,128)S(1)}, f32[2,96,128]{2,1,0:T(8,128)S...) custom-call(s32[1]{0:T(128)} %bitcast.1.odd_ref, ...), custom_call_target="tpu_custom_call" | custom-call | flops 60000000 | bytes 40000000 | tf_op jit(solution)/shard_map/partial_step/pallas_call | solution.py:132
  157.1 2.8 finish_even.2
  159.9 3.7 collective-permute-start.23
  166.3 82.1 %collective-permute-done.10.r2 = f32[16,96,128]{2,1,0:T(8,128)S(1)} collective-permute-done((f32[16,96,128]{2,1,0:T(8,128)S(1)}, f32[16,96,128]{2,1,0:T(8,128)S(1)}, u32[]{:S(2)}, u32[]{:S(2)}) %collective-permute-start.10) | collective-permute-done | bytes 786464 | tf_op jit(solution)/shard_map/ppermute | solution.py:312
  248.4 4.4 finish_odd.2
  252.9 24.3 %collective-permute-start.16 = (f32[48,96,128]{2,1,0:T(8,128)}, f32[48,96,128]{2,1,0:T(8,128)S(1)}, u32[]{:S(2)}, u32[]{:S(2)}) collective-permute-start(f32[48,96,128]{2,1,0:T(8,128)} %get-tuple-element.58), channel_id=1, source_target_pairs={{16,32},{32,16},{48,64},{64,48},{80,96},{96,80},{17,33},{33,17},{4... | collective-permute-start | bytes 7077896 | tf_op jit(solution)/shard_map/ppermute | solution.py:310
  277.1 1.9 collective-permute-start.14
  281.7 44.4 %collective-permute-done.14.refs_15_ = f32[4,64,128]{2,1,0:T(8,128)S(1)} collective-permute-done((f32[4,64,128]{2,1,0:T(8,128)S(1)}, f32[4,64,128]{2,1,0:T(8,128)S(1)}, u32[]{:S(2)}, u32[]{:S(2)}) %collective-permute-start.14) | collective-permute-done | bytes 131104 | tf_op jit(solution)/shard_map/ppermute | solution.py:308
  326.1 1.9 collective-permute-start.15
  328.0 6.3 %collective-permute-done.15.refs_16_ = f32[4,64,128]{2,1,0:T(8,128)S(1)} collective-permute-done((f32[4,64,128]{2,1,0:T(8,128)S(1)}, f32[4,64,128]{2,1,0:T(8,128)S(1)}, u32[]{:S(2)}, u32[]{:S(2)}) %collective-permute-start.15) | collective-permute-done | bytes 131104 | tf_op jit(solution)/shard_map/ppermute | solution.py:308
  337.1 10.6 %partial_step.4 = (f32[64,96,128]{2,1,0:T(8,128)S(1)}, f32[64,96,128]{2,1,0:T(8,128)S(1)}, f32[2,64,96,128]{3,2,1,0:T(8,128)S(1)}, f32[2,96,128]{2,1,0:T(8,128)S...) custom-call(s32[1]{0:T(128)} %bitcast.1.odd_ref, ...), custom_call_target="tpu_custom_call" | custom-call | flops 60000000 | bytes 40000000 | tf_op jit(solution)/shard_map/partial_step/pallas_call | solution.py:132
  356.2 16.7 %collective-permute-start.35 = (f32[64,96,128]{2,1,0:T(8,128)S(1)}, f32[64,96,128]{2,1,0:T(8,128)S(1)}, u32[]{:S(2)}, u32[]{:S(2)}) collective-permute-start(f32[64,96,128]{2,1,0:T(8,128)S(1)} %get-tuple-element.69.refs_9_.refs_10_.refs_11_), channel_id=1, source_target_pairs={{0,16},{16,0},{32,48},{48,32},{64,80},{80,64},{96,112},{112,96},{1... | collective-permute-start | bytes 9437192 | tf_op jit(solution)/shard_map/ppermute | solution.py:317
  372.9 36.5 %collective-permute-done.22.r2 = f32[16,96,128]{2,1,0:T(8,128)S(1)} collective-permute-done((f32[16,96,128]{2,1,0:T(8,128)S(1)}, f32[16,96,128]{2,1,0:T(8,128)S(1)}, u32[]{:S(2)}, u32[]{:S(2)}) %collective-permute-start.22) | collective-permute-done | bytes 786464 | tf_op jit(solution)/shard_map/ppermute | solution.py:312
  410.4 1.9 collective-permute-start.28
  412.3 3.9 collective-permute-start.26
  418.9 70.9 %collective-permute-done.26.refs_15_ = f32[4,64,128]{2,1,0:T(8,128)S(1)} collective-permute-done((f32[4,64,128]{2,1,0:T(8,128)S(1)}, f32[4,64,128]{2,1,0:T(8,128)S(1)}, u32[]{:S(2)}, u32[]{:S(2)}) %collective-permute-start.26) | collective-permute-done | bytes 131104 | tf_op jit(solution)/shard_map/ppermute | solution.py:308
  489.8 1.9 collective-permute-start.27
  491.7 6.3 %collective-permute-done.27.refs_16_ = f32[4,64,128]{2,1,0:T(8,128)S(1)} collective-permute-done((f32[4,64,128]{2,1,0:T(8,128)S(1)}, f32[4,64,128]{2,1,0:T(8,128)S(1)}, u32[]{:S(2)}, u32[]{:S(2)}) %collective-permute-start.27) | collective-permute-done | bytes 131104 | tf_op jit(solution)/shard_map/ppermute | solution.py:308
  500.8 9.2 %collective-permute-done.29 = f32[16,96,128]{2,1,0:T(8,128)S(1)} collective-permute-done((f32[16,96,128]{2,1,0:T(8,128)S(1)}, f32[16,96,128]{2,1,0:T(8,128)S(1)}, u32[]{:S(2)}, u32[]{:S(2)}) %collective-permute-start.29) | collective-permute-done | bytes 786464 | tf_op jit(solution)/shard_map/ppermute | solution.py:307
  512.8 4.6 copy-done.1
  517.4 9.5 %partial_step.5 = (f32[64,96,128]{2,1,0:T(8,128)S(1)}, f32[64,96,128]{2,1,0:T(8,128)S(1)}, f32[4,64,96,128]{3,2,1,0:T(8,128)}) custom-call(s32[1]{0:T(128)} %bitcast.1.odd_ref, f32[64,96,128]{2,1,0:T(8,128)S(1)} %get-tuple-element.67.refs_0_.refs_1_.refs_2_, f32[64,96,128]{2,1,0:T(8,128)S(1)} %get-tuple-element.67.refs_0_.refs_1_.refs_2_, ...), custom_call_target="tpu_custom_call" | custom-call | flops 60000000 | bytes 40000000 | tf_op jit(solution)/shard_map/partial_step/pallas_call | solution.py:132
  526.8 2.2 place.2.whole
  529.0 33.8 %collective-permute-done.34.r2 = f32[16,96,128]{2,1,0:T(8,128)S(1)} collective-permute-done((f32[16,96,128]{2,1,0:T(8,128)S(1)}, f32[16,96,128]{2,1,0:T(8,128)S(1)}, u32[]{:S(2)}, u32[]{:S(2)}) %collective-permute-start.34) | collective-permute-done | bytes 786464 | tf_op jit(solution)/shard_map/ppermute | solution.py:312
  562.8 2.3 place.3
  (68 shorter events, 38.2 us)
Async XLA Ops:
  5.9 151.1 %collective-permute-start.11 = (f32[64,96,128]{2,1,0:T(8,128)}, f32[64,96,128]{2,1,0:T(8,128)}, u32[]{:S(2)}, u32[]{:S(2)}) collective-permute-start(f32[64,96,128]{2,1,0:T(8,128)} %get-tuple-element.83.refs_9_.refs_10_.refs_11_), channel_id=1, source_target_pairs={{0,16},{16,0},{32,48},{48,32},{64,80},{80,64},{96,112},{112,96},{1... | collective-permute-start | bytes 9437192 | tf_op jit(solution)/shard_map/ppermute | solution.py:303
  10.6 237.9 %collective-permute-start.4 = (f32[48,96,128]{2,1,0:T(8,128)}, f32[48,96,128]{2,1,0:T(8,128)}, u32[]{:S(2)}, u32[]{:S(2)}) collective-permute-start(f32[48,96,128]{2,1,0:T(8,128)} %dynamic-slice_bitcast_fusion.2), channel_id=1, source_target_pairs={{16,32},{32,16},{48,64},{64,48},{80,96},{96,80},{17,33},{33,17},{4... | collective-permute-start | bytes 7077896 | tf_op jit(solution)/shard_map/ppermute | solution.py:310
  17.4 111.3 %collective-permute-start.2 = (f32[4,64,128]{2,1,0:T(8,128)S(1)}, f32[4,64,128]{2,1,0:T(8,128)S(1)}, u32[]{:S(2)}, u32[]{:S(2)}) collective-permute-start(f32[4,64,128]{2,1,0:T(8,128)S(1)} %bitcast.26), channel_id=1, source_target_pairs={{0,1},{1,2},{2,3},{4,5},{5,6},{6,7},{8,9},{9,10},{10,11},{12,13},{... | collective-permute-start | bytes 393224 | tf_op jit(solution)/shard_map/ppermute | solution.py:308
  22.2 115.0 %collective-permute-start = (f32[4,96,128]{2,1,0:T(8,128)S(1)}, f32[4,96,128]{2,1,0:T(8,128)S(1)}, u32[]{:S(2)}, u32[]{:S(2)}) collective-permute-start(f32[4,96,128]{2,1,0:T(8,128)S(1)} %get-tuple-element.82), channel_id=1, source_target_pairs={{0,4},{4,8},{8,12},{1,5},{5,9},{9,13},{2,6},{6,10},{10,14},{3,7},{... | collective-permute-start | bytes 589832 | tf_op jit(solution)/shard_map/ppermute | solution.py:309
  23.5 115.1 %collective-permute-start.1 = (f32[4,96,128]{2,1,0:T(8,128)S(1)}, f32[4,96,128]{2,1,0:T(8,128)S(1)}, u32[]{:S(2)}, u32[]{:S(2)}) collective-permute-start(f32[4,96,128]{2,1,0:T(8,128)S(1)} %get-tuple-element.81), channel_id=1, source_target_pairs={{4,0},{8,4},{12,8},{5,1},{9,5},{13,9},{6,2},{10,6},{14,10},{7,3},{... | collective-permute-start | bytes 589832 | tf_op jit(solution)/shard_map/ppermute | solution.py:309
  136.5 27.1 %collective-permute-start.9 = (f32[16,96,128]{2,1,0:T(8,128)S(1)}, f32[16,96,128]{2,1,0:T(8,128)S(1)}, u32[]{:S(2)}, u32[]{:S(2)}) collective-permute-start(f32[16,96,128]{2,1,0:T(8,128)S(1)} %dynamic-slice_bitcast_fusion.3), channel_id=1, source_target_pairs={{96,0},{16,112},{97,1},{17,113},{98,2},{18,114},{99,3},{19,115},{1... | collective-permute-start | bytes 2359304 | tf_op jit(solution)/shard_map/ppermute | solution.py:307
  137.2 27.6 %collective-permute-start.5 = (f32[16,96,128]{2,1,0:T(8,128)S(1)}, f32[16,96,128]{2,1,0:T(8,128)S(1)}, u32[]{:S(2)}, u32[]{:S(2)}) collective-permute-start(f32[16,96,128]{2,1,0:T(8,128)S(1)} %dynamic-slice_bitcast_fusion.3), channel_id=1, source_target_pairs={{32,0},{80,112},{33,1},{81,113},{34,2},{82,114},{35,3},{83,115},{3... | collective-permute-start | bytes 2359304 | tf_op jit(solution)/shard_map/ppermute | solution.py:307
  138.6 27.0 %collective-permute-start.7 = (f32[16,96,128]{2,1,0:T(8,128)S(1)}, f32[16,96,128]{2,1,0:T(8,128)S(1)}, u32[]{:S(2)}, u32[]{:S(2)}) collective-permute-start(f32[16,96,128]{2,1,0:T(8,128)S(1)} %dynamic-slice_bitcast_fusion.3), channel_id=1, source_target_pairs={{64,0},{48,112},{65,1},{49,113},{66,2},{50,114},{67,3},{51,115},{6... | collective-permute-start | bytes 2359304 | tf_op jit(solution)/shard_map/ppermute | solution.py:307
  159.9 192.2 %collective-permute-start.23 = (f32[64,96,128]{2,1,0:T(8,128)S(1)}, f32[64,96,128]{2,1,0:T(8,128)S(1)}, u32[]{:S(2)}, u32[]{:S(2)}) collective-permute-start(f32[64,96,128]{2,1,0:T(8,128)S(1)} %get-tuple-element.52.refs_9_.refs_10_.refs_11_), channel_id=1, source_target_pairs={{0,16},{16,0},{32,48},{48,32},{64,80},{80,64},{96,112},{112,96},{1... | collective-permute-start | bytes 9437192 | tf_op jit(solution)/shard_map/ppermute | solution.py:317
  163.6 84.8 %collective-permute-start.10 = (f32[16,96,128]{2,1,0:T(8,128)S(1)}, f32[16,96,128]{2,1,0:T(8,128)S(1)}, u32[]{:S(2)}, u32[]{:S(2)}) collective-permute-start(f32[16,96,128]{2,1,0:T(8,128)S(1)} %collective-permute-done.9), channel_id=1, source_target_pairs={{0,80},{112,32},{1,81},{113,33},{2,82},{114,34},{3,83},{115,35},{4... | collective-permute-start | bytes 2359304 | tf_op jit(solution)/shard_map/ppermute | solution.py:312
  164.9 83.5 %collective-permute-start.6 = (f32[16,96,128]{2,1,0:T(8,128)S(1)}, f32[16,96,128]{2,1,0:T(8,128)S(1)}, u32[]{:S(2)}, u32[]{:S(2)}) collective-permute-start(f32[16,96,128]{2,1,0:T(8,128)S(1)} %collective-permute-done.5), channel_id=1, source_target_pairs={{0,16},{112,96},{1,17},{113,97},{2,18},{114,98},{3,19},{115,99},{4... | collective-permute-start | bytes 2359304 | tf_op jit(solution)/shard_map/ppermute | solution.py:312
  165.6 82.8 %collective-permute-start.8 = (f32[16,96,128]{2,1,0:T(8,128)S(1)}, f32[16,96,128]{2,1,0:T(8,128)S(1)}, u32[]{:S(2)}, u32[]{:S(2)}) collective-permute-start(f32[16,96,128]{2,1,0:T(8,128)S(1)} %collective-permute-done.7), channel_id=1, source_target_pairs={{0,48},{112,64},{1,49},{113,65},{2,50},{114,66},{3,51},{115,67},{4... | collective-permute-start | bytes 2359304 | tf_op jit(solution)/shard_map/ppermute | solution.py:312
  252.9 156.5 %collective-permute-start.16 = (f32[48,96,128]{2,1,0:T(8,128)}, f32[48,96,128]{2,1,0:T(8,128)S(1)}, u32[]{:S(2)}, u32[]{:S(2)}) collective-permute-start(f32[48,96,128]{2,1,0:T(8,128)} %get-tuple-element.58), channel_id=1, source_target_pairs={{16,32},{32,16},{48,64},{64,48},{80,96},{96,80},{17,33},{33,17},{4... | collective-permute-start | bytes 7077896 | tf_op jit(solution)/shard_map/ppermute | solution.py:310
  277.1 48.9 %collective-permute-start.14 = (f32[4,64,128]{2,1,0:T(8,128)S(1)}, f32[4,64,128]{2,1,0:T(8,128)S(1)}, u32[]{:S(2)}, u32[]{:S(2)}) collective-permute-start(f32[4,64,128]{2,1,0:T(8,128)S(1)} %get-tuple-element.55), channel_id=1, source_target_pairs={{0,1},{1,2},{2,3},{4,5},{5,6},{6,7},{8,9},{9,10},{10,11},{12,13},{... | collective-permute-start | bytes 393224 | tf_op jit(solution)/shard_map/ppermute | solution.py:308
  279.1 56.5 %collective-permute-start.12 = (f32[4,96,128]{2,1,0:T(8,128)S(1)}, f32[4,96,128]{2,1,0:T(8,128)S(1)}, u32[]{:S(2)}, u32[]{:S(2)}) collective-permute-start(f32[4,96,128]{2,1,0:T(8,128)S(1)} %get-tuple-element.53), channel_id=1, source_target_pairs={{0,4},{4,8},{8,12},{1,5},{5,9},{9,13},{2,6},{6,10},{10,14},{3,7},{... | collective-permute-start | bytes 589832 | tf_op jit(solution)/shard_map/ppermute | solution.py:309
  280.4 56.0 %collective-permute-start.13 = (f32[4,96,128]{2,1,0:T(8,128)S(1)}, f32[4,96,128]{2,1,0:T(8,128)S(1)}, u32[]{:S(2)}, u32[]{:S(2)}) collective-permute-start(f32[4,96,128]{2,1,0:T(8,128)S(1)} %get-tuple-element.54), channel_id=1, source_target_pairs={{4,0},{8,4},{12,8},{5,1},{9,5},{13,9},{6,2},{10,6},{14,10},{7,3},{... | collective-permute-start | bytes 589832 | tf_op jit(solution)/shard_map/ppermute | solution.py:309
  334.3 15.1 %collective-permute-start.17 = (f32[16,96,128]{2,1,0:T(8,128)S(1)}, f32[16,96,128]{2,1,0:T(8,128)S(1)}, u32[]{:S(2)}, u32[]{:S(2)}) collective-permute-start(f32[16,96,128]{2,1,0:T(8,128)S(1)} %get-tuple-element.59), channel_id=1, source_target_pairs={{32,0},{80,112},{33,1},{81,113},{34,2},{82,114},{35,3},{83,115},{3... | collective-permute-start | bytes 2359304 | tf_op jit(solution)/shard_map/ppermute | solution.py:307
  335.6 14.4 %collective-permute-start.19 = (f32[16,96,128]{2,1,0:T(8,128)S(1)}, f32[16,96,128]{2,1,0:T(8,128)S(1)}, u32[]{:S(2)}, u32[]{:S(2)}) collective-permute-start(f32[16,96,128]{2,1,0:T(8,128)S(1)} %get-tuple-element.59), channel_id=1, source_target_pairs={{64,0},{48,112},{65,1},{49,113},{66,2},{50,114},{67,3},{51,115},{6... | collective-permute-start | bytes 2359304 | tf_op jit(solution)/shard_map/ppermute | solution.py:307
  336.3 14.4 %collective-permute-start.21 = (f32[16,96,128]{2,1,0:T(8,128)S(1)}, f32[16,96,128]{2,1,0:T(8,128)S(1)}, u32[]{:S(2)}, u32[]{:S(2)}) collective-permute-start(f32[16,96,128]{2,1,0:T(8,128)S(1)} %get-tuple-element.59), channel_id=1, source_target_pairs={{96,0},{16,112},{97,1},{17,113},{98,2},{18,114},{99,3},{19,115},{1... | collective-permute-start | bytes 2359304 | tf_op jit(solution)/shard_map/ppermute | solution.py:307
  349.4 23.5 %collective-permute-start.18 = (f32[16,96,128]{2,1,0:T(8,128)S(1)}, f32[16,96,128]{2,1,0:T(8,128)S(1)}, u32[]{:S(2)}, u32[]{:S(2)}) collective-permute-start(f32[16,96,128]{2,1,0:T(8,128)S(1)} %collective-permute-done.17), channel_id=1, source_target_pairs={{0,16},{112,96},{1,17},{113,97},{2,18},{114,98},{3,19},{115,99},{4... | collective-permute-start | bytes 2359304 | tf_op jit(solution)/shard_map/ppermute | solution.py:312
  350.1 22.8 %collective-permute-start.20 = (f32[16,96,128]{2,1,0:T(8,128)S(1)}, f32[16,96,128]{2,1,0:T(8,128)S(1)}, u32[]{:S(2)}, u32[]{:S(2)}) collective-permute-start(f32[16,96,128]{2,1,0:T(8,128)S(1)} %collective-permute-done.19), channel_id=1, source_target_pairs={{0,48},{112,64},{1,49},{113,65},{2,50},{114,66},{3,51},{115,67},{4... | collective-permute-start | bytes 2359304 | tf_op jit(solution)/shard_map/ppermute | solution.py:312
  350.8 58.6 %collective-permute-start.22 = (f32[16,96,128]{2,1,0:T(8,128)S(1)}, f32[16,96,128]{2,1,0:T(8,128)S(1)}, u32[]{:S(2)}, u32[]{:S(2)}) collective-permute-start(f32[16,96,128]{2,1,0:T(8,128)S(1)} %collective-permute-done.21), channel_id=1, source_target_pairs={{0,80},{112,32},{1,81},{113,33},{2,82},{114,34},{3,83},{115,35},{4... | collective-permute-start | bytes 2359304 | tf_op jit(solution)/shard_map/ppermute | solution.py:312
  356.2 170.6 %collective-permute-start.35 = (f32[64,96,128]{2,1,0:T(8,128)S(1)}, f32[64,96,128]{2,1,0:T(8,128)S(1)}, u32[]{:S(2)}, u32[]{:S(2)}) collective-permute-start(f32[64,96,128]{2,1,0:T(8,128)S(1)} %get-tuple-element.69.refs_9_.refs_10_.refs_11_), channel_id=1, source_target_pairs={{0,16},{16,0},{32,48},{48,32},{64,80},{80,64},{96,112},{112,96},{1... | collective-permute-start | bytes 9437192 | tf_op jit(solution)/shard_map/ppermute | solution.py:317
  410.4 152.4 %collective-permute-start.28 = (f32[48,96,128]{2,1,0:T(8,128)S(1)}, f32[48,96,128]{2,1,0:T(8,128)S(1)}, u32[]{:S(2)}, u32[]{:S(2)}) collective-permute-start(f32[48,96,128]{2,1,0:T(8,128)S(1)} %get-tuple-element.75), channel_id=1, source_target_pairs={{16,32},{32,16},{48,64},{64,48},{80,96},{96,80},{17,33},{33,17},{4... | collective-permute-start | bytes 7077896 | tf_op jit(solution)/shard_map/ppermute | solution.py:310
  412.3 77.5 %collective-permute-start.26 = (f32[4,64,128]{2,1,0:T(8,128)S(1)}, f32[4,64,128]{2,1,0:T(8,128)S(1)}, u32[]{:S(2)}, u32[]{:S(2)}) collective-permute-start(f32[4,64,128]{2,1,0:T(8,128)S(1)} %get-tuple-element.72), channel_id=1, source_target_pairs={{0,1},{1,2},{2,3},{4,5},{5,6},{6,7},{8,9},{9,10},{10,11},{12,13},{... | collective-permute-start | bytes 393224 | tf_op jit(solution)/shard_map/ppermute | solution.py:308
  416.3 83.1 %collective-permute-start.24 = (f32[4,96,128]{2,1,0:T(8,128)S(1)}, f32[4,96,128]{2,1,0:T(8,128)S(1)}, u32[]{:S(2)}, u32[]{:S(2)}) collective-permute-start(f32[4,96,128]{2,1,0:T(8,128)S(1)} %get-tuple-element.70), channel_id=1, source_target_pairs={{0,4},{4,8},{8,12},{1,5},{5,9},{9,13},{2,6},{6,10},{10,14},{3,7},{... | collective-permute-start | bytes 589832 | tf_op jit(solution)/shard_map/ppermute | solution.py:309
  417.6 82.5 %collective-permute-start.25 = (f32[4,96,128]{2,1,0:T(8,128)S(1)}, f32[4,96,128]{2,1,0:T(8,128)S(1)}, u32[]{:S(2)}, u32[]{:S(2)}) collective-permute-start(f32[4,96,128]{2,1,0:T(8,128)S(1)} %get-tuple-element.71), channel_id=1, source_target_pairs={{4,0},{8,4},{12,8},{5,1},{9,5},{13,9},{6,2},{10,6},{14,10},{7,3},{... | collective-permute-start | bytes 589832 | tf_op jit(solution)/shard_map/ppermute | solution.py:309
  498.0 12.0 %collective-permute-start.29 = (f32[16,96,128]{2,1,0:T(8,128)S(1)}, f32[16,96,128]{2,1,0:T(8,128)S(1)}, u32[]{:S(2)}, u32[]{:S(2)}) collective-permute-start(f32[16,96,128]{2,1,0:T(8,128)S(1)} %get-tuple-element.76), channel_id=1, source_target_pairs={{32,0},{80,112},{33,1},{81,113},{34,2},{82,114},{35,3},{83,115},{3... | collective-permute-start | bytes 2359304 | tf_op jit(solution)/shard_map/ppermute | solution.py:307
  500.1 11.4 %collective-permute-start.33 = (f32[16,96,128]{2,1,0:T(8,128)S(1)}, f32[16,96,128]{2,1,0:T(8,128)S(1)}, u32[]{:S(2)}, u32[]{:S(2)}) collective-permute-start(f32[16,96,128]{2,1,0:T(8,128)S(1)} %get-tuple-element.76), channel_id=1, source_target_pairs={{96,0},{16,112},{97,1},{17,113},{98,2},{18,114},{99,3},{19,115},{1... | collective-permute-start | bytes 2359304 | tf_op jit(solution)/shard_map/ppermute | solution.py:307
  510.0 19.0 %collective-permute-start.30 = (f32[16,96,128]{2,1,0:T(8,128)S(1)}, f32[16,96,128]{2,1,0:T(8,128)S(1)}, u32[]{:S(2)}, u32[]{:S(2)}) collective-permute-start(f32[16,96,128]{2,1,0:T(8,128)S(1)} %collective-permute-done.29), channel_id=1, source_target_pairs={{0,16},{112,96},{1,17},{113,97},{2,18},{114,98},{3,19},{115,99},{4... | collective-permute-start | bytes 2359304 | tf_op jit(solution)/shard_map/ppermute | solution.py:312
  510.7 18.3 %collective-permute-start.32 = (f32[16,96,128]{2,1,0:T(8,128)S(1)}, f32[16,96,128]{2,1,0:T(8,128)S(1)}, u32[]{:S(2)}, u32[]{:S(2)}) collective-permute-start(f32[16,96,128]{2,1,0:T(8,128)S(1)} %collective-permute-done.31), channel_id=1, source_target_pairs={{0,48},{112,64},{1,49},{113,65},{2,50},{114,66},{3,51},{115,67},{4... | collective-permute-start | bytes 2359304 | tf_op jit(solution)/shard_map/ppermute | solution.py:312
  511.5 51.3 %collective-permute-start.34 = (f32[16,96,128]{2,1,0:T(8,128)S(1)}, f32[16,96,128]{2,1,0:T(8,128)S(1)}, u32[]{:S(2)}, u32[]{:S(2)}) collective-permute-start(f32[16,96,128]{2,1,0:T(8,128)S(1)} %collective-permute-done.33), channel_id=1, source_target_pairs={{0,80},{112,32},{1,81},{113,33},{2,82},{114,34},{3,83},{115,35},{4... | collective-permute-start | bytes 2359304 | tf_op jit(solution)/shard_map/ppermute | solution.py:312
  (11 other events, 105.6 us)

commit v2 on v1

--- a/solution.py
+++ b/solution.py
@@ -33,10 +33,10 @@
 
 def partial_kernel(first, last, odd_ref, *refs):
     planes = [refs[3 * s : 3 * s + 3] for s in range(4)]
-    inverse, px_low, px_high, pz_low, pz_high = refs[12:17]
-    part_o, part_e, kept, mx_low, mx_high, mz_low, mz_high = (refs[17:] + (None,) * 4)[:7]
+    inverse, px_low, px_high, z_even, z_odd, z_on = refs[12:18]
+    part_o, part_e, kept, mx_low, mx_high, mz_even, mz_odd = (refs[18:] + (None,) * 4)[:7]
     i, blocks = pl.program_id(0), pl.num_programs(0)
-    odd = odd_ref[0]
+    odd, pz_odd = odd_ref[0], odd_ref[1] == 1
     shape = px_low.shape[1:]
     depth = shape[0]
     z = lax.broadcasted_iota(jnp.int32, shape, 0)
@@ -54,8 +54,10 @@
     def one_row(r, before, after):
         for s in range(4):
             c = main(s, r)
-            below = jnp.where(z == 0, pz_low[edge(s), pl.ds(r, 1), :], pltpu.roll(c, 1, 0))
-            above = jnp.where(z == depth - 1, pz_high[edge(s), pl.ds(r, 1), :], pltpu.roll(c, depth - 1, 0))
+            over_even, over_odd, over_on = (v[edge(s), pl.ds(r, 1), :] for v in (z_even, z_odd, z_on))
+            over_odd = jnp.where(2 * i < blocks, over_odd, over_on)
+            below = jnp.where(z == 0, jnp.where(pz_odd, over_even, over_odd), pltpu.roll(c, 1, 0))
+            above = jnp.where(z == depth - 1, jnp.where(pz_odd, over_odd, over_even), pltpu.roll(c, depth - 1, 0))
             total = (before(s) + after(s)) + (below + above)
             if s > 0:
                 total = total + main(s - 1, r)
@@ -70,8 +72,9 @@
                 kept[stored(s), r] = value
             else:
                 kept[s - 1, r] = value
-                mz_low[s - 1, pl.ds(r, 1), :] = value[0:1, :]
-                mz_high[s - 1, pl.ds(r, 1), :] = value[depth - 1 : depth, :]
+                low, high = value[0:1, :], value[depth - 1 : depth, :]
+                mz_even[s - 1, pl.ds(r, 1), :] = jnp.where(pz_odd, low, high)
+                mz_odd[s - 1, pl.ds(r, 1), :] = jnp.where(pz_odd, high, low)
 
     def earlier(s):
         return jnp.where(i == 0, px_low[edge(s)], planes[s][1][...].reshape(shape))
@@ -97,7 +100,7 @@
             mx_high[...] = kept[:, ROWS - 1]
 
 
-def partial_step(step, odd, o, mid, e, inverse, px, pz):
+def partial_step(step, odd, o, mid, e, inverse, halo_ends):
     first, last = step == 0, step == STEPS - 1
     rows, depth, levels = o.shape
 
@@ -123,6 +126,11 @@
     def ends(planes):
         return pl.BlockSpec((planes, ROWS, levels), lambda i, odd_ref: (0, i, 0))
 
+    half = rows // ROWS // 2
+    half_ends = [
+        pl.BlockSpec((4, ROWS, levels), lambda i, odd_ref: (0, jnp.minimum(i, half - 1), 0)),
+        pl.BlockSpec((4, ROWS, levels), lambda i, odd_ref: (0, jnp.maximum(i - half, 0), 0)),
+    ]
     face = pl.BlockSpec((ROWS, depth, levels), lambda i, odd_ref: (i, 0, 0))
     out_specs = [face, face, block(4 if last else 2)]
     out_shape = [struct(*o.shape), struct(*o.shape), struct(4 if last else 2, *o.shape)]
@@ -138,22 +146,26 @@
             + specs(middle(1))
             + specs(middle(2))
             + specs(None)
-            + [block(4), fixed(4, depth, levels), fixed(4, depth, levels), ends(4), ends(4)],
+            + [block(4), fixed(4, depth, levels), fixed(4, depth, levels), ends(4), *half_ends],
             out_specs=out_specs,
         ),
         out_shape=out_shape,
         compiler_params=pltpu.CompilerParams(vmem_limit_bytes=VMEM),
         cost_estimate=pl.CostEstimate(flops=60_000_000, bytes_accessed=40_000_000, transcendentals=0),
         name="partial_step",
-    )(odd, *([o] * 3), *([mid] * 6), *([e] * 3), inverse, *px, *pz)
-
-
-def finish_even_kernel(part, halo, face, x_ends, z_ends):
+    )(odd, *([o] * 3), *([mid] * 6), *([e] * 3), inverse, *halo_ends)
+
+
+def z_ends_of(odd_ref, face):
+    low, high = face[:, 0, :], face[:, face.shape[1] - 1, :]
+    pz_odd = odd_ref[1] == 1
+    return jnp.where(pz_odd, low, high), jnp.where(pz_odd, high, low)
+
+
+def finish_even_kernel(odd_ref, part, halo, face, x_ends, z_ends):
     i, blocks = pl.program_id(0), pl.num_programs(0)
-    depth = face.shape[1]
     face[...] = part[...] + 0.1 * halo[...]
-    z_ends[0] = face[:, 0, :]
-    z_ends[1] = face[:, depth - 1, :]
+    z_ends[0], z_ends[1] = z_ends_of(odd_ref, face)
 
     @pl.when(i == 0)
     def _():
@@ -164,23 +176,26 @@
         x_ends[1] = face[TILE - 1]
 
 
-def finish_even(part, halo):
+def finish_even(odd, part, halo):
     rows, depth, levels = part.shape
-    face = pl.BlockSpec((TILE, depth, levels), lambda i: (i, 0, 0))
+    face = pl.BlockSpec((TILE, depth, levels), lambda i, _: (i, 0, 0))
     return pl.pallas_call(
         finish_even_kernel,
-        grid=(rows // TILE,),
-        in_specs=[face, face],
-        out_specs=[face, fixed(2, depth, levels), pl.BlockSpec((2, TILE, levels), lambda i: (0, i, 0))],
+        grid_spec=pltpu.PrefetchScalarGridSpec(
+            num_scalar_prefetch=1,
+            grid=(rows // TILE,),
+            in_specs=[face, face],
+            out_specs=[face, fixed(2, depth, levels), pl.BlockSpec((2, TILE, levels), lambda i, _: (0, i, 0))],
+        ),
         out_shape=[struct(*part.shape), struct(2, depth, levels), struct(2, rows, levels)],
         compiler_params=pltpu.CompilerParams(vmem_limit_bytes=VMEM),
         cost_estimate=pl.CostEstimate(flops=6_000_000, bytes_accessed=9_500_000, transcendentals=0),
         name="finish_even",
-    )(part, halo)
+    )(odd, part, halo)
 
 
 def odd_halo(i, halo, relayed, store):
-    straight = DIRECT // TILE
+    straight = DIRECT // halo.shape[0]
 
     @pl.when(i < straight)
     def _():
@@ -191,17 +206,16 @@
         store(relayed[0][...] + relayed[1][...] + relayed[2][...])
 
 
-def odd_halo_specs(depth, levels):
-    straight = DIRECT // TILE
-    top = pl.BlockSpec((TILE, depth, levels), lambda i, *_: (jnp.minimum(i, straight - 1), 0, 0))
-    rest = pl.BlockSpec((TILE, depth, levels), lambda i, *_: (jnp.maximum(i - straight, 0), 0, 0))
+def odd_halo_specs(depth, levels, tile):
+    straight = DIRECT // tile
+    top = pl.BlockSpec((tile, depth, levels), lambda i, *_: (jnp.minimum(i, straight - 1), 0, 0))
+    rest = pl.BlockSpec((tile, depth, levels), lambda i, *_: (jnp.maximum(i - straight, 0), 0, 0))
     return top, rest
 
 
-def finish_odd_kernel(part, halo, r0, r1, r2, mx_low, mx_high, mz_low, mz_high, ex, ez, *outs):
-    face, top, rest, x_low, x_high, z_low, z_high = outs
+def finish_odd_kernel(odd_ref, part, halo, r0, r1, r2, mx_low, mx_high, mz_even, mz_odd, ex, ez, *outs):
+    face, top, rest, x_low, x_high, z_even, z_odd = outs
     i, blocks = pl.program_id(0), pl.num_programs(0)
-    depth = face.shape[1]
 
     def store(h):
         face[...] = part[...] + 0.1 * h
@@ -216,8 +230,8 @@
     def _():
         rest[...] = face[...]
 
-    for z_out, z_mid, k, at in ((z_low, mz_low, 0, 0), (z_high, mz_high, 1, depth - 1)):
-        z_out[0] = face[:, at, :]
+    z_even[0], z_odd[0] = z_ends_of(odd_ref, face)
+    for k, (z_out, z_mid) in enumerate(((z_even, mz_even), (z_odd, mz_odd))):
         z_out[1:3] = z_mid[...]
         z_out[3] = ez[k]
 
@@ -234,27 +248,30 @@
         x_high[3] = ex[1]
 
 
-def finish_odd(part, halo, relayed, mids, ex, ez):
+def finish_odd(odd, part, halo, relayed, mids, ex, ez):
     rows, depth, levels = part.shape
-    face = pl.BlockSpec((TILE, depth, levels), lambda i: (i, 0, 0))
-    top, rest = odd_halo_specs(depth, levels)
+    face = pl.BlockSpec((TILE, depth, levels), lambda i, _: (i, 0, 0))
+    top, rest = odd_halo_specs(depth, levels, TILE)
 
     def ends(planes):
-        return pl.BlockSpec((planes, TILE, levels), lambda i: (0, i, 0))
+        return pl.BlockSpec((planes, TILE, levels), lambda i, _: (0, i, 0))
 
     x2, x4 = fixed(2, depth, levels), fixed(4, depth, levels)
     return pl.pallas_call(
         finish_odd_kernel,
-        grid=(rows // TILE,),
-        in_specs=[face, top, rest, rest, rest, x2, x2, ends(2), ends(2), x2, ends(2)],
-        out_specs=[face, top, rest, x4, x4, ends(4), ends(4)],
+        grid_spec=pltpu.PrefetchScalarGridSpec(
+            num_scalar_prefetch=1,
+            grid=(rows // TILE,),
+            in_specs=[face, top, rest, rest, rest, x2, x2, ends(2), ends(2), x2, ends(2)],
+            out_specs=[face, top, rest, x4, x4, ends(4), ends(4)],
+        ),
         out_shape=[struct(*part.shape), struct(DIRECT, depth, levels), struct(rows - DIRECT, depth, levels)]
         + [struct(4, depth, levels)] * 2
         + [struct(4, rows, levels)] * 2,
         compiler_params=pltpu.CompilerParams(vmem_limit_bytes=VMEM),
         cost_estimate=pl.CostEstimate(flops=6_000_000, bytes_accessed=12_600_000, transcendentals=0),
         name="finish_odd",
-    )(part, halo, *relayed, *mids, ex, ez)
+    )(odd, part, halo, *relayed, *mids, ex, ez)
 
 
 def place_even_kernel(at_ref, part, halo, whole, out):
@@ -270,14 +287,14 @@
 
 def place(kernel, at, part, halos, whole, specs):
     rows, depth, levels = part.shape
-    face = pl.BlockSpec((TILE, depth, levels), lambda i, at_ref: (i, 0, 0))
+    face = pl.BlockSpec((ROWS, depth, levels), lambda i, at_ref: (i, 0, 0))
     return pl.pallas_call(
         kernel,
         grid_spec=pltpu.PrefetchScalarGridSpec(
             num_scalar_prefetch=1,
-            grid=(rows // TILE,),
+            grid=(rows // ROWS,),
             in_specs=[face, *(specs or [face]), pl.BlockSpec(memory_space=pl.ANY)],
-            out_specs=pl.BlockSpec((1, TILE, depth, levels), lambda i, at_ref: (at_ref[0], i, 0, 0)),
+            out_specs=pl.BlockSpec((1, ROWS, depth, levels), lambda i, at_ref: (at_ref[0], i, 0, 0)),
         ),
         out_shape=struct(*whole.shape),
         input_output_aliases={2 + len(halos): 0},
@@ -287,37 +304,69 @@
     )(at.astype(jnp.int32).reshape(1), part, *halos, whole)
 
 
+def pick_kernel(at_ref, density, *outs_and_sems):
+    outs, sems = outs_and_sems[:-1], outs_and_sems[-1]
+    plane = density.at[at_ref[0]]
+    starts = [0, 0, DIRECT]
+    copies = [
+        pltpu.make_async_copy(plane.at[pl.ds(starts[k], out.shape[0])], out, sems.at[k]) for k, out in enumerate(outs)
+    ]
+    for copy in copies:
+        copy.start()
+    for copy in copies:
+        copy.wait()
+
+
+def pick(density, at, parts, grant):
+    _, rows, depth, levels = density.shape
+    sizes = (rows, DIRECT, rows - DIRECT)[:parts]
+    return pl.pallas_call(
+        pick_kernel,
+        in_specs=[pl.BlockSpec(memory_space=pltpu.SMEM), pl.BlockSpec(memory_space=pltpu.HBM)],
+        out_specs=[pl.BlockSpec(memory_space=pltpu.VMEM)] * parts,
+        out_shape=[struct(size, depth, levels) for size in sizes],
+        scratch_shapes=[pltpu.SemaphoreType.DMA((parts,))],
+        compiler_params=pltpu.CompilerParams(vmem_limit_bytes=grant * 1024 * 1024),
+        cost_estimate=pl.CostEstimate(flops=1_000_000, bytes_accessed=6_300_000, transcendentals=0),
+    )(at.astype(jnp.int32).reshape(1), density)
+
+
 def local(density, inverse):
-    odd = lax.axis_index("py") % 2
-    odd_ref = odd.astype(jnp.int32).reshape(1)
+    odd, pz_odd = lax.axis_index("py") % 2, lax.axis_index("pz") % 2
+    odd_ref = jnp.stack([odd, pz_odd]).astype(jnp.int32)
     e_plane, o_plane = 3 * (1 - odd), 3 * odd
-    e = lax.dynamic_index_in_dim(density, e_plane, 0, keepdims=False)
-    o = lax.dynamic_index_in_dim(density, o_plane, 0, keepdims=False)
+    (e,) = pick(density, e_plane, 1, 50)
+    e_halo = lax.ppermute(e, "py", EVEN_CUTS)
+    o, top, rest = pick(density, o_plane, 3, 46)
     mid = density
     rows, depth, levels = o.shape
-    top, rest = o[:DIRECT], o[DIRECT:]
     x_low, x_high = density[:, 0], density[:, rows - 1]
     z_low, z_high = density[:, :, 0], density[:, :, depth - 1]
+    z_even, z_odd = jnp.where(pz_odd == 1, z_low, z_high), jnp.where(pz_odd == 1, z_high, z_low)
     up = [(k, k + 1) for k in range(3)]
     down = [(b, a) for a, b in up]
-    e_halo = lax.ppermute(e, "py", EVEN_CUTS)
+    half = rows // 2
     for step in range(STEPS):
+        z_by = lax.ppermute(z_odd[:, half:], "pz", [(1, 3), (2, 0)])
+        z_even = lax.ppermute(z_even, "pz", [(0, 1), (1, 0), (2, 3), (3, 2)])
+        z_odd = lax.ppermute(z_odd[:, :half], "pz", [(1, 2), (2, 1)])
+        z_by = lax.ppermute(z_by, "pz", [(3, 2), (0, 1)])
         relayed = []
         for to, _ in RELAYS:
             relayed.append(lax.ppermute(rest, "py", to))
-        pz = [lax.ppermute(z_high, "pz", up), lax.ppermute(z_low, "pz", down)]
         px = [lax.ppermute(x_high, "px", up), lax.ppermute(x_low, "px", down)]
         o_halo = lax.ppermute(top, "py", ODD_CUTS)
         for k, (_, on) in enumerate(RELAYS):
             relayed[k] = lax.ppermute(relayed[k], "py", on)
-        o_part, e_part, mid, *mids = partial_step(step, odd_ref, o, mid, e, inverse, px, pz)
+        ends = [*px, z_even, z_odd, z_by]
+        o_part, e_part, mid, *mids = partial_step(step, odd_ref, o, mid, e, inverse, ends)
         if step == STEPS - 1:
             break
-        e, ex, ez = finish_even(e_part, e_halo)
+        e, ex, ez = finish_even(odd_ref, e_part, e_halo)
         e_halo = lax.ppermute(e, "py", EVEN_CUTS)
-        o, top, rest, x_low, x_high, z_low, z_high = finish_odd(o_part, o_halo, relayed, mids, ex, ez)
+        o, top, rest, x_low, x_high, z_even, z_odd = finish_odd(odd_ref, o_part, o_halo, relayed, mids, ex, ez)
     out = place(place_even_kernel, e_plane, e_part, (e_halo,), mid, None)
-    halo, relay = odd_halo_specs(depth, levels)
+    halo, relay = odd_halo_specs(depth, levels, ROWS)
     return place(place_odd_kernel, o_plane, o_part, (o_halo, *relayed), out, [halo] + [relay] * 3)
 
 

time: 566 us -> 589 us (1.041)
  the two profiles are of different devices: /device:TPU:70 before, /device:TPU:32 now
where the time goes in v2:
time: 589 us; the launch traced here: 588 us
  waiting for transfers between devices  430 us (73%)
  starting transfers between devices  77.4 us (13%)
  Pallas kernels  59.4 us (10%)
  local copies, waits for them, and re-layouts  20.7 us (4%)
    ppermute x9, waiting for transfers between devices, local(): relayed[k] = lax.ppermute(relayed[k], 'py', on)  198 us
    ppermute x3, waiting for transfers between devices, local(): z_by = lax.ppermute(z_by, 'pz', [(3, 2), (0, 1)])  188 us
    pallas_call x3, Pallas kernels, partial_step(): pl.pallas_call(functools.partial(partial_kernel, first, last), grid_spec=...  33.8 us
    ppermute x3, starting transfers between devices, local(): o_halo = lax.ppermute(top, 'py', ODD_CUTS)  19.5 us
    ppermute x9, waiting for transfers between devices, local(): relayed.append(lax.ppermute(rest, 'py', to))  19.3 us
    unnamed x16, local copies, waits for them, and re-layouts  17.8 us
    ppermute x3, starting transfers between devices, local(): z_even = lax.ppermute(z_even, 'pz', [(0, 1), (1, 0), (2, 3), (3, 2)])  14.9 us
    ppermute x3, waiting for transfers between devices, local(): z_by = lax.ppermute(z_odd[:, half:], 'pz', [(1, 3), (2, 0)])  13.7 us
  transfers between devices with their start and end apart: 42, of which 14 were waited for; matrix products, arithmetic and copies ran while one was open for 0% of the time, Pallas kernels for 9%

profile of v2, /device:TPU:32, one launch (start us, length us, event | category | flops | bytes accessed | tf_op | source)
XLA Modules:
  0.0 588.0 jit_solution(16216039852978510432)
XLA Ops:
  0.0 3.5 shard_map.29.refs_9_.refs_10_.refs_11_
  3.5 3.1 collective-permute-start.13
  6.6 4.2 shard_map.28
  18.2 4.2 collective-permute-done.4
  22.4 3.1 collective-permute-start.5
  29.2 97.0 %collective-permute-done.5.refs_17_ = f32[4,32,128]{2,1,0:T(8,128)S(1)} collective-permute-done((f32[4,32,128]{2,1,0:T(8,128)S(1)}, f32[4,32,128]{2,1,0:T(8,128)S(1)}, u32[]{:S(2)}, u32[]{:S(2)}) %collective-permute-start.5) | collective-permute-done | bytes 65568 | tf_op jit(solution)/shard_map/ppermute | solution.py:353
  126.2 4.9 collective-permute-start.2
  131.1 3.8 collective-permute-done.2.refs_15_
  137.7 4.6 copy-done
  144.2 12.1 %partial_step.3 = (f32[64,96,128]{2,1,0:T(8,128)S(1)}, f32[64,96,128]{2,1,0:T(8,128)S(1)}, f32[2,64,96,128]{3,2,1,0:T(8,128)S(1)}, f32[2,96,128]{2,1,0:T(8,128)S...) custom-call(s32[2]{0:T(128)S(1)} %pad_add_fusion.odd_ref, ...), custom_call_target="tpu_custom_call" | custom-call | flops 60000000 | bytes 40000000 | tf_op jit(solution)/shard_map/partial_step/pallas_call | solution.py:140
  156.3 3.4 finish_even.2
  163.1 105.3 %collective-permute-done.12.r2 = f32[16,96,128]{2,1,0:T(8,128)S(1)} collective-permute-done((f32[16,96,128]{2,1,0:T(8,128)S(1)}, f32[16,96,128]{2,1,0:T(8,128)S(1)}, u32[]{:S(2)}, u32[]{:S(2)}) %collective-permute-start.12) | collective-permute-done | bytes 786464 | tf_op jit(solution)/shard_map/ppermute | solution.py:360
  268.4 5.1 finish_odd.2
  273.5 15.7 %collective-permute-start.20 = (f32[48,96,128]{2,1,0:T(8,128)}, f32[48,96,128]{2,1,0:T(8,128)S(1)}, u32[]{:S(2)}, u32[]{:S(2)}) collective-permute-start(f32[48,96,128]{2,1,0:T(8,128)} %get-tuple-element.64), channel_id=1, source_target_pairs={{16,32},{32,16},{48,64},{64,48},{80,96},{96,80},{17,33},{33,17},{4... | collective-permute-start | bytes 7077896 | tf_op jit(solution)/shard_map/ppermute | solution.py:358
  291.2 4.2 collective-permute-done.18
  295.4 3.1 collective-permute-start.19
  301.1 39.7 %collective-permute-done.19.refs_17_ = f32[4,32,128]{2,1,0:T(8,128)S(1)} collective-permute-done((f32[4,32,128]{2,1,0:T(8,128)S(1)}, f32[4,32,128]{2,1,0:T(8,128)S(1)}, u32[]{:S(2)}, u32[]{:S(2)}) %collective-permute-start.19) | collective-permute-done | bytes 65568 | tf_op jit(solution)/shard_map/ppermute | solution.py:353
  340.9 5.8 collective-permute-start.16
  346.7 3.9 collective-permute-done.16.refs_15_
  353.4 11.3 %partial_step.4 = (f32[64,96,128]{2,1,0:T(8,128)S(1)}, f32[64,96,128]{2,1,0:T(8,128)S(1)}, f32[2,64,96,128]{3,2,1,0:T(8,128)S(1)}, f32[2,96,128]{2,1,0:T(8,128)S...) custom-call(s32[2]{0:T(128)S(1)} %pad_add_fusion.odd_ref, ...), custom_call_target="tpu_custom_call" | custom-call | flops 60000000 | bytes 40000000 | tf_op jit(solution)/shard_map/partial_step/pallas_call | solution.py:140
  376.9 52.1 %collective-permute-done.26.r2 = f32[16,96,128]{2,1,0:T(8,128)S(1)} collective-permute-done((f32[16,96,128]{2,1,0:T(8,128)S(1)}, f32[16,96,128]{2,1,0:T(8,128)S(1)}, u32[]{:S(2)}, u32[]{:S(2)}) %collective-permute-start.26) | collective-permute-done | bytes 786464 | tf_op jit(solution)/shard_map/ppermute | solution.py:360
  434.6 5.3 collective-permute-done.32
  439.9 3.1 collective-permute-start.33
  445.6 50.8 %collective-permute-done.33.refs_17_ = f32[4,32,128]{2,1,0:T(8,128)S(1)} collective-permute-done((f32[4,32,128]{2,1,0:T(8,128)S(1)}, f32[4,32,128]{2,1,0:T(8,128)S(1)}, u32[]{:S(2)}, u32[]{:S(2)}) %collective-permute-start.33) | collective-permute-done | bytes 65568 | tf_op jit(solution)/shard_map/ppermute | solution.py:353
  496.4 4.2 collective-permute-start.30
  500.5 3.9 collective-permute-done.30.refs_15_
  507.3 16.3 %collective-permute-done.35 = f32[16,96,128]{2,1,0:T(8,128)S(1)} collective-permute-done((f32[16,96,128]{2,1,0:T(8,128)S(1)}, f32[16,96,128]{2,1,0:T(8,128)S(1)}, u32[]{:S(2)}, u32[]{:S(2)}) %collective-permute-start.35) | collective-permute-done | bytes 786464 | tf_op jit(solution)/shard_map/ppermute | solution.py:356
  526.3 4.6 copy-done.1
  530.9 10.3 %partial_step.5 = (f32[64,96,128]{2,1,0:T(8,128)S(1)}, f32[64,96,128]{2,1,0:T(8,128)S(1)}, f32[4,64,96,128]{3,2,1,0:T(8,128)}) custom-call(s32[2]{0:T(128)S(1)} %pad_add_fusion.odd_ref, f32[64,96,128]{2,1,0:T(8,128)S(1)} %get-tuple-element.73.refs_0_.refs_1_.refs_2_, f32[64,96,128]{2,1,0:T(8,128)S(1)} %get-tuple-element.73.refs_0_.refs_1_.refs_2_, ...), custom_call_target="tpu_custom_call" | custom-call | flops 60000000 | bytes 40000000 | tf_op jit(solution)/shard_map/partial_step/pallas_call | solution.py:140
  541.2 3.3 place.2.whole
  544.5 40.1 %collective-permute-done.40.r2 = f32[16,96,128]{2,1,0:T(8,128)S(1)} collective-permute-done((f32[16,96,128]{2,1,0:T(8,128)S(1)}, f32[16,96,128]{2,1,0:T(8,128)S(1)}, u32[]{:S(2)}, u32[]{:S(2)}) %collective-permute-start.40) | collective-permute-done | bytes 786464 | tf_op jit(solution)/shard_map/ppermute | solution.py:360
  584.6 3.4 place.3
  (86 shorter events, 52.0 us)
Async XLA Ops:
  3.5 152.8 %collective-permute-start.13 = (f32[64,96,128]{2,1,0:T(8,128)}, f32[64,96,128]{2,1,0:T(8,128)}, u32[]{:S(2)}, u32[]{:S(2)}) collective-permute-start(f32[64,96,128]{2,1,0:T(8,128)} %shard_map.29.refs_9_.refs_10_.refs_11_), channel_id=1, source_target_pairs={{0,16},{16,0},{32,48},{48,32},{64,80},{80,64},{96,112},{112,96},{1... | collective-permute-start | bytes 9437192 | tf_op jit(solution)/shard_map/ppermute | solution.py:339
  12.5 255.9 %collective-permute-start.6 = (f32[48,96,128]{2,1,0:T(8,128)}, f32[48,96,128]{2,1,0:T(8,128)}, u32[]{:S(2)}, u32[]{:S(2)}) collective-permute-start(f32[48,96,128]{2,1,0:T(8,128)} %get-tuple-element.47), channel_id=1, source_target_pairs={{16,32},{32,16},{48,64},{64,48},{80,96},{96,80},{17,33},{33,17},{4... | collective-permute-start | bytes 7077896 | tf_op jit(solution)/shard_map/ppermute | solution.py:358
  17.5 10.3 %collective-permute-start.3 = (f32[4,32,128]{2,1,0:T(8,128)S(1)}, f32[4,32,128]{2,1,0:T(8,128)S(1)}, u32[]{:S(2)}, u32[]{:S(2)}) collective-permute-start(f32[4,32,128]{2,1,0:T(8,128)S(1)} %get-tuple-element.96), channel_id=1, source_target_pairs={{1,2},{2,1},{5,6},{6,5},{9,10},{10,9},{13,14},{14,13},{17,18},{18,... | collective-permute-start | bytes 196616 | tf_op jit(solution)/shard_map/ppermute | solution.py:352
  22.4 103.7 %collective-permute-start.5 = (f32[4,32,128]{2,1,0:T(8,128)S(1)}, f32[4,32,128]{2,1,0:T(8,128)S(1)}, u32[]{:S(2)}, u32[]{:S(2)}) collective-permute-start(f32[4,32,128]{2,1,0:T(8,128)S(1)} %collective-permute-done.4), channel_id=1, source_target_pairs={{3,2},{0,1},{7,6},{4,5},{11,10},{8,9},{15,14},{12,13},{19,18},{16,... | collective-permute-start | bytes 196616 | tf_op jit(solution)/shard_map/ppermute | solution.py:353
  26.5 109.1 %collective-permute-start = (f32[4,96,128]{2,1,0:T(8,128)S(1)}, f32[4,96,128]{2,1,0:T(8,128)S(1)}, u32[]{:S(2)}, u32[]{:S(2)}) collective-permute-start(f32[4,96,128]{2,1,0:T(8,128)S(1)} %get-tuple-element.88), channel_id=1, source_target_pairs={{0,4},{4,8},{8,12},{1,5},{5,9},{9,13},{2,6},{6,10},{10,14},{3,7},{... | collective-permute-start | bytes 589832 | tf_op jit(solution)/shard_map/ppermute | solution.py:357
  27.9 108.5 %collective-permute-start.1 = (f32[4,96,128]{2,1,0:T(8,128)S(1)}, f32[4,96,128]{2,1,0:T(8,128)S(1)}, u32[]{:S(2)}, u32[]{:S(2)}) collective-permute-start(f32[4,96,128]{2,1,0:T(8,128)S(1)} %get-tuple-element.87), channel_id=1, source_target_pairs={{4,0},{8,4},{12,8},{5,1},{9,5},{13,9},{6,2},{10,6},{14,10},{7,3},{... | collective-permute-start | bytes 589832 | tf_op jit(solution)/shard_map/ppermute | solution.py:357
  134.9 25.4 %collective-permute-start.9 = (f32[16,96,128]{2,1,0:T(8,128)S(1)}, f32[16,96,128]{2,1,0:T(8,128)S(1)}, u32[]{:S(2)}, u32[]{:S(2)}) collective-permute-start(f32[16,96,128]{2,1,0:T(8,128)S(1)} %get-tuple-element.48), channel_id=1, source_target_pairs={{64,0},{48,112},{65,1},{49,113},{66,2},{50,114},{67,3},{51,115},{6... | collective-permute-start | bytes 2359304 | tf_op jit(solution)/shard_map/ppermute | solution.py:356
  135.7 25.4 %collective-permute-start.11 = (f32[16,96,128]{2,1,0:T(8,128)S(1)}, f32[16,96,128]{2,1,0:T(8,128)S(1)}, u32[]{:S(2)}, u32[]{:S(2)}) collective-permute-start(f32[16,96,128]{2,1,0:T(8,128)S(1)} %get-tuple-element.48), channel_id=1, source_target_pairs={{96,0},{16,112},{97,1},{17,113},{98,2},{18,114},{99,3},{19,115},{1... | collective-permute-start | bytes 2359304 | tf_op jit(solution)/shard_map/ppermute | solution.py:356
  136.4 25.9 %collective-permute-start.7 = (f32[16,96,128]{2,1,0:T(8,128)S(1)}, f32[16,96,128]{2,1,0:T(8,128)S(1)}, u32[]{:S(2)}, u32[]{:S(2)}) collective-permute-start(f32[16,96,128]{2,1,0:T(8,128)S(1)} %get-tuple-element.48), channel_id=1, source_target_pairs={{32,0},{80,112},{33,1},{81,113},{34,2},{82,114},{35,3},{83,115},{3... | collective-permute-start | bytes 2359304 | tf_op jit(solution)/shard_map/ppermute | solution.py:356
  159.7 212.4 %collective-permute-start.27 = (f32[64,96,128]{2,1,0:T(8,128)S(1)}, f32[64,96,128]{2,1,0:T(8,128)S(1)}, u32[]{:S(2)}, u32[]{:S(2)}) collective-permute-start(f32[64,96,128]{2,1,0:T(8,128)S(1)} %get-tuple-element.58.refs_9_.refs_10_.refs_11_), channel_id=1, source_target_pairs={{0,16},{16,0},{32,48},{48,32},{64,80},{80,64},{96,112},{112,96},{1... | collective-permute-start | bytes 9437192 | tf_op jit(solution)/shard_map/ppermute | solution.py:366
  161.0 107.4 %collective-permute-start.12 = (f32[16,96,128]{2,1,0:T(8,128)S(1)}, f32[16,96,128]{2,1,0:T(8,128)S(1)}, u32[]{:S(2)}, u32[]{:S(2)}) collective-permute-start(f32[16,96,128]{2,1,0:T(8,128)S(1)} %collective-permute-done.11), channel_id=1, source_target_pairs={{0,80},{112,32},{1,81},{113,33},{2,82},{114,34},{3,83},{115,35},{4... | collective-permute-start | bytes 2359304 | tf_op jit(solution)/shard_map/ppermute | solution.py:360
  162.3 106.1 %collective-permute-start.8 = (f32[16,96,128]{2,1,0:T(8,128)S(1)}, f32[16,96,128]{2,1,0:T(8,128)S(1)}, u32[]{:S(2)}, u32[]{:S(2)}) collective-permute-start(f32[16,96,128]{2,1,0:T(8,128)S(1)} %collective-permute-done.7), channel_id=1, source_target_pairs={{0,16},{112,96},{1,17},{113,97},{2,18},{114,98},{3,19},{115,99},{4... | collective-permute-start | bytes 2359304 | tf_op jit(solution)/shard_map/ppermute | solution.py:360
  273.5 155.5 %collective-permute-start.20 = (f32[48,96,128]{2,1,0:T(8,128)}, f32[48,96,128]{2,1,0:T(8,128)S(1)}, u32[]{:S(2)}, u32[]{:S(2)}) collective-permute-start(f32[48,96,128]{2,1,0:T(8,128)} %get-tuple-element.64), channel_id=1, source_target_pairs={{16,32},{32,16},{48,64},{64,48},{80,96},{96,80},{17,33},{33,17},{4... | collective-permute-start | bytes 7077896 | tf_op jit(solution)/shard_map/ppermute | solution.py:358
  295.4 45.5 %collective-permute-start.19 = (f32[4,32,128]{2,1,0:T(8,128)S(1)}, f32[4,32,128]{2,1,0:T(8,128)S(1)}, u32[]{:S(2)}, u32[]{:S(2)}) collective-permute-start(f32[4,32,128]{2,1,0:T(8,128)S(1)} %collective-permute-done.18), channel_id=1, source_target_pairs={{3,2},{0,1},{7,6},{4,5},{11,10},{8,9},{15,14},{12,13},{19,18},{16,... | collective-permute-start | bytes 196616 | tf_op jit(solution)/shard_map/ppermute | solution.py:353
  298.5 53.4 %collective-permute-start.14 = (f32[4,96,128]{2,1,0:T(8,128)S(1)}, f32[4,96,128]{2,1,0:T(8,128)S(1)}, u32[]{:S(2)}, u32[]{:S(2)}) collective-permute-start(f32[4,96,128]{2,1,0:T(8,128)S(1)} %get-tuple-element.59), channel_id=1, source_target_pairs={{0,4},{4,8},{8,12},{1,5},{5,9},{9,13},{2,6},{6,10},{10,14},{3,7},{... | collective-permute-start | bytes 589832 | tf_op jit(solution)/shard_map/ppermute | solution.py:357
  299.8 52.9 %collective-permute-start.15 = (f32[4,96,128]{2,1,0:T(8,128)S(1)}, f32[4,96,128]{2,1,0:T(8,128)S(1)}, u32[]{:S(2)}, u32[]{:S(2)}) collective-permute-start(f32[4,96,128]{2,1,0:T(8,128)S(1)} %get-tuple-element.60), channel_id=1, source_target_pairs={{4,0},{8,4},{12,8},{5,1},{9,5},{13,9},{6,2},{10,6},{14,10},{7,3},{... | collective-permute-start | bytes 589832 | tf_op jit(solution)/shard_map/ppermute | solution.py:357
  350.6 18.8 %collective-permute-start.21 = (f32[16,96,128]{2,1,0:T(8,128)S(1)}, f32[16,96,128]{2,1,0:T(8,128)S(1)}, u32[]{:S(2)}, u32[]{:S(2)}) collective-permute-start(f32[16,96,128]{2,1,0:T(8,128)S(1)} %get-tuple-element.65), channel_id=1, source_target_pairs={{32,0},{80,112},{33,1},{81,113},{34,2},{82,114},{35,3},{83,115},{3... | collective-permute-start | bytes 2359304 | tf_op jit(solution)/shard_map/ppermute | solution.py:356
  352.0 18.1 %collective-permute-start.23 = (f32[16,96,128]{2,1,0:T(8,128)S(1)}, f32[16,96,128]{2,1,0:T(8,128)S(1)}, u32[]{:S(2)}, u32[]{:S(2)}) collective-permute-start(f32[16,96,128]{2,1,0:T(8,128)S(1)} %get-tuple-element.65), channel_id=1, source_target_pairs={{64,0},{48,112},{65,1},{49,113},{66,2},{50,114},{67,3},{51,115},{6... | collective-permute-start | bytes 2359304 | tf_op jit(solution)/shard_map/ppermute | solution.py:356
  352.7 18.1 %collective-permute-start.25 = (f32[16,96,128]{2,1,0:T(8,128)S(1)}, f32[16,96,128]{2,1,0:T(8,128)S(1)}, u32[]{:S(2)}, u32[]{:S(2)}) collective-permute-start(f32[16,96,128]{2,1,0:T(8,128)S(1)} %get-tuple-element.65), channel_id=1, source_target_pairs={{96,0},{16,112},{97,1},{17,113},{98,2},{18,114},{99,3},{19,115},{1... | collective-permute-start | bytes 2359304 | tf_op jit(solution)/shard_map/ppermute | solution.py:356
  370.8 58.2 %collective-permute-start.26 = (f32[16,96,128]{2,1,0:T(8,128)S(1)}, f32[16,96,128]{2,1,0:T(8,128)S(1)}, u32[]{:S(2)}, u32[]{:S(2)}) collective-permute-start(f32[16,96,128]{2,1,0:T(8,128)S(1)} %collective-permute-done.25), channel_id=1, source_target_pairs={{0,80},{112,32},{1,81},{113,33},{2,82},{114,34},{3,83},{115,35},{4... | collective-permute-start | bytes 2359304 | tf_op jit(solution)/shard_map/ppermute | solution.py:360
  376.8 164.4 %collective-permute-start.41 = (f32[64,96,128]{2,1,0:T(8,128)S(1)}, f32[64,96,128]{2,1,0:T(8,128)S(1)}, u32[]{:S(2)}, u32[]{:S(2)}) collective-permute-start(f32[64,96,128]{2,1,0:T(8,128)S(1)} %get-tuple-element.75.refs_9_.refs_10_.refs_11_), channel_id=1, source_target_pairs={{0,16},{16,0},{32,48},{48,32},{64,80},{80,64},{96,112},{112,96},{1... | collective-permute-start | bytes 9437192 | tf_op jit(solution)/shard_map/ppermute | solution.py:366
  430.7 154.0 %collective-permute-start.34 = (f32[48,96,128]{2,1,0:T(8,128)S(1)}, f32[48,96,128]{2,1,0:T(8,128)S(1)}, u32[]{:S(2)}, u32[]{:S(2)}) collective-permute-start(f32[48,96,128]{2,1,0:T(8,128)S(1)} %get-tuple-element.81), channel_id=1, source_target_pairs={{16,32},{32,16},{48,64},{64,48},{80,96},{96,80},{17,33},{33,17},{4... | collective-permute-start | bytes 7077896 | tf_op jit(solution)/shard_map/ppermute | solution.py:358
  433.9 10.4 %collective-permute-start.31 = (f32[4,32,128]{2,1,0:T(8,128)S(1)}, f32[4,32,128]{2,1,0:T(8,128)S(1)}, u32[]{:S(2)}, u32[]{:S(2)}) collective-permute-start(f32[4,32,128]{2,1,0:T(8,128)S(1)} %get-tuple-element.92), channel_id=1, source_target_pairs={{1,2},{2,1},{5,6},{6,5},{9,10},{10,9},{13,14},{14,13},{17,18},{18,... | collective-permute-start | bytes 196616 | tf_op jit(solution)/shard_map/ppermute | solution.py:352
  439.9 56.5 %collective-permute-start.33 = (f32[4,32,128]{2,1,0:T(8,128)S(1)}, f32[4,32,128]{2,1,0:T(8,128)S(1)}, u32[]{:S(2)}, u32[]{:S(2)}) collective-permute-start(f32[4,32,128]{2,1,0:T(8,128)S(1)} %collective-permute-done.32), channel_id=1, source_target_pairs={{3,2},{0,1},{7,6},{4,5},{11,10},{8,9},{15,14},{12,13},{19,18},{16,... | collective-permute-start | bytes 196616 | tf_op jit(solution)/shard_map/ppermute | solution.py:353
  443.0 62.8 %collective-permute-start.28 = (f32[4,96,128]{2,1,0:T(8,128)S(1)}, f32[4,96,128]{2,1,0:T(8,128)S(1)}, u32[]{:S(2)}, u32[]{:S(2)}) collective-permute-start(f32[4,96,128]{2,1,0:T(8,128)S(1)} %get-tuple-element.76), channel_id=1, source_target_pairs={{0,4},{4,8},{8,12},{1,5},{5,9},{9,13},{2,6},{6,10},{10,14},{3,7},{... | collective-permute-start | bytes 589832 | tf_op jit(solution)/shard_map/ppermute | solution.py:357
  444.3 62.2 %collective-permute-start.29 = (f32[4,96,128]{2,1,0:T(8,128)S(1)}, f32[4,96,128]{2,1,0:T(8,128)S(1)}, u32[]{:S(2)}, u32[]{:S(2)}) collective-permute-start(f32[4,96,128]{2,1,0:T(8,128)S(1)} %get-tuple-element.77), channel_id=1, source_target_pairs={{4,0},{8,4},{12,8},{5,1},{9,5},{13,9},{6,2},{10,6},{14,10},{7,3},{... | collective-permute-start | bytes 589832 | tf_op jit(solution)/shard_map/ppermute | solution.py:357
  504.5 19.1 %collective-permute-start.35 = (f32[16,96,128]{2,1,0:T(8,128)S(1)}, f32[16,96,128]{2,1,0:T(8,128)S(1)}, u32[]{:S(2)}, u32[]{:S(2)}) collective-permute-start(f32[16,96,128]{2,1,0:T(8,128)S(1)} %get-tuple-element.82), channel_id=1, source_target_pairs={{32,0},{80,112},{33,1},{81,113},{34,2},{82,114},{35,3},{83,115},{3... | collective-permute-start | bytes 2359304 | tf_op jit(solution)/shard_map/ppermute | solution.py:356
  505.8 18.4 %collective-permute-start.37 = (f32[16,96,128]{2,1,0:T(8,128)S(1)}, f32[16,96,128]{2,1,0:T(8,128)S(1)}, u32[]{:S(2)}, u32[]{:S(2)}) collective-permute-start(f32[16,96,128]{2,1,0:T(8,128)S(1)} %get-tuple-element.82), channel_id=1, source_target_pairs={{64,0},{48,112},{65,1},{49,113},{66,2},{50,114},{67,3},{51,115},{6... | collective-permute-start | bytes 2359304 | tf_op jit(solution)/shard_map/ppermute | solution.py:356
  506.5 18.4 %collective-permute-start.39 = (f32[16,96,128]{2,1,0:T(8,128)S(1)}, f32[16,96,128]{2,1,0:T(8,128)S(1)}, u32[]{:S(2)}, u32[]{:S(2)}) collective-permute-start(f32[16,96,128]{2,1,0:T(8,128)S(1)} %get-tuple-element.82), channel_id=1, source_target_pairs={{96,0},{16,112},{97,1},{17,113},{98,2},{18,114},{99,3},{19,115},{1... | collective-permute-start | bytes 2359304 | tf_op jit(solution)/shard_map/ppermute | solution.py:356
  523.5 21.0 %collective-permute-start.36 = (f32[16,96,128]{2,1,0:T(8,128)S(1)}, f32[16,96,128]{2,1,0:T(8,128)S(1)}, u32[]{:S(2)}, u32[]{:S(2)}) collective-permute-start(f32[16,96,128]{2,1,0:T(8,128)S(1)} %collective-permute-done.35), channel_id=1, source_target_pairs={{0,16},{112,96},{1,17},{113,97},{2,18},{114,98},{3,19},{115,99},{4... | collective-permute-start | bytes 2359304 | tf_op jit(solution)/shard_map/ppermute | solution.py:360
  524.2 20.3 %collective-permute-start.38 = (f32[16,96,128]{2,1,0:T(8,128)S(1)}, f32[16,96,128]{2,1,0:T(8,128)S(1)}, u32[]{:S(2)}, u32[]{:S(2)}) collective-permute-start(f32[16,96,128]{2,1,0:T(8,128)S(1)} %collective-permute-done.37), channel_id=1, source_target_pairs={{0,48},{112,64},{1,49},{113,65},{2,50},{114,66},{3,51},{115,67},{4... | collective-permute-start | bytes 2359304 | tf_op jit(solution)/shard_map/ppermute | solution.py:360
  525.0 59.6 %collective-permute-start.40 = (f32[16,96,128]{2,1,0:T(8,128)S(1)}, f32[16,96,128]{2,1,0:T(8,128)S(1)}, u32[]{:S(2)}, u32[]{:S(2)}) collective-permute-start(f32[16,96,128]{2,1,0:T(8,128)S(1)} %collective-permute-done.39), channel_id=1, source_target_pairs={{0,80},{112,32},{1,81},{113,33},{2,82},{114,34},{3,83},{115,35},{4... | collective-permute-start | bytes 2359304 | tf_op jit(solution)/shard_map/ppermute | solution.py:360
  (18 other events, 144.0 us)

commit v3 on v2

--- a/solution.py
+++ b/solution.py
@@ -195,7 +195,7 @@
 
 
 def odd_halo(i, halo, relayed, store):
-    straight = DIRECT // halo.shape[0]
+    straight = DIRECT // TILE
 
     @pl.when(i < straight)
     def _():
@@ -206,10 +206,10 @@
         store(relayed[0][...] + relayed[1][...] + relayed[2][...])
 
 
-def odd_halo_specs(depth, levels, tile):
-    straight = DIRECT // tile
-    top = pl.BlockSpec((tile, depth, levels), lambda i, *_: (jnp.minimum(i, straight - 1), 0, 0))
-    rest = pl.BlockSpec((tile, depth, levels), lambda i, *_: (jnp.maximum(i - straight, 0), 0, 0))
+def odd_halo_specs(depth, levels):
+    straight = DIRECT // TILE
+    top = pl.BlockSpec((TILE, depth, levels), lambda i, *_: (jnp.minimum(i, straight - 1), 0, 0))
+    rest = pl.BlockSpec((TILE, depth, levels), lambda i, *_: (jnp.maximum(i - straight, 0), 0, 0))
     return top, rest
 
 
@@ -251,7 +251,7 @@
 def finish_odd(odd, part, halo, relayed, mids, ex, ez):
     rows, depth, levels = part.shape
     face = pl.BlockSpec((TILE, depth, levels), lambda i, _: (i, 0, 0))
-    top, rest = odd_halo_specs(depth, levels, TILE)
+    top, rest = odd_halo_specs(depth, levels)
 
     def ends(planes):
         return pl.BlockSpec((planes, TILE, levels), lambda i, _: (0, i, 0))
@@ -274,29 +274,36 @@
     )(odd, part, halo, *relayed, *mids, ex, ez)
 
 
-def place_even_kernel(at_ref, part, halo, whole, out):
-    out[0] = part[...] + 0.1 * halo[...]
-
-
-def place_odd_kernel(at_ref, part, halo, r0, r1, r2, whole, out):
-    def store(h):
-        out[0] = part[...] + 0.1 * h
-
-    odd_halo(pl.program_id(0), halo, (r0, r1, r2), store)
-
-
-def place(kernel, at, part, halos, whole, specs):
-    rows, depth, levels = part.shape
-    face = pl.BlockSpec((ROWS, depth, levels), lambda i, at_ref: (i, 0, 0))
-    return pl.pallas_call(
-        kernel,
-        grid_spec=pltpu.PrefetchScalarGridSpec(
-            num_scalar_prefetch=1,
-            grid=(rows // ROWS,),
-            in_specs=[face, *(specs or [face]), pl.BlockSpec(memory_space=pl.ANY)],
-            out_specs=pl.BlockSpec((1, ROWS, depth, levels), lambda i, at_ref: (at_ref[0], i, 0, 0)),
-        ),
+def place_kernel(at_ref, part, *refs):
+    halos, (_, out, done, sems) = refs[:-4], refs[-4:]
+    plane = out.at[at_ref[0]]
+    copies = []
+    for k in range(part.shape[0] // TILE):
+        own = pl.ds(k * TILE, TILE)
+        if len(halos) == 1:
+            halo = halos[0][own]
+        elif k < DIRECT // TILE:
+            halo = halos[0][own]
+        else:
+            rest = pl.ds(k * TILE - DIRECT, TILE)
+            halo = halos[1][rest] + halos[2][rest] + halos[3][rest]
+        done[own] = part[own] + 0.1 * halo
+        copies.append(pltpu.make_async_copy(done.at[own], plane.at[own], sems.at[k]))
+        copies[-1].start()
+    for copy in copies:
+        copy.wait()
+
+
+def place(at, part, halos, whole):
+    held = pl.BlockSpec(memory_space=pltpu.VMEM)
+    return pl.pallas_call(
+        place_kernel,
+        in_specs=[pl.BlockSpec(memory_space=pltpu.SMEM), held]
+        + [held] * len(halos)
+        + [pl.BlockSpec(memory_space=pltpu.HBM)],
+        out_specs=pl.BlockSpec(memory_space=pltpu.HBM),
         out_shape=struct(*whole.shape),
+        scratch_shapes=[pltpu.VMEM(part.shape, jnp.float32), pltpu.SemaphoreType.DMA((part.shape[0] // TILE,))],
         input_output_aliases={2 + len(halos): 0},
         compiler_params=pltpu.CompilerParams(vmem_limit_bytes=VMEM),
         cost_estimate=pl.CostEstimate(flops=6_000_000, bytes_accessed=9_500_000, transcendentals=0),
@@ -304,10 +311,9 @@
     )(at.astype(jnp.int32).reshape(1), part, *halos, whole)
 
 
-def pick_kernel(at_ref, density, *outs_and_sems):
+def pick_kernel(starts, at_ref, density, *outs_and_sems):
     outs, sems = outs_and_sems[:-1], outs_and_sems[-1]
     plane = density.at[at_ref[0]]
-    starts = [0, 0, DIRECT]
     copies = [
         pltpu.make_async_copy(plane.at[pl.ds(starts[k], out.shape[0])], out, sems.at[k]) for k, out in enumerate(outs)
     ]
@@ -317,15 +323,14 @@
         copy.wait()
 
 
-def pick(density, at, parts, grant):
-    _, rows, depth, levels = density.shape
-    sizes = (rows, DIRECT, rows - DIRECT)[:parts]
-    return pl.pallas_call(
-        pick_kernel,
+def pick(density, at, spans, grant):
+    _, _, depth, levels = density.shape
+    return pl.pallas_call(
+        functools.partial(pick_kernel, [start for start, _ in spans]),
         in_specs=[pl.BlockSpec(memory_space=pltpu.SMEM), pl.BlockSpec(memory_space=pltpu.HBM)],
-        out_specs=[pl.BlockSpec(memory_space=pltpu.VMEM)] * parts,
-        out_shape=[struct(size, depth, levels) for size in sizes],
-        scratch_shapes=[pltpu.SemaphoreType.DMA((parts,))],
+        out_specs=[pl.BlockSpec(memory_space=pltpu.VMEM)] * len(spans),
+        out_shape=[struct(stop - start, depth, levels) for start, stop in spans],
+        scratch_shapes=[pltpu.SemaphoreType.DMA((len(spans),))],
         compiler_params=pltpu.CompilerParams(vmem_limit_bytes=grant * 1024 * 1024),
         cost_estimate=pl.CostEstimate(flops=1_000_000, bytes_accessed=6_300_000, transcendentals=0),
     )(at.astype(jnp.int32).reshape(1), density)
@@ -335,11 +340,14 @@
     odd, pz_odd = lax.axis_index("py") % 2, lax.axis_index("pz") % 2
     odd_ref = jnp.stack([odd, pz_odd]).astype(jnp.int32)
     e_plane, o_plane = 3 * (1 - odd), 3 * odd
-    (e,) = pick(density, e_plane, 1, 50)
-    e_halo = lax.ppermute(e, "py", EVEN_CUTS)
-    o, top, rest = pick(density, o_plane, 3, 46)
+    rows = density.shape[1]
+    (e_first,) = pick(density, e_plane, [(0, TILE)], 52)
+    first_halo = lax.ppermute(e_first, "py", EVEN_CUTS)
+    e, e_rest = pick(density, e_plane, [(0, rows), (TILE, rows)], 50)
+    e_halo = lax.ppermute(e_rest, "py", EVEN_CUTS)
+    o, top, rest = pick(density, o_plane, [(0, rows), (0, DIRECT), (DIRECT, rows)], 46)
     mid = density
-    rows, depth, levels = o.shape
+    rows, depth, _ = o.shape
     x_low, x_high = density[:, 0], density[:, rows - 1]
     z_low, z_high = density[:, :, 0], density[:, :, depth - 1]
     z_even, z_odd = jnp.where(pz_odd == 1, z_low, z_high), jnp.where(pz_odd == 1, z_high, z_low)
@@ -362,12 +370,13 @@
         o_part, e_part, mid, *mids = partial_step(step, odd_ref, o, mid, e, inverse, ends)
         if step == STEPS - 1:
             break
+        if step == 0:
+            e_halo = jnp.concatenate([first_halo, e_halo])
         e, ex, ez = finish_even(odd_ref, e_part, e_halo)
         e_halo = lax.ppermute(e, "py", EVEN_CUTS)
         o, top, rest, x_low, x_high, z_even, z_odd = finish_odd(odd_ref, o_part, o_halo, relayed, mids, ex, ez)
-    out = place(place_even_kernel, e_plane, e_part, (e_halo,), mid, None)
-    halo, relay = odd_halo_specs(depth, levels, ROWS)
-    return place(place_odd_kernel, o_plane, o_part, (o_halo, *relayed), out, [halo] + [relay] * 3)
+    out = place(e_plane, e_part, (e_halo,), mid)
+    return place(o_plane, o_part, (o_halo, *relayed), out)
 
 
 def solution(mesh):

time: 589 us -> 587 us (level)
  the two profiles are of different devices: /device:TPU:32 before, /device:TPU:76 now
where the time goes in v3:
time: 587 us; the launch traced here: 586 us
  waiting for transfers between devices  415 us (71%)
  starting transfers between devices  89.2 us (15%)
  Pallas kernels  56.4 us (10%)
  local copies, waits for them, and re-layouts  22.6 us (4%)
    ppermute x3, waiting for transfers between devices, local(): z_odd = lax.ppermute(z_odd[:, :half], 'pz', [(1, 2), (2, 1)])  196 us
    ppermute x9, waiting for transfers between devices, local(): relayed[k] = lax.ppermute(relayed[k], 'py', on)  182 us
    pallas_call x3, Pallas kernels, partial_step(): pl.pallas_call(functools.partial(partial_kernel, first, last), grid_spec=...  32.9 us
    ppermute x3, starting transfers between devices, local(): o_halo = lax.ppermute(top, 'py', ODD_CUTS)  27.5 us
    unnamed x18, local copies, waits for them, and re-layouts  19.7 us
    ppermute x9, waiting for transfers between devices, local(): relayed.append(lax.ppermute(rest, 'py', to))  19.7 us
    ppermute x6, starting transfers between devices, local(): px = [lax.ppermute(x_high, 'px', up), lax.ppermute(x_low, 'px', down)]  15.6 us
    ppermute x3, starting transfers between devices, local(): z_odd = lax.ppermute(z_odd[:, :half], 'pz', [(1, 2), (2, 1)])  12.6 us
  transfers between devices with their start and end apart: 43, of which 13 were waited for; matrix products, arithmetic and copies ran while one was open for 1% of the time, Pallas kernels for 8%

profile of v3, /device:TPU:76, one launch (start us, length us, event | category | flops | bytes accessed | tf_op | source)
XLA Modules:
  0.0 585.6 jit_solution(18097846350679925602)
XLA Ops:
  0.0 5.1 shard_map.29
  6.8 3.1 collective-permute-start.13
  9.9 4.6 shard_map.28
  16.2 3.4 collective-permute-start.6
  21.4 2.4 collective-permute-start.4
  23.7 5.0 collective-permute-start.3
  29.6 99.1 %collective-permute-done.3.refs_16_ = f32[4,32,128]{2,1,0:T(8,128)S(1)} collective-permute-done((f32[4,32,128]{2,1,0:T(8,128)S(1)}, f32[4,32,128]{2,1,0:T(8,128)S(1)}, u32[]{:S(2)}, u32[]{:S(2)}) %collective-permute-start.3) | collective-permute-done | bytes 65568 | tf_op jit(solution)/shard_map/ppermute | solution.py:360
  131.1 3.8 collective-permute-done.5.refs_17_
  138.3 4.1 collective-permute-done.1.refs_14_
  143.1 4.6 copy-done
  151.4 11.3 %partial_step.3 = (f32[64,96,128]{2,1,0:T(8,128)S(1)}, f32[64,96,128]{2,1,0:T(8,128)S(1)}, f32[2,64,96,128]{3,2,1,0:T(8,128)S(1)}, f32[2,96,128]{2,1,0:T(8,128)S...) custom-call(s32[2]{0:T(128)S(1)} %pad_add_fusion.odd_ref, ...), custom_call_target="tpu_custom_call" | custom-call | flops 60000000 | bytes 40000000 | tf_op jit(solution)/shard_map/partial_step/pallas_call | solution.py:140
  164.1 2.0 pad_maximum_fusion.halo
  170.3 7.0 %collective-permute-done.7 = f32[16,96,128]{2,1,0:T(8,128)S(1)} collective-permute-done((f32[16,96,128]{2,1,0:T(8,128)}, f32[16,96,128]{2,1,0:T(8,128)S(1)}, u32[]{:S(2)}, u32[]{:S(2)}) %collective-permute-start.7) | collective-permute-done | bytes 786464 | tf_op jit(solution)/shard_map/ppermute | solution.py:364
  178.0 89.9 %collective-permute-done.12.r2 = f32[16,96,128]{2,1,0:T(8,128)S(1)} collective-permute-done((f32[16,96,128]{2,1,0:T(8,128)S(1)}, f32[16,96,128]{2,1,0:T(8,128)S(1)}, u32[]{:S(2)}, u32[]{:S(2)}) %collective-permute-start.12) | collective-permute-done | bytes 786464 | tf_op jit(solution)/shard_map/ppermute | solution.py:368
  267.9 5.1 finish_odd.2
  273.1 22.2 %collective-permute-start.21 = (f32[48,96,128]{2,1,0:T(8,128)}, f32[48,96,128]{2,1,0:T(8,128)S(1)}, u32[]{:S(2)}, u32[]{:S(2)}) collective-permute-start(f32[48,96,128]{2,1,0:T(8,128)} %get-tuple-element.68), channel_id=1, source_target_pairs={{16,32},{32,16},{48,64},{64,48},{80,96},{96,80},{17,33},{33,17},{4... | collective-permute-start | bytes 7077896 | tf_op jit(solution)/shard_map/ppermute | solution.py:366
  295.3 2.9 collective-permute-start.19
  298.2 3.7 collective-permute-start.18
  303.2 5.9 %collective-permute-start.15 = (f32[4,96,128]{2,1,0:T(8,128)S(1)}, f32[4,96,128]{2,1,0:T(8,128)S(1)}, u32[]{:S(2)}, u32[]{:S(2)}) collective-permute-start(f32[4,96,128]{2,1,0:T(8,128)S(1)} %get-tuple-element.63), channel_id=1, source_target_pairs={{0,4},{4,8},{8,12},{1,5},{5,9},{9,13},{2,6},{6,10},{10,14},{3,7},{... | collective-permute-start | bytes 589832 | tf_op jit(solution)/shard_map/ppermute | solution.py:365
  309.1 39.7 %collective-permute-done.18.refs_16_ = f32[4,32,128]{2,1,0:T(8,128)S(1)} collective-permute-done((f32[4,32,128]{2,1,0:T(8,128)S(1)}, f32[4,32,128]{2,1,0:T(8,128)S(1)}, u32[]{:S(2)}, u32[]{:S(2)}) %collective-permute-start.18) | collective-permute-done | bytes 65568 | tf_op jit(solution)/shard_map/ppermute | solution.py:360
  350.2 5.0 collective-permute-done.17.refs_15_
  358.0 11.3 %partial_step.4 = (f32[64,96,128]{2,1,0:T(8,128)S(1)}, f32[64,96,128]{2,1,0:T(8,128)S(1)}, f32[2,64,96,128]{3,2,1,0:T(8,128)S(1)}, f32[2,96,128]{2,1,0:T(8,128)S...) custom-call(s32[2]{0:T(128)S(1)} %pad_add_fusion.odd_ref, ...), custom_call_target="tpu_custom_call" | custom-call | flops 60000000 | bytes 40000000 | tf_op jit(solution)/shard_map/partial_step/pallas_call | solution.py:140
  378.7 44.5 %collective-permute-done.27.r2 = f32[16,96,128]{2,1,0:T(8,128)S(1)} collective-permute-done((f32[16,96,128]{2,1,0:T(8,128)S(1)}, f32[16,96,128]{2,1,0:T(8,128)S(1)}, u32[]{:S(2)}, u32[]{:S(2)}) %collective-permute-start.27) | collective-permute-done | bytes 786464 | tf_op jit(solution)/shard_map/ppermute | solution.py:368
  426.8 2.2 collective-permute-start.33
  429.0 3.9 collective-permute-start.32
  434.2 4.6 collective-permute-start.29
  438.8 56.7 %collective-permute-done.32.refs_16_ = f32[4,32,128]{2,1,0:T(8,128)S(1)} collective-permute-done((f32[4,32,128]{2,1,0:T(8,128)S(1)}, f32[4,32,128]{2,1,0:T(8,128)S(1)}, u32[]{:S(2)}, u32[]{:S(2)}) %collective-permute-start.32) | collective-permute-done | bytes 65568 | tf_op jit(solution)/shard_map/ppermute | solution.py:360
  497.0 5.0 collective-permute-done.31.refs_15_
  504.7 12.5 %collective-permute-done.36 = f32[16,96,128]{2,1,0:T(8,128)S(1)} collective-permute-done((f32[16,96,128]{2,1,0:T(8,128)S(1)}, f32[16,96,128]{2,1,0:T(8,128)S(1)}, u32[]{:S(2)}, u32[]{:S(2)}) %collective-permute-start.36) | collective-permute-done | bytes 786464 | tf_op jit(solution)/shard_map/ppermute | solution.py:364
  519.9 4.6 copy-done.1
  524.5 10.3 %partial_step.5 = (f32[64,96,128]{2,1,0:T(8,128)S(1)}, f32[64,96,128]{2,1,0:T(8,128)S(1)}, f32[4,64,96,128]{3,2,1,0:T(8,128)}) custom-call(s32[2]{0:T(128)S(1)} %pad_add_fusion.odd_ref, f32[64,96,128]{2,1,0:T(8,128)S(1)} %get-tuple-element.77.refs_0_.refs_1_.refs_2_, f32[64,96,128]{2,1,0:T(8,128)S(1)} %get-tuple-element.77.refs_0_.refs_1_.refs_2_, ...), custom_call_target="tpu_custom_call" | custom-call | flops 60000000 | bytes 40000000 | tf_op jit(solution)/shard_map/partial_step/pallas_call | solution.py:140
  536.7 47.1 %collective-permute-done.41.refs_3_ = f32[16,96,128]{2,1,0:T(8,128)S(1)} collective-permute-done((f32[16,96,128]{2,1,0:T(8,128)S(1)}, f32[16,96,128]{2,1,0:T(8,128)S(1)}, u32[]{:S(2)}, u32[]{:S(2)}) %collective-permute-start.41) | collective-permute-done | bytes 786464 | tf_op jit(solution)/shard_map/ppermute | solution.py:368
  (92 shorter events, 52.4 us)
Async XLA Ops:
  5.1 159.0 %collective-permute-start.14 = (f32[48,96,128]{2,1,0:T(8,128)}, f32[48,96,128]{2,1,0:T(8,128)}, u32[]{:S(2)}, u32[]{:S(2)}) collective-permute-start(f32[48,96,128]{2,1,0:T(8,128)} %get-tuple-element.57), channel_id=1, source_target_pairs={{0,16},{16,0},{32,48},{48,32},{64,80},{80,64},{96,112},{112,96},{1... | collective-permute-start | bytes 7077896 | tf_op jit(solution)/shard_map/ppermute | solution.py:347
  6.8 155.9 %collective-permute-start.13 = (f32[16,96,128]{2,1,0:T(8,128)S(1)}, f32[16,96,128]{2,1,0:T(8,128)}, u32[]{:S(2)}, u32[]{:S(2)}) collective-permute-start(f32[16,96,128]{2,1,0:T(8,128)S(1)} %shard_map.30), channel_id=1, source_target_pairs={{0,16},{16,0},{32,48},{48,32},{64,80},{80,64},{96,112},{112,96},{1... | collective-permute-start | bytes 2359304 | tf_op jit(solution)/shard_map/ppermute | solution.py:345
  16.2 251.7 %collective-permute-start.6 = (f32[48,96,128]{2,1,0:T(8,128)}, f32[48,96,128]{2,1,0:T(8,128)}, u32[]{:S(2)}, u32[]{:S(2)}) collective-permute-start(f32[48,96,128]{2,1,0:T(8,128)} %get-tuple-element.50), channel_id=1, source_target_pairs={{16,32},{32,16},{48,64},{64,48},{80,96},{96,80},{17,33},{33,17},{4... | collective-permute-start | bytes 7077896 | tf_op jit(solution)/shard_map/ppermute | solution.py:366
  23.7 105.0 %collective-permute-start.3 = (f32[4,32,128]{2,1,0:T(8,128)S(1)}, f32[4,32,128]{2,1,0:T(8,128)S(1)}, u32[]{:S(2)}, u32[]{:S(2)}) collective-permute-start(f32[4,32,128]{2,1,0:T(8,128)S(1)} %get-tuple-element.100), channel_id=1, source_target_pairs={{1,2},{2,1},{5,6},{6,5},{9,10},{10,9},{13,14},{14,13},{17,18},{18,... | collective-permute-start | bytes 196616 | tf_op jit(solution)/shard_map/ppermute | solution.py:360
  28.8 107.4 %collective-permute-start.2 = (f32[4,64,128]{2,1,0:T(8,128)S(1)}, f32[4,64,128]{2,1,0:T(8,128)S(1)}, u32[]{:S(2)}, u32[]{:S(2)}) collective-permute-start(f32[4,64,128]{2,1,0:T(8,128)S(1)} %get-tuple-element.94), channel_id=1, source_target_pairs={{0,1},{1,0},{2,3},{3,2},{4,5},{5,4},{6,7},{7,6},{8,9},{9,8},{10,11... | collective-permute-start | bytes 393224 | tf_op jit(solution)/shard_map/ppermute | solution.py:359
  137.6 30.6 %collective-permute-start.9 = (f32[16,96,128]{2,1,0:T(8,128)}, f32[16,96,128]{2,1,0:T(8,128)S(1)}, u32[]{:S(2)}, u32[]{:S(2)}) collective-permute-start(f32[16,96,128]{2,1,0:T(8,128)} %get-tuple-element.51), channel_id=1, source_target_pairs={{64,0},{48,112},{65,1},{49,113},{66,2},{50,114},{67,3},{51,115},{6... | collective-permute-start | bytes 2359304 | tf_op jit(solution)/shard_map/ppermute | solution.py:364
  142.4 26.6 %collective-permute-start.11 = (f32[16,96,128]{2,1,0:T(8,128)}, f32[16,96,128]{2,1,0:T(8,128)S(1)}, u32[]{:S(2)}, u32[]{:S(2)}) collective-permute-start(f32[16,96,128]{2,1,0:T(8,128)} %get-tuple-element.51), channel_id=1, source_target_pairs={{96,0},{16,112},{97,1},{17,113},{98,2},{18,114},{99,3},{19,115},{1... | collective-permute-start | bytes 2359304 | tf_op jit(solution)/shard_map/ppermute | solution.py:364
  162.7 14.6 %collective-permute-start.7 = (f32[16,96,128]{2,1,0:T(8,128)}, f32[16,96,128]{2,1,0:T(8,128)S(1)}, u32[]{:S(2)}, u32[]{:S(2)}) collective-permute-start(f32[16,96,128]{2,1,0:T(8,128)} %get-tuple-element.51), channel_id=1, source_target_pairs={{32,0},{80,112},{33,1},{81,113},{34,2},{82,114},{35,3},{83,115},{3... | collective-permute-start | bytes 2359304 | tf_op jit(solution)/shard_map/ppermute | solution.py:364
  167.3 206.7 %collective-permute-start.28 = (f32[64,96,128]{2,1,0:T(8,128)S(1)}, f32[64,96,128]{2,1,0:T(8,128)S(1)}, u32[]{:S(2)}, u32[]{:S(2)}) collective-permute-start(f32[64,96,128]{2,1,0:T(8,128)S(1)} %get-tuple-element.62.refs_9_.refs_10_.refs_11_), channel_id=1, source_target_pairs={{0,16},{16,0},{32,48},{48,32},{64,80},{80,64},{96,112},{112,96},{1... | collective-permute-start | bytes 9437192 | tf_op jit(solution)/shard_map/ppermute | solution.py:376
  168.2 9.7 %collective-permute-start.10 = (f32[16,96,128]{2,1,0:T(8,128)S(1)}, f32[16,96,128]{2,1,0:T(8,128)S(1)}, u32[]{:S(2)}, u32[]{:S(2)}) collective-permute-start(f32[16,96,128]{2,1,0:T(8,128)S(1)} %collective-permute-done.9), channel_id=1, source_target_pairs={{0,48},{112,64},{1,49},{113,65},{2,50},{114,66},{3,51},{115,67},{4... | collective-permute-start | bytes 2359304 | tf_op jit(solution)/shard_map/ppermute | solution.py:368
  169.0 99.0 %collective-permute-start.12 = (f32[16,96,128]{2,1,0:T(8,128)S(1)}, f32[16,96,128]{2,1,0:T(8,128)S(1)}, u32[]{:S(2)}, u32[]{:S(2)}) collective-permute-start(f32[16,96,128]{2,1,0:T(8,128)S(1)} %collective-permute-done.11), channel_id=1, source_target_pairs={{0,80},{112,32},{1,81},{113,33},{2,82},{114,34},{3,83},{115,35},{4... | collective-permute-start | bytes 2359304 | tf_op jit(solution)/shard_map/ppermute | solution.py:368
  177.3 90.7 %collective-permute-start.8 = (f32[16,96,128]{2,1,0:T(8,128)S(1)}, f32[16,96,128]{2,1,0:T(8,128)S(1)}, u32[]{:S(2)}, u32[]{:S(2)}) collective-permute-start(f32[16,96,128]{2,1,0:T(8,128)S(1)} %collective-permute-done.7), channel_id=1, source_target_pairs={{0,16},{112,96},{1,17},{113,97},{2,18},{114,98},{3,19},{115,99},{4... | collective-permute-start | bytes 2359304 | tf_op jit(solution)/shard_map/ppermute | solution.py:368
  273.1 150.2 %collective-permute-start.21 = (f32[48,96,128]{2,1,0:T(8,128)}, f32[48,96,128]{2,1,0:T(8,128)S(1)}, u32[]{:S(2)}, u32[]{:S(2)}) collective-permute-start(f32[48,96,128]{2,1,0:T(8,128)} %get-tuple-element.68), channel_id=1, source_target_pairs={{16,32},{32,16},{48,64},{64,48},{80,96},{96,80},{17,33},{33,17},{4... | collective-permute-start | bytes 7077896 | tf_op jit(solution)/shard_map/ppermute | solution.py:366
  298.2 50.6 %collective-permute-start.18 = (f32[4,32,128]{2,1,0:T(8,128)S(1)}, f32[4,32,128]{2,1,0:T(8,128)S(1)}, u32[]{:S(2)}, u32[]{:S(2)}) collective-permute-start(f32[4,32,128]{2,1,0:T(8,128)S(1)} %get-tuple-element.98), channel_id=1, source_target_pairs={{1,2},{2,1},{5,6},{6,5},{9,10},{10,9},{13,14},{14,13},{17,18},{18,... | collective-permute-start | bytes 196616 | tf_op jit(solution)/shard_map/ppermute | solution.py:360
  301.9 48.2 %collective-permute-start.20 = (f32[4,32,128]{2,1,0:T(8,128)S(1)}, f32[4,32,128]{2,1,0:T(8,128)S(1)}, u32[]{:S(2)}, u32[]{:S(2)}) collective-permute-start(f32[4,32,128]{2,1,0:T(8,128)S(1)} %collective-permute-done.19), channel_id=1, source_target_pairs={{3,2},{0,1},{7,6},{4,5},{11,10},{8,9},{15,14},{12,13},{19,18},{16,... | collective-permute-start | bytes 196616 | tf_op jit(solution)/shard_map/ppermute | solution.py:361
  303.2 53.3 %collective-permute-start.15 = (f32[4,96,128]{2,1,0:T(8,128)S(1)}, f32[4,96,128]{2,1,0:T(8,128)S(1)}, u32[]{:S(2)}, u32[]{:S(2)}) collective-permute-start(f32[4,96,128]{2,1,0:T(8,128)S(1)} %get-tuple-element.63), channel_id=1, source_target_pairs={{0,4},{4,8},{8,12},{1,5},{5,9},{9,13},{2,6},{6,10},{10,14},{3,7},{... | collective-permute-start | bytes 589832 | tf_op jit(solution)/shard_map/ppermute | solution.py:365
  348.8 8.4 %collective-permute-start.16 = (f32[4,96,128]{2,1,0:T(8,128)S(1)}, f32[4,96,128]{2,1,0:T(8,128)S(1)}, u32[]{:S(2)}, u32[]{:S(2)}) collective-permute-start(f32[4,96,128]{2,1,0:T(8,128)S(1)} %get-tuple-element.64), channel_id=1, source_target_pairs={{4,0},{8,4},{12,8},{5,1},{9,5},{13,9},{6,2},{10,6},{14,10},{7,3},{... | collective-permute-start | bytes 589832 | tf_op jit(solution)/shard_map/ppermute | solution.py:365
  355.2 16.0 %collective-permute-start.22 = (f32[16,96,128]{2,1,0:T(8,128)S(1)}, f32[16,96,128]{2,1,0:T(8,128)S(1)}, u32[]{:S(2)}, u32[]{:S(2)}) collective-permute-start(f32[16,96,128]{2,1,0:T(8,128)S(1)} %get-tuple-element.69), channel_id=1, source_target_pairs={{32,0},{80,112},{33,1},{81,113},{34,2},{82,114},{35,3},{83,115},{3... | collective-permute-start | bytes 2359304 | tf_op jit(solution)/shard_map/ppermute | solution.py:364
  356.5 15.4 %collective-permute-start.24 = (f32[16,96,128]{2,1,0:T(8,128)S(1)}, f32[16,96,128]{2,1,0:T(8,128)S(1)}, u32[]{:S(2)}, u32[]{:S(2)}) collective-permute-start(f32[16,96,128]{2,1,0:T(8,128)S(1)} %get-tuple-element.69), channel_id=1, source_target_pairs={{64,0},{48,112},{65,1},{49,113},{66,2},{50,114},{67,3},{51,115},{6... | collective-permute-start | bytes 2359304 | tf_op jit(solution)/shard_map/ppermute | solution.py:364
  357.3 15.4 %collective-permute-start.26 = (f32[16,96,128]{2,1,0:T(8,128)S(1)}, f32[16,96,128]{2,1,0:T(8,128)S(1)}, u32[]{:S(2)}, u32[]{:S(2)}) collective-permute-start(f32[16,96,128]{2,1,0:T(8,128)S(1)} %get-tuple-element.69), channel_id=1, source_target_pairs={{96,0},{16,112},{97,1},{17,113},{98,2},{18,114},{99,3},{19,115},{1... | collective-permute-start | bytes 2359304 | tf_op jit(solution)/shard_map/ppermute | solution.py:364
  372.6 50.6 %collective-permute-start.27 = (f32[16,96,128]{2,1,0:T(8,128)S(1)}, f32[16,96,128]{2,1,0:T(8,128)S(1)}, u32[]{:S(2)}, u32[]{:S(2)}) collective-permute-start(f32[16,96,128]{2,1,0:T(8,128)S(1)} %collective-permute-done.26), channel_id=1, source_target_pairs={{0,80},{112,32},{1,81},{113,33},{2,82},{114,34},{3,83},{115,35},{4... | collective-permute-start | bytes 2359304 | tf_op jit(solution)/shard_map/ppermute | solution.py:368
  378.6 156.2 %collective-permute-start.42 = (f32[64,96,128]{2,1,0:T(8,128)S(1)}, f32[64,96,128]{2,1,0:T(8,128)S(1)}, u32[]{:S(2)}, u32[]{:S(2)}) collective-permute-start(f32[64,96,128]{2,1,0:T(8,128)S(1)} %get-tuple-element.79.refs_9_.refs_10_.refs_11_), channel_id=1, source_target_pairs={{0,16},{16,0},{32,48},{48,32},{64,80},{80,64},{96,112},{112,96},{1... | collective-permute-start | bytes 9437192 | tf_op jit(solution)/shard_map/ppermute | solution.py:376
  424.8 158.9 %collective-permute-start.35 = (f32[48,96,128]{2,1,0:T(8,128)S(1)}, f32[48,96,128]{2,1,0:T(8,128)S(1)}, u32[]{:S(2)}, u32[]{:S(2)}) collective-permute-start(f32[48,96,128]{2,1,0:T(8,128)S(1)} %get-tuple-element.85), channel_id=1, source_target_pairs={{16,32},{32,16},{48,64},{64,48},{80,96},{96,80},{17,33},{33,17},{4... | collective-permute-start | bytes 7077896 | tf_op jit(solution)/shard_map/ppermute | solution.py:366
  429.0 66.6 %collective-permute-start.32 = (f32[4,32,128]{2,1,0:T(8,128)S(1)}, f32[4,32,128]{2,1,0:T(8,128)S(1)}, u32[]{:S(2)}, u32[]{:S(2)}) collective-permute-start(f32[4,32,128]{2,1,0:T(8,128)S(1)} %get-tuple-element.96), channel_id=1, source_target_pairs={{1,2},{2,1},{5,6},{6,5},{9,10},{10,9},{13,14},{14,13},{17,18},{18,... | collective-permute-start | bytes 196616 | tf_op jit(solution)/shard_map/ppermute | solution.py:360
  432.9 64.0 %collective-permute-start.34 = (f32[4,32,128]{2,1,0:T(8,128)S(1)}, f32[4,32,128]{2,1,0:T(8,128)S(1)}, u32[]{:S(2)}, u32[]{:S(2)}) collective-permute-start(f32[4,32,128]{2,1,0:T(8,128)S(1)} %collective-permute-done.33), channel_id=1, source_target_pairs={{3,2},{0,1},{7,6},{4,5},{11,10},{8,9},{15,14},{12,13},{19,18},{16,... | collective-permute-start | bytes 196616 | tf_op jit(solution)/shard_map/ppermute | solution.py:361
  434.2 69.1 %collective-permute-start.29 = (f32[4,96,128]{2,1,0:T(8,128)S(1)}, f32[4,96,128]{2,1,0:T(8,128)S(1)}, u32[]{:S(2)}, u32[]{:S(2)}) collective-permute-start(f32[4,96,128]{2,1,0:T(8,128)S(1)} %get-tuple-element.80), channel_id=1, source_target_pairs={{0,4},{4,8},{8,12},{1,5},{5,9},{9,13},{2,6},{6,10},{10,14},{3,7},{... | collective-permute-start | bytes 589832 | tf_op jit(solution)/shard_map/ppermute | solution.py:365
  501.9 15.3 %collective-permute-start.36 = (f32[16,96,128]{2,1,0:T(8,128)S(1)}, f32[16,96,128]{2,1,0:T(8,128)S(1)}, u32[]{:S(2)}, u32[]{:S(2)}) collective-permute-start(f32[16,96,128]{2,1,0:T(8,128)S(1)} %get-tuple-element.86), channel_id=1, source_target_pairs={{32,0},{80,112},{33,1},{81,113},{34,2},{82,114},{35,3},{83,115},{3... | collective-permute-start | bytes 2359304 | tf_op jit(solution)/shard_map/ppermute | solution.py:364
  503.3 14.6 %collective-permute-start.38 = (f32[16,96,128]{2,1,0:T(8,128)S(1)}, f32[16,96,128]{2,1,0:T(8,128)S(1)}, u32[]{:S(2)}, u32[]{:S(2)}) collective-permute-start(f32[16,96,128]{2,1,0:T(8,128)S(1)} %get-tuple-element.86), channel_id=1, source_target_pairs={{64,0},{48,112},{65,1},{49,113},{66,2},{50,114},{67,3},{51,115},{6... | collective-permute-start | bytes 2359304 | tf_op jit(solution)/shard_map/ppermute | solution.py:364
  504.0 14.6 %collective-permute-start.40 = (f32[16,96,128]{2,1,0:T(8,128)S(1)}, f32[16,96,128]{2,1,0:T(8,128)S(1)}, u32[]{:S(2)}, u32[]{:S(2)}) collective-permute-start(f32[16,96,128]{2,1,0:T(8,128)S(1)} %get-tuple-element.86), channel_id=1, source_target_pairs={{96,0},{16,112},{97,1},{17,113},{98,2},{18,114},{99,3},{19,115},{1... | collective-permute-start | bytes 2359304 | tf_op jit(solution)/shard_map/ppermute | solution.py:364
  517.2 19.5 %collective-permute-start.37 = (f32[16,96,128]{2,1,0:T(8,128)S(1)}, f32[16,96,128]{2,1,0:T(8,128)S(1)}, u32[]{:S(2)}, u32[]{:S(2)}) collective-permute-start(f32[16,96,128]{2,1,0:T(8,128)S(1)} %collective-permute-done.36), channel_id=1, source_target_pairs={{0,16},{112,96},{1,17},{113,97},{2,18},{114,98},{3,19},{115,99},{4... | collective-permute-start | bytes 2359304 | tf_op jit(solution)/shard_map/ppermute | solution.py:368
  517.9 18.7 %collective-permute-start.39 = (f32[16,96,128]{2,1,0:T(8,128)S(1)}, f32[16,96,128]{2,1,0:T(8,128)S(1)}, u32[]{:S(2)}, u32[]{:S(2)}) collective-permute-start(f32[16,96,128]{2,1,0:T(8,128)S(1)} %collective-permute-done.38), channel_id=1, source_target_pairs={{0,48},{112,64},{1,49},{113,65},{2,50},{114,66},{3,51},{115,67},{4... | collective-permute-start | bytes 2359304 | tf_op jit(solution)/shard_map/ppermute | solution.py:368
  518.6 65.1 %collective-permute-start.41 = (f32[16,96,128]{2,1,0:T(8,128)S(1)}, f32[16,96,128]{2,1,0:T(8,128)S(1)}, u32[]{:S(2)}, u32[]{:S(2)}) collective-permute-start(f32[16,96,128]{2,1,0:T(8,128)S(1)} %collective-permute-done.40), channel_id=1, source_target_pairs={{0,80},{112,32},{1,81},{113,33},{2,82},{114,34},{3,83},{115,35},{4... | collective-permute-start | bytes 2359304 | tf_op jit(solution)/shard_map/ppermute | solution.py:368
  (20 other events, 133.5 us)

commit v4 on v3

--- a/solution.py
+++ b/solution.py
@@ -11,16 +11,20 @@
 STEPS = 3
 ROWS = 8
 TILE = 16
+EARLY = 16
 DIRECT = 48
 
 EVEN_CUTS = [(0, 1), (1, 0), (2, 3), (3, 2), (4, 5), (5, 4), (6, 7), (7, 6)]
 ODD_CUTS = [(1, 2), (2, 1), (3, 4), (4, 3), (5, 6), (6, 5)]
 RELAYS = [
+    ([(6, 0), (1, 7)], [(0, 5), (7, 2)]),
+    ([(4, 0), (3, 7)], [(0, 3), (7, 4)]),
     ([(2, 0), (5, 7)], [(0, 1), (7, 6)]),
-    ([(4, 0), (3, 7)], [(0, 3), (7, 4)]),
-    ([(6, 0), (1, 7)], [(0, 5), (7, 2)]),
 ]
+CORNERS_UP = [(4 * a + k, 4 * b + k + 1) for a, b in EVEN_CUTS for k in range(3)]
+CORNERS_DOWN = [(4 * a + k + 1, 4 * b + k) for a, b in EVEN_CUTS for k in range(3)]
 VMEM = 20 * 1024 * 1024
+PART_VMEM = 24 * 1024 * 1024
 
 
 def struct(*shape):
@@ -47,6 +51,9 @@
     def edge(s):
         return stored(s) if first else s
 
+    def z_edge(s):
+        return stored(s) - odd if first else s
+
     def main(s, r):
         ref = planes[s][0]
         return ref[r] if len(ref.shape) == 3 else ref[0, r]
@@ -54,10 +61,14 @@
     def one_row(r, before, after):
         for s in range(4):
             c = main(s, r)
-            over_even, over_odd, over_on = (v[edge(s), pl.ds(r, 1), :] for v in (z_even, z_odd, z_on))
-            over_odd = jnp.where(2 * i < blocks, over_odd, over_on)
-            below = jnp.where(z == 0, jnp.where(pz_odd, over_even, over_odd), pltpu.roll(c, 1, 0))
-            above = jnp.where(z == depth - 1, jnp.where(pz_odd, over_odd, over_even), pltpu.roll(c, depth - 1, 0))
+            if s < 3:
+                over_even, over_odd, over_on = (v[z_edge(s), pl.ds(r, 1), :] for v in (z_even, z_odd, z_on))
+                over_odd = jnp.where(2 * i < blocks, over_odd, over_on)
+                low, high = jnp.where(pz_odd, over_even, over_odd), jnp.where(pz_odd, over_odd, over_even)
+            else:
+                low = high = 0.0
+            below = jnp.where(z == 0, low, pltpu.roll(c, 1, 0))
+            above = jnp.where(z == depth - 1, high, pltpu.roll(c, depth - 1, 0))
             total = (before(s) + after(s)) + (below + above)
             if s > 0:
                 total = total + main(s - 1, r)
@@ -128,8 +139,8 @@
 
     half = rows // ROWS // 2
     half_ends = [
-        pl.BlockSpec((4, ROWS, levels), lambda i, odd_ref: (0, jnp.minimum(i, half - 1), 0)),
-        pl.BlockSpec((4, ROWS, levels), lambda i, odd_ref: (0, jnp.maximum(i - half, 0), 0)),
+        pl.BlockSpec((3, ROWS, levels), lambda i, odd_ref: (0, jnp.minimum(i, half - 1), 0)),
+        pl.BlockSpec((3, ROWS, levels), lambda i, odd_ref: (0, jnp.maximum(i - half, 0), 0)),
     ]
     face = pl.BlockSpec((ROWS, depth, levels), lambda i, odd_ref: (i, 0, 0))
     out_specs = [face, face, block(4 if last else 2)]
@@ -146,11 +157,11 @@
             + specs(middle(1))
             + specs(middle(2))
             + specs(None)
-            + [block(4), fixed(4, depth, levels), fixed(4, depth, levels), ends(4), *half_ends],
+            + [block(4), fixed(4, depth, levels), fixed(4, depth, levels), ends(3), *half_ends],
             out_specs=out_specs,
         ),
         out_shape=out_shape,
-        compiler_params=pltpu.CompilerParams(vmem_limit_bytes=VMEM),
+        compiler_params=pltpu.CompilerParams(vmem_limit_bytes=PART_VMEM),
         cost_estimate=pl.CostEstimate(flops=60_000_000, bytes_accessed=40_000_000, transcendentals=0),
         name="partial_step",
     )(odd, *([o] * 3), *([mid] * 6), *([e] * 3), inverse, *halo_ends)
@@ -162,10 +173,12 @@
     return jnp.where(pz_odd, low, high), jnp.where(pz_odd, high, low)
 
 
-def finish_even_kernel(odd_ref, part, halo, face, x_ends, z_ends):
+def finish_even_kernel(part, halo, low, high, face, x_ends):
     i, blocks = pl.program_id(0), pl.num_programs(0)
+    depth = face.shape[1]
     face[...] = part[...] + 0.1 * halo[...]
-    z_ends[0], z_ends[1] = z_ends_of(odd_ref, face)
+    face[:, 0, :] = face[:, 0, :] + 0.1 * low[...]
+    face[:, depth - 1, :] = face[:, depth - 1, :] + 0.1 * high[...]
 
     @pl.when(i == 0)
     def _():
@@ -176,64 +189,69 @@
         x_ends[1] = face[TILE - 1]
 
 
-def finish_even(odd, part, halo):
+def finish_even(part, halo, low, high):
     rows, depth, levels = part.shape
-    face = pl.BlockSpec((TILE, depth, levels), lambda i, _: (i, 0, 0))
+    face = pl.BlockSpec((TILE, depth, levels), lambda i: (i, 0, 0))
+    column = pl.BlockSpec((TILE, levels), lambda i: (i, 0))
     return pl.pallas_call(
         finish_even_kernel,
-        grid_spec=pltpu.PrefetchScalarGridSpec(
-            num_scalar_prefetch=1,
-            grid=(rows // TILE,),
-            in_specs=[face, face],
-            out_specs=[face, fixed(2, depth, levels), pl.BlockSpec((2, TILE, levels), lambda i, _: (0, i, 0))],
-        ),
-        out_shape=[struct(*part.shape), struct(2, depth, levels), struct(2, rows, levels)],
+        grid=(rows // TILE,),
+        in_specs=[face, face, column, column],
+        out_specs=[face, fixed(2, depth, levels)],
+        out_shape=[struct(*part.shape), struct(2, depth, levels)],
         compiler_params=pltpu.CompilerParams(vmem_limit_bytes=VMEM),
         cost_estimate=pl.CostEstimate(flops=6_000_000, bytes_accessed=9_500_000, transcendentals=0),
         name="finish_even",
-    )(odd, part, halo)
-
-
-def odd_halo(i, halo, relayed, store):
-    straight = DIRECT // TILE
-
-    @pl.when(i < straight)
-    def _():
-        store(halo[...])
-
-    @pl.when(i >= straight)
-    def _():
-        store(relayed[0][...] + relayed[1][...] + relayed[2][...])
-
-
-def odd_halo_specs(depth, levels):
-    straight = DIRECT // TILE
-    top = pl.BlockSpec((TILE, depth, levels), lambda i, *_: (jnp.minimum(i, straight - 1), 0, 0))
-    rest = pl.BlockSpec((TILE, depth, levels), lambda i, *_: (jnp.maximum(i - straight, 0), 0, 0))
-    return top, rest
-
-
-def finish_odd_kernel(odd_ref, part, halo, r0, r1, r2, mx_low, mx_high, mz_even, mz_odd, ex, ez, *outs):
-    face, top, rest, x_low, x_high, z_even, z_odd = outs
+    )(part, halo, low, high)
+
+
+def columns_kernel(halo, low, high):
+    low[...] = halo[:, 0, :]
+    high[...] = halo[:, halo.shape[1] - 1, :]
+
+
+def columns(halo):
+    rows, _, levels = halo.shape
+    return pl.pallas_call(
+        columns_kernel,
+        in_specs=[pl.BlockSpec(memory_space=pltpu.VMEM)],
+        out_specs=[pl.BlockSpec(memory_space=pltpu.VMEM)] * 2,
+        out_shape=[struct(rows, levels)] * 2,
+        compiler_params=pltpu.CompilerParams(vmem_limit_bytes=VMEM),
+        cost_estimate=pl.CostEstimate(flops=1_000_000, bytes_accessed=100_000, transcendentals=0),
+        name="columns",
+    )(halo)
+
+
+def odd_pieces():
+    return ((0, EARLY // TILE), (EARLY // TILE, DIRECT // TILE), (DIRECT // TILE, None))
+
+
+def in_piece(i, piece):
+    return i >= piece[0] if piece[1] is None else (i >= piece[0]) & (i < piece[1])
+
+
+def odd_specs(rows, depth, levels):
+    def spec(start, stop):
+        last = (rows // TILE if stop is None else stop) - start - 1
+        return pl.BlockSpec((TILE, depth, levels), lambda i, *_: (jnp.clip(i - start, 0, last), 0, 0))
+
+    return [spec(*piece) for piece in odd_pieces()]
+
+
+def finish_odd_kernel(odd_ref, part, early, late, r0, r1, r2, mx_low, mx_high, mz_even, mz_odd, ex, *outs):
+    face, *pieces, x_low, x_high, z_even, z_odd = outs
     i, blocks = pl.program_id(0), pl.num_programs(0)
 
-    def store(h):
-        face[...] = part[...] + 0.1 * h
-
-    odd_halo(i, halo, (r0, r1, r2), store)
-
-    @pl.when(i < DIRECT // TILE)
-    def _():
-        top[...] = face[...]
-
-    @pl.when(i >= DIRECT // TILE)
-    def _():
-        rest[...] = face[...]
+    for (piece, out), halos in zip(zip(odd_pieces(), pieces), ((early,), (late,), (r0, r1, r2))):
+
+        @pl.when(in_piece(i, piece))
+        def _(out=out, halos=halos):
+            face[...] = part[...] + 0.1 * sum((h[...] for h in halos[1:]), halos[0][...])
+            out[...] = face[...]
 
     z_even[0], z_odd[0] = z_ends_of(odd_ref, face)
-    for k, (z_out, z_mid) in enumerate(((z_even, mz_even), (z_odd, mz_odd))):
-        z_out[1:3] = z_mid[...]
-        z_out[3] = ez[k]
+    z_even[1:3], z_odd[1:3] = mz_even[...], mz_odd[...]
 
     @pl.when(i == 0)
     def _():
@@ -248,10 +266,10 @@
         x_high[3] = ex[1]
 
 
-def finish_odd(odd, part, halo, relayed, mids, ex, ez):
+def finish_odd(odd, part, halos, relayed, mids, ex):
     rows, depth, levels = part.shape
     face = pl.BlockSpec((TILE, depth, levels), lambda i, _: (i, 0, 0))
-    top, rest = odd_halo_specs(depth, levels)
+    early, late, relay = odd_specs(rows, depth, levels)
 
     def ends(planes):
         return pl.BlockSpec((planes, TILE, levels), lambda i, _: (0, i, 0))
@@ -262,16 +280,17 @@
         grid_spec=pltpu.PrefetchScalarGridSpec(
             num_scalar_prefetch=1,
             grid=(rows // TILE,),
-            in_specs=[face, top, rest, rest, rest, x2, x2, ends(2), ends(2), x2, ends(2)],
-            out_specs=[face, top, rest, x4, x4, ends(4), ends(4)],
+            in_specs=[face, early, late, relay, relay, relay, x2, x2, ends(2), ends(2), x2],
+            out_specs=[face, early, late, relay, x4, x4, ends(3), ends(3)],
         ),
-        out_shape=[struct(*part.shape), struct(DIRECT, depth, levels), struct(rows - DIRECT, depth, levels)]
+        out_shape=[struct(*part.shape)]
+        + [struct(size, depth, levels) for size in (EARLY, DIRECT - EARLY, rows - DIRECT)]
         + [struct(4, depth, levels)] * 2
-        + [struct(4, rows, levels)] * 2,
+        + [struct(3, rows, levels)] * 2,
         compiler_params=pltpu.CompilerParams(vmem_limit_bytes=VMEM),
         cost_estimate=pl.CostEstimate(flops=6_000_000, bytes_accessed=12_600_000, transcendentals=0),
         name="finish_odd",
-    )(odd, part, halo, *relayed, *mids, ex, ez)
+    )(odd, part, *halos, *relayed, *mids, ex)
 
 
 def place_kernel(at_ref, part, *refs):
@@ -280,14 +299,19 @@
     copies = []
     for k in range(part.shape[0] // TILE):
         own = pl.ds(k * TILE, TILE)
-        if len(halos) == 1:
+        if len(halos) == 3:
             halo = halos[0][own]
-        elif k < DIRECT // TILE:
+        elif k * TILE < EARLY:
             halo = halos[0][own]
+        elif k * TILE < DIRECT:
+            halo = halos[1][pl.ds(k * TILE - EARLY, TILE)]
         else:
             rest = pl.ds(k * TILE - DIRECT, TILE)
-            halo = halos[1][rest] + halos[2][rest] + halos[3][rest]
+            halo = halos[2][rest] + halos[3][rest] + halos[4][rest]
         done[own] = part[own] + 0.1 * halo
+        if len(halos) == 3:
+            for column, at in zip(halos[1:], (0, part.shape[1] - 1)):
+                done[own, at, :] = done[own, at, :] + 0.1 * column[own]
         copies.append(pltpu.make_async_copy(done.at[own], plane.at[own], sems.at[k]))
         copies[-1].start()
     for copy in copies:
@@ -345,11 +369,12 @@
     first_halo = lax.ppermute(e_first, "py", EVEN_CUTS)
     e, e_rest = pick(density, e_plane, [(0, rows), (TILE, rows)], 50)
     e_halo = lax.ppermute(e_rest, "py", EVEN_CUTS)
-    o, top, rest = pick(density, o_plane, [(0, rows), (0, DIRECT), (DIRECT, rows)], 46)
+    spans = [(0, rows), (0, EARLY), (EARLY, DIRECT), (DIRECT, rows)]
+    o, early, late, rest = pick(density, o_plane, spans, 46)
     mid = density
     rows, depth, _ = o.shape
     x_low, x_high = density[:, 0], density[:, rows - 1]
-    z_low, z_high = density[:, :, 0], density[:, :, depth - 1]
+    z_low, z_high = (lax.dynamic_slice_in_dim(density[:, :, k], odd, 3, 0) for k in (0, depth - 1))
     z_even, z_odd = jnp.where(pz_odd == 1, z_low, z_high), jnp.where(pz_odd == 1, z_high, z_low)
     up = [(k, k + 1) for k in range(3)]
     down = [(b, a) for a, b in up]
@@ -363,20 +388,24 @@
         for to, _ in RELAYS:
             relayed.append(lax.ppermute(rest, "py", to))
         px = [lax.ppermute(x_high, "px", up), lax.ppermute(x_low, "px", down)]
-        o_halo = lax.ppermute(top, "py", ODD_CUTS)
+        o_early = lax.ppermute(early, "py", ODD_CUTS)
         for k, (_, on) in enumerate(RELAYS):
             relayed[k] = lax.ppermute(relayed[k], "py", on)
+        if step == 0:
+            e_halo = jnp.concatenate([first_halo, e_halo])
+        low, high = columns(e_halo)
+        low, high = lax.ppermute(high, ("py", "pz"), CORNERS_UP), lax.ppermute(low, ("py", "pz"), CORNERS_DOWN)
+        o_halos = [o_early, lax.ppermute(late, "py", ODD_CUTS)]
         ends = [*px, z_even, z_odd, z_by]
         o_part, e_part, mid, *mids = partial_step(step, odd_ref, o, mid, e, inverse, ends)
         if step == STEPS - 1:
             break
-        if step == 0:
-            e_halo = jnp.concatenate([first_halo, e_halo])
-        e, ex, ez = finish_even(odd_ref, e_part, e_halo)
+        e, ex = finish_even(e_part, e_halo, low, high)
         e_halo = lax.ppermute(e, "py", EVEN_CUTS)
-        o, top, rest, x_low, x_high, z_even, z_odd = finish_odd(odd_ref, o_part, o_halo, relayed, mids, ex, ez)
-    out = place(e_plane, e_part, (e_halo,), mid)
-    return place(o_plane, o_part, (o_halo, *relayed), out)
+        outs = finish_odd(odd_ref, o_part, o_halos, relayed, mids, ex)
+        o, early, late, rest, x_low, x_high, z_even, z_odd = outs
+    out = place(e_plane, e_part, (e_halo, low, high), mid)
+    return place(o_plane, o_part, (*o_halos, *relayed), out)
 
 
 def solution(mesh):

time: 587 us -> 548 us (0.934)
  the two profiles are of different devices: /device:TPU:76 before, /device:TPU:6 now
where the time goes in v4:
time: 548 us; the launch traced here: 546 us
  waiting for transfers between devices  370 us (68%)
  starting transfers between devices  108 us (20%)
  Pallas kernels  58.2 us (11%)
  local copies, waits for them, and re-layouts  8.14 us (1%)
    ppermute x3, waiting for transfers between devices, local(): o_early = lax.ppermute(early, 'py', ODD_CUTS)  122 us
    ppermute x9, waiting for transfers between devices, local(): relayed[k] = lax.ppermute(relayed[k], 'py', on)  98 us
    ppermute x1, waiting for transfers between devices, local(): first_halo = lax.ppermute(e_first, 'py', EVEN_CUTS)  57.6 us
    pallas_call x3, Pallas kernels, partial_step(): pl.pallas_call(functools.partial(partial_kernel, first, last), grid_spec=...  38.7 us
    ppermute x9, waiting for transfers between devices, local(): relayed.append(lax.ppermute(rest, 'py', to))  33.3 us
    ppermute x3, waiting for transfers between devices, local(): lax.ppermute(high, ('py', 'pz'), CORNERS_UP)  25.6 us
    ppermute x3, waiting for transfers between devices, local(): o_halos = [o_early, lax.ppermute(late, 'py', ODD_CUTS)]  18.9 us
    ppermute x3, starting transfers between devices, local(): lax.ppermute(low, ('py', 'pz'), CORNERS_DOWN)  15.7 us
  transfers between devices with their start and end apart: 52, of which 16 were waited for; matrix products, arithmetic and copies ran while one was open for 1% of the time, Pallas kernels for 9%

profile of v4, /device:TPU:6, one launch (start us, length us, event | category | flops | bytes accessed | tf_op | source)
XLA Modules:
  0.0 546.3 jit_solution(7081560798230993830)
XLA Ops:
  0.0 5.1 shard_map.29
  7.7 2.2 collective-permute-start.14
  12.4 3.5 collective-permute-start.4
  15.9 2.6 collective-permute-start.3
  20.4 57.6 %collective-permute-done.14 = f32[16,96,128]{2,1,0:T(8,128)} collective-permute-done((f32[16,96,128]{2,1,0:T(8,128)S(1)}, f32[16,96,128]{2,1,0:T(8,128)}, u32[]{:S(2)}, u32[]{:S(2)}) %collective-permute-start.14) | collective-permute-done | bytes 786464 | tf_op jit(solution)/shard_map/ppermute | solution.py:369
  86.3 3.4 collective-permute-start.16
  90.3 4.2 collective-permute-start.17
  94.6 3.0 shard_map.28
  98.6 13.1 %partial_step.3 = (f32[64,96,128]{2,1,0:T(8,128)S(1)}, f32[64,96,128]{2,1,0:T(8,128)S(1)}, f32[2,64,96,128]{3,2,1,0:T(8,128)S(1)}, f32[2,96,128]{2,1,0:T(8,128)S...) custom-call(s32[2]{0:T(128)S(1)} %pad_add_fusion.odd_ref, ...), custom_call_target="tpu_custom_call" | custom-call | flops 60000000 | bytes 40000000 | tf_op jit(solution)/shard_map/partial_step/pallas_call | solution.py:151
  116.0 7.2 %collective-permute-start.8 = (f32[16,96,128]{2,1,0:T(8,128)S(1)}, f32[16,96,128]{2,1,0:T(8,128)S(1)}, u32[]{:S(2)}, u32[]{:S(2)}) collective-permute-start(f32[16,96,128]{2,1,0:T(8,128)S(1)} %copy-done.4), channel_id=1, source_target_pairs={{96,0},{16,112},{97,1},{17,113},{98,2},{18,114},{99,3},{19,115},{1... | collective-permute-start | bytes 2359304 | tf_op jit(solution)/shard_map/ppermute | solution.py:389
  125.1 6.3 %collective-permute-start.7 = (f32[32,96,128]{2,1,0:T(8,128)S(1)}, f32[32,96,128]{2,1,0:T(8,128)S(1)}, u32[]{:S(2)}, u32[]{:S(2)}) collective-permute-start(f32[32,96,128]{2,1,0:T(8,128)S(1)} %get-tuple-element.58), channel_id=1, source_target_pairs={{16,32},{32,16},{48,64},{64,48},{80,96},{96,80},{17,33},{33,17},{4... | collective-permute-start | bytes 4718600 | tf_op jit(solution)/shard_map/ppermute | solution.py:398
  132.2 23.3 %collective-permute-done.8 = f32[16,96,128]{2,1,0:T(8,128)S(1)} collective-permute-done((f32[16,96,128]{2,1,0:T(8,128)S(1)}, f32[16,96,128]{2,1,0:T(8,128)S(1)}, u32[]{:S(2)}, u32[]{:S(2)}) %collective-permute-start.8) | collective-permute-done | bytes 786464 | tf_op jit(solution)/shard_map/ppermute | solution.py:389
  156.8 45.3 %collective-permute-done.6.early = f32[16,96,128]{2,1,0:T(8,128)S(1)} collective-permute-done((f32[16,96,128]{2,1,0:T(8,128)S(1)}, f32[16,96,128]{2,1,0:T(8,128)S(1)}, u32[]{:S(2)}, u32[]{:S(2)}) %collective-permute-start.6) | collective-permute-done | bytes 786464 | tf_op jit(solution)/shard_map/ppermute | solution.py:391
  202.8 14.8 %collective-permute-done.13.r2 = f32[16,96,128]{2,1,0:T(8,128)S(1)} collective-permute-done((f32[16,96,128]{2,1,0:T(8,128)S(1)}, f32[16,96,128]{2,1,0:T(8,128)S(1)}, u32[]{:S(2)}, u32[]{:S(2)}) %collective-permute-start.13) | collective-permute-done | bytes 786464 | tf_op jit(solution)/shard_map/ppermute | solution.py:393
  217.6 18.2 %collective-permute-done.7.late = f32[32,96,128]{2,1,0:T(8,128)S(1)} collective-permute-done((f32[32,96,128]{2,1,0:T(8,128)S(1)}, f32[32,96,128]{2,1,0:T(8,128)S(1)}, u32[]{:S(2)}, u32[]{:S(2)}) %collective-permute-start.7) | collective-permute-done | bytes 1572896 | tf_op jit(solution)/shard_map/ppermute | solution.py:398
  237.4 4.1 collective-permute-start.18
  242.9 4.9 collective-permute-start.22
  249.8 4.9 collective-permute-done.21.refs_16_
  257.4 4.6 collective-permute-done.23.refs_17_
  263.9 5.1 collective-permute-start.34
  269.1 11.2 %partial_step.4 = (f32[64,96,128]{2,1,0:T(8,128)S(1)}, f32[64,96,128]{2,1,0:T(8,128)S(1)}, f32[2,64,96,128]{3,2,1,0:T(8,128)S(1)}, f32[2,96,128]{2,1,0:T(8,128)S...) custom-call(s32[2]{0:T(128)S(1)} %pad_add_fusion.odd_ref, ...), custom_call_target="tpu_custom_call" | custom-call | flops 60000000 | bytes 40000000 | tf_op jit(solution)/shard_map/partial_step/pallas_call | solution.py:151
  282.6 8.7 %collective-permute-start.24 = (f32[16,96,128]{2,1,0:T(8,128)S(1)}, f32[16,96,128]{2,1,0:T(8,128)S(1)}, u32[]{:S(2)}, u32[]{:S(2)}) collective-permute-start(f32[16,96,128]{2,1,0:T(8,128)S(1)} %get-tuple-element.77), channel_id=1, source_target_pairs={{16,32},{32,16},{48,64},{64,48},{80,96},{96,80},{17,33},{33,17},{4... | collective-permute-start | bytes 2359304 | tf_op jit(solution)/shard_map/ppermute | solution.py:391
  294.7 76.5 %collective-permute-done.24.early = f32[16,96,128]{2,1,0:T(8,128)S(1)} collective-permute-done((f32[16,96,128]{2,1,0:T(8,128)S(1)}, f32[16,96,128]{2,1,0:T(8,128)S(1)}, u32[]{:S(2)}, u32[]{:S(2)}) %collective-permute-start.24) | collective-permute-done | bytes 786464 | tf_op jit(solution)/shard_map/ppermute | solution.py:391
  372.5 30.7 %collective-permute-done.31.r2 = f32[16,96,128]{2,1,0:T(8,128)S(1)} collective-permute-done((f32[16,96,128]{2,1,0:T(8,128)S(1)}, f32[16,96,128]{2,1,0:T(8,128)S(1)}, u32[]{:S(2)}, u32[]{:S(2)}) %collective-permute-start.31) | collective-permute-done | bytes 786464 | tf_op jit(solution)/shard_map/ppermute | solution.py:393
  408.3 2.5 collective-permute-start.38
  412.1 3.1 collective-permute-done.38.refs_16_
  418.2 5.7 %collective-permute-start.42 = (f32[32,96,128]{2,1,0:T(8,128)S(1)}, f32[32,96,128]{2,1,0:T(8,128)S(1)}, u32[]{:S(2)}, u32[]{:S(2)}) collective-permute-start(f32[32,96,128]{2,1,0:T(8,128)S(1)} %get-tuple-element.97), channel_id=1, source_target_pairs={{16,32},{32,16},{48,64},{64,48},{80,96},{96,80},{17,33},{33,17},{4... | collective-permute-start | bytes 4718600 | tf_op jit(solution)/shard_map/ppermute | solution.py:398
  429.2 9.9 %collective-permute-done.43 = f32[16,96,128]{2,1,0:T(8,128)S(1)} collective-permute-done((f32[16,96,128]{2,1,0:T(8,128)S(1)}, f32[16,96,128]{2,1,0:T(8,128)S(1)}, u32[]{:S(2)}, u32[]{:S(2)}) %collective-permute-start.43) | collective-permute-done | bytes 786464 | tf_op jit(solution)/shard_map/ppermute | solution.py:389
  439.1 6.3 %collective-permute-start.51 = (f32[64,128]{1,0:T(8,128)S(1)}, f32[64,128]{1,0:T(8,128)S(1)}, u32[]{:S(2)}, u32[]{:S(2)}) collective-permute-start(f32[64,128]{1,0:T(8,128)S(1)} %get-tuple-element.101), channel_id=1, source_target_pairs={{1,16},{2,17},{3,18},{17,0},{18,1},{19,2},{33,48},{34,49},{35,50},... | collective-permute-start | bytes 98312 | tf_op jit(solution)/shard_map/ppermute | solution.py:397
  448.1 25.6 %collective-permute-done.50.refs_1_ = f32[64,128]{1,0:T(8,128)S(1)} collective-permute-done((f32[64,128]{1,0:T(8,128)S(1)}, f32[64,128]{1,0:T(8,128)S(1)}, u32[]{:S(2)}, u32[]{:S(2)}) %collective-permute-start.50) | collective-permute-done | bytes 32800 | tf_op jit(solution)/shard_map/ppermute | solution.py:397
  475.8 14.3 %partial_step.5 = (f32[64,96,128]{2,1,0:T(8,128)S(1)}, f32[64,96,128]{2,1,0:T(8,128)S(1)}, f32[4,64,96,128]{3,2,1,0:T(8,128)}) custom-call(s32[2]{0:T(128)S(1)} %pad_add_fusion.odd_ref, f32[64,96,128]{2,1,0:T(8,128)S(1)} %get-tuple-element.88.refs_0_.refs_1_.refs_2_, f32[64,96,128]{2,1,0:T(8,128)S(1)} %get-tuple-element.88.refs_0_.refs_1_.refs_2_, ...), custom_call_target="tpu_custom_call" | custom-call | flops 60000000 | bytes 40000000 | tf_op jit(solution)/shard_map/partial_step/pallas_call | solution.py:151
  491.9 52.5 %collective-permute-done.48.refs_4_ = f32[16,96,128]{2,1,0:T(8,128)S(1)} collective-permute-done((f32[16,96,128]{2,1,0:T(8,128)S(1)}, f32[16,96,128]{2,1,0:T(8,128)S(1)}, u32[]{:S(2)}, u32[]{:S(2)}) %collective-permute-start.48) | collective-permute-done | bytes 786464 | tf_op jit(solution)/shard_map/ppermute | solution.py:393
  (107 shorter events, 64.9 us)
Async XLA Ops:
  5.1 77.3 %collective-permute-start.15 = (f32[48,96,128]{2,1,0:T(8,128)}, f32[48,96,128]{2,1,0:T(8,128)}, u32[]{:S(2)}, u32[]{:S(2)}) collective-permute-start(f32[48,96,128]{2,1,0:T(8,128)} %get-tuple-element.65), channel_id=1, source_target_pairs={{0,16},{16,0},{32,48},{48,32},{64,80},{80,64},{96,112},{112,96},{1... | collective-permute-start | bytes 7077896 | tf_op jit(solution)/shard_map/ppermute | solution.py:371
  7.7 70.3 %collective-permute-start.14 = (f32[16,96,128]{2,1,0:T(8,128)S(1)}, f32[16,96,128]{2,1,0:T(8,128)}, u32[]{:S(2)}, u32[]{:S(2)}) collective-permute-start(f32[16,96,128]{2,1,0:T(8,128)S(1)} %shard_map.30), channel_id=1, source_target_pairs={{0,16},{16,0},{32,48},{48,32},{64,80},{80,64},{96,112},{112,96},{1... | collective-permute-start | bytes 2359304 | tf_op jit(solution)/shard_map/ppermute | solution.py:369
  12.4 68.8 %collective-permute-start.4 = (f32[3,32,128]{2,1,0:T(8,128)S(1)}, f32[3,32,128]{2,1,0:T(8,128)S(1)}, u32[]{:S(2)}, u32[]{:S(2)}) collective-permute-start(f32[3,32,128]{2,1,0:T(8,128)S(1)} %get-tuple-element.113), channel_id=1, source_target_pairs={{1,3},{2,0},{5,7},{6,4},{9,11},{10,8},{13,15},{14,12},{17,19},{18,... | collective-permute-start | bytes 147464 | tf_op jit(solution)/shard_map/ppermute | solution.py:383
  15.9 70.4 %collective-permute-start.3 = (f32[3,32,128]{2,1,0:T(8,128)S(1)}, f32[3,32,128]{2,1,0:T(8,128)S(1)}, u32[]{:S(2)}, u32[]{:S(2)}) collective-permute-start(f32[3,32,128]{2,1,0:T(8,128)S(1)} %get-tuple-element.114), channel_id=1, source_target_pairs={{1,2},{2,1},{5,6},{6,5},{9,10},{10,9},{13,14},{14,13},{17,18},{18,... | collective-permute-start | bytes 147464 | tf_op jit(solution)/shard_map/ppermute | solution.py:385
  18.5 80.0 %collective-permute-start.2 = (f32[3,64,128]{2,1,0:T(8,128)}, f32[3,64,128]{2,1,0:T(8,128)}, u32[]{:S(2)}, u32[]{:S(2)}) collective-permute-start(f32[3,64,128]{2,1,0:T(8,128)} %get-tuple-element.108), channel_id=1, source_target_pairs={{0,1},{1,0},{2,3},{3,2},{4,5},{5,4},{6,7},{7,6},{8,9},{9,8},{10,11... | collective-permute-start | bytes 294920 | tf_op jit(solution)/shard_map/ppermute | solution.py:384
  78.0 20.5 %collective-permute-start = (f32[4,96,128]{2,1,0:T(8,128)}, f32[4,96,128]{2,1,0:T(8,128)}, u32[]{:S(2)}, u32[]{:S(2)}) collective-permute-start(f32[4,96,128]{2,1,0:T(8,128)} %get-tuple-element.106), channel_id=1, source_target_pairs={{0,4},{4,8},{8,12},{1,5},{5,9},{9,13},{2,6},{6,10},{10,14},{3,7},{... | collective-permute-start | bytes 589832 | tf_op jit(solution)/shard_map/ppermute | solution.py:390
  86.3 25.4 %collective-permute-start.16 = (f32[64,128]{1,0:T(8,128)}, f32[64,128]{1,0:T(8,128)}, u32[]{:S(2)}, u32[]{:S(2)}) collective-permute-start(f32[64,128]{1,0:T(8,128)} %get-tuple-element.66), channel_id=1, source_target_pairs={{0,17},{1,18},{2,19},{16,1},{17,2},{18,3},{32,49},{33,50},{34,51},... | collective-permute-start | bytes 98312 | tf_op jit(solution)/shard_map/ppermute | solution.py:397
  90.3 21.4 %collective-permute-start.17 = (f32[64,128]{1,0:T(8,128)}, f32[64,128]{1,0:T(8,128)}, u32[]{:S(2)}, u32[]{:S(2)}) collective-permute-start(f32[64,128]{1,0:T(8,128)} %get-tuple-element.67), channel_id=1, source_target_pairs={{1,16},{2,17},{3,18},{17,0},{18,1},{19,2},{33,48},{34,49},{35,50},... | collective-permute-start | bytes 98312 | tf_op jit(solution)/shard_map/ppermute | solution.py:397
  113.7 142.3 %collective-permute-start.32 = (f32[64,96,128]{2,1,0:T(8,128)S(1)}, f32[64,96,128]{2,1,0:T(8,128)S(1)}, u32[]{:S(2)}, u32[]{:S(2)}) collective-permute-start(f32[64,96,128]{2,1,0:T(8,128)S(1)} %get-tuple-element.71.refs_9_.refs_10_.refs_11_), channel_id=1, source_target_pairs={{0,16},{16,0},{32,48},{48,32},{64,80},{80,64},{96,112},{112,96},{1... | collective-permute-start | bytes 9437192 | tf_op jit(solution)/shard_map/ppermute | solution.py:404
  116.0 39.5 %collective-permute-start.8 = (f32[16,96,128]{2,1,0:T(8,128)S(1)}, f32[16,96,128]{2,1,0:T(8,128)S(1)}, u32[]{:S(2)}, u32[]{:S(2)}) collective-permute-start(f32[16,96,128]{2,1,0:T(8,128)S(1)} %copy-done.4), channel_id=1, source_target_pairs={{96,0},{16,112},{97,1},{17,113},{98,2},{18,114},{99,3},{19,115},{1... | collective-permute-start | bytes 2359304 | tf_op jit(solution)/shard_map/ppermute | solution.py:389
  123.2 78.9 %collective-permute-start.6 = (f32[16,96,128]{2,1,0:T(8,128)S(1)}, f32[16,96,128]{2,1,0:T(8,128)S(1)}, u32[]{:S(2)}, u32[]{:S(2)}) collective-permute-start(f32[16,96,128]{2,1,0:T(8,128)S(1)} %get-tuple-element.57), channel_id=1, source_target_pairs={{16,32},{32,16},{48,64},{64,48},{80,96},{96,80},{17,33},{33,17},{4... | collective-permute-start | bytes 2359304 | tf_op jit(solution)/shard_map/ppermute | solution.py:391
  125.1 110.7 %collective-permute-start.7 = (f32[32,96,128]{2,1,0:T(8,128)S(1)}, f32[32,96,128]{2,1,0:T(8,128)S(1)}, u32[]{:S(2)}, u32[]{:S(2)}) collective-permute-start(f32[32,96,128]{2,1,0:T(8,128)S(1)} %get-tuple-element.58), channel_id=1, source_target_pairs={{16,32},{32,16},{48,64},{64,48},{80,96},{96,80},{17,33},{33,17},{4... | collective-permute-start | bytes 4718600 | tf_op jit(solution)/shard_map/ppermute | solution.py:398
  131.5 71.3 %collective-permute-start.11 = (f32[16,96,128]{2,1,0:T(8,128)S(1)}, f32[16,96,128]{2,1,0:T(8,128)S(1)}, u32[]{:S(2)}, u32[]{:S(2)}) collective-permute-start(f32[16,96,128]{2,1,0:T(8,128)S(1)} %collective-permute-done.10), channel_id=1, source_target_pairs={{0,48},{112,64},{1,49},{113,65},{2,50},{114,66},{3,51},{115,67},{4... | collective-permute-start | bytes 2359304 | tf_op jit(solution)/shard_map/ppermute | solution.py:393
  155.5 62.1 %collective-permute-start.13 = (f32[16,96,128]{2,1,0:T(8,128)S(1)}, f32[16,96,128]{2,1,0:T(8,128)S(1)}, u32[]{:S(2)}, u32[]{:S(2)}) collective-permute-start(f32[16,96,128]{2,1,0:T(8,128)S(1)} %collective-permute-done.12), channel_id=1, source_target_pairs={{0,16},{112,96},{1,17},{113,97},{2,18},{114,98},{3,19},{115,99},{4... | collective-permute-start | bytes 2359304 | tf_op jit(solution)/shard_map/ppermute | solution.py:393
  237.4 31.7 %collective-permute-start.18 = (f32[4,96,128]{2,1,0:T(8,128)S(1)}, f32[4,96,128]{2,1,0:T(8,128)S(1)}, u32[]{:S(2)}, u32[]{:S(2)}) collective-permute-start(f32[4,96,128]{2,1,0:T(8,128)S(1)} %get-tuple-element.72), channel_id=1, source_target_pairs={{0,4},{4,8},{8,12},{1,5},{5,9},{9,13},{2,6},{6,10},{10,14},{3,7},{... | collective-permute-start | bytes 589832 | tf_op jit(solution)/shard_map/ppermute | solution.py:390
  241.5 27.6 %collective-permute-start.19 = (f32[4,96,128]{2,1,0:T(8,128)S(1)}, f32[4,96,128]{2,1,0:T(8,128)S(1)}, u32[]{:S(2)}, u32[]{:S(2)}) collective-permute-start(f32[4,96,128]{2,1,0:T(8,128)S(1)} %get-tuple-element.73), channel_id=1, source_target_pairs={{4,0},{8,4},{12,8},{5,1},{9,5},{13,9},{6,2},{10,6},{14,10},{7,3},{... | collective-permute-start | bytes 589832 | tf_op jit(solution)/shard_map/ppermute | solution.py:390
  254.7 36.6 %collective-permute-start.26 = (f32[16,96,128]{2,1,0:T(8,128)S(1)}, f32[16,96,128]{2,1,0:T(8,128)S(1)}, u32[]{:S(2)}, u32[]{:S(2)}) collective-permute-start(f32[16,96,128]{2,1,0:T(8,128)S(1)} %get-tuple-element.79), channel_id=1, source_target_pairs={{96,0},{16,112},{97,1},{17,113},{98,2},{18,114},{99,3},{19,115},{1... | collective-permute-start | bytes 2359304 | tf_op jit(solution)/shard_map/ppermute | solution.py:389
  281.0 142.9 %collective-permute-start.49 = (f32[64,96,128]{2,1,0:T(8,128)S(1)}, f32[64,96,128]{2,1,0:T(8,128)S(1)}, u32[]{:S(2)}, u32[]{:S(2)}) collective-permute-start(f32[64,96,128]{2,1,0:T(8,128)S(1)} %get-tuple-element.90.refs_9_.refs_10_.refs_11_), channel_id=1, source_target_pairs={{0,16},{16,0},{32,48},{48,32},{64,80},{80,64},{96,112},{112,96},{1... | collective-permute-start | bytes 9437192 | tf_op jit(solution)/shard_map/ppermute | solution.py:404
  282.6 88.6 %collective-permute-start.24 = (f32[16,96,128]{2,1,0:T(8,128)S(1)}, f32[16,96,128]{2,1,0:T(8,128)S(1)}, u32[]{:S(2)}, u32[]{:S(2)}) collective-permute-start(f32[16,96,128]{2,1,0:T(8,128)S(1)} %get-tuple-element.77), channel_id=1, source_target_pairs={{16,32},{32,16},{48,64},{64,48},{80,96},{96,80},{17,33},{33,17},{4... | collective-permute-start | bytes 2359304 | tf_op jit(solution)/shard_map/ppermute | solution.py:391
  291.3 112.6 %collective-permute-start.25 = (f32[32,96,128]{2,1,0:T(8,128)S(1)}, f32[32,96,128]{2,1,0:T(8,128)S(1)}, u32[]{:S(2)}, u32[]{:S(2)}) collective-permute-start(f32[32,96,128]{2,1,0:T(8,128)S(1)} %get-tuple-element.78), channel_id=1, source_target_pairs={{16,32},{32,16},{48,64},{64,48},{80,96},{96,80},{17,33},{33,17},{4... | collective-permute-start | bytes 4718600 | tf_op jit(solution)/shard_map/ppermute | solution.py:398
  293.2 79.2 %collective-permute-start.27 = (f32[16,96,128]{2,1,0:T(8,128)S(1)}, f32[16,96,128]{2,1,0:T(8,128)S(1)}, u32[]{:S(2)}, u32[]{:S(2)}) collective-permute-start(f32[16,96,128]{2,1,0:T(8,128)S(1)} %collective-permute-done.26), channel_id=1, source_target_pairs={{0,80},{112,32},{1,81},{113,33},{2,82},{114,34},{3,83},{115,35},{4... | collective-permute-start | bytes 2359304 | tf_op jit(solution)/shard_map/ppermute | solution.py:393
  293.9 78.5 %collective-permute-start.29 = (f32[16,96,128]{2,1,0:T(8,128)S(1)}, f32[16,96,128]{2,1,0:T(8,128)S(1)}, u32[]{:S(2)}, u32[]{:S(2)}) collective-permute-start(f32[16,96,128]{2,1,0:T(8,128)S(1)} %collective-permute-done.28), channel_id=1, source_target_pairs={{0,48},{112,64},{1,49},{113,65},{2,50},{114,66},{3,51},{115,67},{4... | collective-permute-start | bytes 2359304 | tf_op jit(solution)/shard_map/ppermute | solution.py:393
  371.2 32.0 %collective-permute-start.31 = (f32[16,96,128]{2,1,0:T(8,128)S(1)}, f32[16,96,128]{2,1,0:T(8,128)S(1)}, u32[]{:S(2)}, u32[]{:S(2)}) collective-permute-start(f32[16,96,128]{2,1,0:T(8,128)S(1)} %collective-permute-done.30), channel_id=1, source_target_pairs={{0,16},{112,96},{1,17},{113,97},{2,18},{114,98},{3,19},{115,99},{4... | collective-permute-start | bytes 2359304 | tf_op jit(solution)/shard_map/ppermute | solution.py:393
  415.1 24.0 %collective-permute-start.43 = (f32[16,96,128]{2,1,0:T(8,128)S(1)}, f32[16,96,128]{2,1,0:T(8,128)S(1)}, u32[]{:S(2)}, u32[]{:S(2)}) collective-permute-start(f32[16,96,128]{2,1,0:T(8,128)S(1)} %get-tuple-element.98), channel_id=1, source_target_pairs={{96,0},{16,112},{97,1},{17,113},{98,2},{18,114},{99,3},{19,115},{1... | collective-permute-start | bytes 2359304 | tf_op jit(solution)/shard_map/ppermute | solution.py:389
  416.8 28.7 %collective-permute-start.45 = (f32[16,96,128]{2,1,0:T(8,128)S(1)}, f32[16,96,128]{2,1,0:T(8,128)S(1)}, u32[]{:S(2)}, u32[]{:S(2)}) collective-permute-start(f32[16,96,128]{2,1,0:T(8,128)S(1)} %get-tuple-element.98), channel_id=1, source_target_pairs={{64,0},{48,112},{65,1},{49,113},{66,2},{50,114},{67,3},{51,115},{6... | collective-permute-start | bytes 2359304 | tf_op jit(solution)/shard_map/ppermute | solution.py:389
  417.5 29.9 %collective-permute-start.47 = (f32[16,96,128]{2,1,0:T(8,128)S(1)}, f32[16,96,128]{2,1,0:T(8,128)S(1)}, u32[]{:S(2)}, u32[]{:S(2)}) collective-permute-start(f32[16,96,128]{2,1,0:T(8,128)S(1)} %get-tuple-element.98), channel_id=1, source_target_pairs={{32,0},{80,112},{33,1},{81,113},{34,2},{82,114},{35,3},{83,115},{3... | collective-permute-start | bytes 2359304 | tf_op jit(solution)/shard_map/ppermute | solution.py:389
  418.2 126.3 %collective-permute-start.42 = (f32[32,96,128]{2,1,0:T(8,128)S(1)}, f32[32,96,128]{2,1,0:T(8,128)S(1)}, u32[]{:S(2)}, u32[]{:S(2)}) collective-permute-start(f32[32,96,128]{2,1,0:T(8,128)S(1)} %get-tuple-element.97), channel_id=1, source_target_pairs={{16,32},{32,16},{48,64},{64,48},{80,96},{96,80},{17,33},{33,17},{4... | collective-permute-start | bytes 4718600 | tf_op jit(solution)/shard_map/ppermute | solution.py:398
  427.3 46.5 %collective-permute-start.50 = (f32[64,128]{1,0:T(8,128)S(1)}, f32[64,128]{1,0:T(8,128)S(1)}, u32[]{:S(2)}, u32[]{:S(2)}) collective-permute-start(f32[64,128]{1,0:T(8,128)S(1)} %get-tuple-element.100), channel_id=1, source_target_pairs={{0,17},{1,18},{2,19},{16,1},{17,2},{18,3},{32,49},{33,50},{34,51},... | collective-permute-start | bytes 98312 | tf_op jit(solution)/shard_map/ppermute | solution.py:397
  439.1 35.3 %collective-permute-start.51 = (f32[64,128]{1,0:T(8,128)S(1)}, f32[64,128]{1,0:T(8,128)S(1)}, u32[]{:S(2)}, u32[]{:S(2)}) collective-permute-start(f32[64,128]{1,0:T(8,128)S(1)} %get-tuple-element.101), channel_id=1, source_target_pairs={{1,16},{2,17},{3,18},{17,0},{18,1},{19,2},{33,48},{34,49},{35,50},... | collective-permute-start | bytes 98312 | tf_op jit(solution)/shard_map/ppermute | solution.py:397
  445.5 46.4 %collective-permute-start.41 = (f32[16,96,128]{2,1,0:T(8,128)S(1)}, f32[16,96,128]{2,1,0:T(8,128)S(1)}, u32[]{:S(2)}, u32[]{:S(2)}) collective-permute-start(f32[16,96,128]{2,1,0:T(8,128)S(1)} %get-tuple-element.96), channel_id=1, source_target_pairs={{16,32},{32,16},{48,64},{64,48},{80,96},{96,80},{17,33},{33,17},{4... | collective-permute-start | bytes 2359304 | tf_op jit(solution)/shard_map/ppermute | solution.py:391
  447.4 44.5 %collective-permute-start.44 = (f32[16,96,128]{2,1,0:T(8,128)S(1)}, f32[16,96,128]{2,1,0:T(8,128)S(1)}, u32[]{:S(2)}, u32[]{:S(2)}) collective-permute-start(f32[16,96,128]{2,1,0:T(8,128)S(1)} %collective-permute-done.43), channel_id=1, source_target_pairs={{0,80},{112,32},{1,81},{113,33},{2,82},{114,34},{3,83},{115,35},{4... | collective-permute-start | bytes 2359304 | tf_op jit(solution)/shard_map/ppermute | solution.py:393
  474.5 70.0 %collective-permute-start.48 = (f32[16,96,128]{2,1,0:T(8,128)S(1)}, f32[16,96,128]{2,1,0:T(8,128)S(1)}, u32[]{:S(2)}, u32[]{:S(2)}) collective-permute-start(f32[16,96,128]{2,1,0:T(8,128)S(1)} %collective-permute-done.47), channel_id=1, source_target_pairs={{0,16},{112,96},{1,17},{113,97},{2,18},{114,98},{3,19},{115,99},{4... | collective-permute-start | bytes 2359304 | tf_op jit(solution)/shard_map/ppermute | solution.py:393
  (25 other events, 232.2 us)

commit v5 on v4

--- a/solution.py
+++ b/solution.py
@@ -293,35 +293,30 @@
     )(odd, part, *halos, *relayed, *mids, ex)
 
 
-def place_kernel(at_ref, part, *refs):
-    halos, (_, out, done, sems) = refs[:-4], refs[-4:]
+def place_kernel(pieces, at_ref, part, *refs):
+    halos, (_, out, done, sems) = list(refs[:-4]), refs[-4:]
     plane = out.at[at_ref[0]]
     copies = []
-    for k in range(part.shape[0] // TILE):
-        own = pl.ds(k * TILE, TILE)
-        if len(halos) == 3:
-            halo = halos[0][own]
-        elif k * TILE < EARLY:
-            halo = halos[0][own]
-        elif k * TILE < DIRECT:
-            halo = halos[1][pl.ds(k * TILE - EARLY, TILE)]
-        else:
-            rest = pl.ds(k * TILE - DIRECT, TILE)
-            halo = halos[2][rest] + halos[3][rest] + halos[4][rest]
-        done[own] = part[own] + 0.1 * halo
-        if len(halos) == 3:
-            for column, at in zip(halos[1:], (0, part.shape[1] - 1)):
-                done[own, at, :] = done[own, at, :] + 0.1 * column[own]
-        copies.append(pltpu.make_async_copy(done.at[own], plane.at[own], sems.at[k]))
-        copies[-1].start()
+    for start, count in pieces:
+        own_halos, halos = halos[:count], halos[count:]
+        for at in range(0, own_halos[0].shape[0], TILE):
+            rows = pl.ds(at, TILE)
+            own = pl.ds(start + at, TILE)
+            done[own] = part[own] + 0.1 * sum((h[rows] for h in own_halos[1:]), own_halos[0][rows])
+            if len(pieces) == 1 and halos:
+                for column, z in zip(halos, (0, part.shape[1] - 1)):
+                    done[own, z, :] = done[own, z, :] + 0.1 * column[own]
+            copies.append(pltpu.make_async_copy(done.at[own], plane.at[own], sems.at[len(copies)]))
+            copies[-1].start()
     for copy in copies:
         copy.wait()
 
 
-def place(at, part, halos, whole):
+def place(at, part, pieces, edges, whole):
     held = pl.BlockSpec(memory_space=pltpu.VMEM)
-    return pl.pallas_call(
-        place_kernel,
+    halos = [h for _, some in pieces for h in some] + list(edges)
+    return pl.pallas_call(
+        functools.partial(place_kernel, [(start, len(some)) for start, some in pieces]),
         in_specs=[pl.BlockSpec(memory_space=pltpu.SMEM), held]
         + [held] * len(halos)
         + [pl.BlockSpec(memory_space=pltpu.HBM)],
@@ -395,7 +390,9 @@
             e_halo = jnp.concatenate([first_halo, e_halo])
         low, high = columns(e_halo)
         low, high = lax.ppermute(high, ("py", "pz"), CORNERS_UP), lax.ppermute(low, ("py", "pz"), CORNERS_DOWN)
-        o_halos = [o_early, lax.ppermute(late, "py", ODD_CUTS)]
+        cut = late.shape[0] if step < STEPS - 1 else late.shape[0] // 2
+        o_halos = [o_early, lax.ppermute(late[:cut], "py", ODD_CUTS)]
+        o_final = lax.ppermute(late[cut:], "py", ODD_CUTS) if step == STEPS - 1 else None
         ends = [*px, z_even, z_odd, z_by]
         o_part, e_part, mid, *mids = partial_step(step, odd_ref, o, mid, e, inverse, ends)
         if step == STEPS - 1:
@@ -404,8 +401,9 @@
         e_halo = lax.ppermute(e, "py", EVEN_CUTS)
         outs = finish_odd(odd_ref, o_part, o_halos, relayed, mids, ex)
         o, early, late, rest, x_low, x_high, z_even, z_odd = outs
-    out = place(e_plane, e_part, (e_halo, low, high), mid)
-    return place(o_plane, o_part, (*o_halos, *relayed), out)
+    out = place(e_plane, e_part, [(0, [e_halo])], (low, high), mid)
+    out = place(o_plane, o_part, [(0, o_halos[:1]), (EARLY, o_halos[1:])], (), out)
+    return place(o_plane, o_part, [(EARLY + cut, [o_final]), (DIRECT, relayed)], (), out)
 
 
 def solution(mesh):

time: 548 us -> 549 us (level)
    ppermute x3, waiting for transfers between devices: 25.6 us -> 0.01 us  [local(): lax.ppermute(high, ('py', 'pz'), CORNERS_UP)]
    ppermute x3 -> x4, waiting for transfers between devices: 18.9 us -> 42.4 us  [the longest x3 31.8 us: local(): o_halos = [o_early, lax.ppermute(late[:cut], 'py', ODD_CUTS)]]
    ppermute x9, waiting for transfers between devices: 98 us -> 112 us  [local(): relayed[k] = lax.ppermute(relayed[k], 'py', on)]
    ppermute x9, waiting for transfers between devices: 33.3 us -> 23.3 us  [local(): relayed.append(lax.ppermute(rest, 'py', to))]
    ppermute x3 -> x4, starting transfers between devices: 14 us -> 14.1 us  [the longest x3 10.5 us: local(): o_halos = [o_early, lax.ppermute(late[:cut], 'py', ODD_CUTS)]]
  transfers between devices with their start and end apart: 52 -> 53, of which waited for: 16 -> 15; matrix products, arithmetic and copies ran while one was open for 1% -> 1% of each run, Pallas kernels for 9% -> 9%
where the time goes in v5:
time: 549 us; the launch traced here: 548 us
  waiting for transfers between devices  373 us (68%)
  starting transfers between devices  106 us (19%)
  Pallas kernels  58.9 us (11%)
  local copies, waits for them, and re-layouts  8.27 us (2%)
    ppermute x3, waiting for transfers between devices, local(): o_early = lax.ppermute(early, 'py', ODD_CUTS)  122 us
    ppermute x9, waiting for transfers between devices, local(): relayed[k] = lax.ppermute(relayed[k], 'py', on)  112 us
    ppermute x1, waiting for transfers between devices, local(): first_halo = lax.ppermute(e_first, 'py', EVEN_CUTS)  57.6 us
    pallas_call x3, Pallas kernels, partial_step(): pl.pallas_call(functools.partial(partial_kernel, first, last), grid_spec=...  38.7 us
    ppermute x3, waiting for transfers between devices, local(): o_halos = [o_early, lax.ppermute(late[:cut], 'py', ODD_CUTS)]  31.8 us
    ppermute x9, waiting for transfers between devices, local(): relayed.append(lax.ppermute(rest, 'py', to))  23.3 us
    ppermute x3, starting transfers between devices, local(): o_early = lax.ppermute(early, 'py', ODD_CUTS)  15.3 us
    ppermute x9, starting transfers between devices, local(): relayed.append(lax.ppermute(rest, 'py', to))  14.2 us
  transfers between devices with their start and end apart: 53, of which 15 were waited for; matrix products, arithmetic and copies ran while one was open for 1% of the time, Pallas kernels for 9%

profile of v5, /device:TPU:6, one launch (start us, length us, event | category | flops | bytes accessed | tf_op | source)
XLA Modules:
  0.0 547.9 jit_solution(18209509772212809872)
XLA Ops:
  0.0 5.1 shard_map.29
  7.7 2.2 collective-permute-start.14
  12.4 3.5 collective-permute-start.4
  15.9 2.6 collective-permute-start.3
  20.4 57.6 %collective-permute-done.14 = f32[16,96,128]{2,1,0:T(8,128)} collective-permute-done((f32[16,96,128]{2,1,0:T(8,128)S(1)}, f32[16,96,128]{2,1,0:T(8,128)}, u32[]{:S(2)}, u32[]{:S(2)}) %collective-permute-start.14) | collective-permute-done | bytes 786464 | tf_op jit(solution)/shard_map/ppermute | solution.py:364
  86.3 3.4 collective-permute-start.16
  90.3 4.3 collective-permute-start.17
  94.7 3.0 shard_map.28
  98.6 13.1 %partial_step.3 = (f32[64,96,128]{2,1,0:T(8,128)S(1)}, f32[64,96,128]{2,1,0:T(8,128)S(1)}, f32[2,64,96,128]{3,2,1,0:T(8,128)S(1)}, f32[2,96,128]{2,1,0:T(8,128)S...) custom-call(s32[2]{0:T(128)S(1)} %pad_add_fusion.odd_ref, ...), custom_call_target="tpu_custom_call" | custom-call | flops 60000000 | bytes 40000000 | tf_op jit(solution)/shard_map/partial_step/pallas_call | solution.py:151
  116.1 7.2 %collective-permute-start.8 = (f32[16,96,128]{2,1,0:T(8,128)S(1)}, f32[16,96,128]{2,1,0:T(8,128)S(1)}, u32[]{:S(2)}, u32[]{:S(2)}) collective-permute-start(f32[16,96,128]{2,1,0:T(8,128)S(1)} %copy-done.4), channel_id=1, source_target_pairs={{96,0},{16,112},{97,1},{17,113},{98,2},{18,114},{99,3},{19,115},{1... | collective-permute-start | bytes 2359304 | tf_op jit(solution)/shard_map/ppermute | solution.py:384
  125.2 6.3 %collective-permute-start.7 = (f32[32,96,128]{2,1,0:T(8,128)S(1)}, f32[32,96,128]{2,1,0:T(8,128)S(1)}, u32[]{:S(2)}, u32[]{:S(2)}) collective-permute-start(f32[32,96,128]{2,1,0:T(8,128)S(1)} %get-tuple-element.58), channel_id=1, source_target_pairs={{16,32},{32,16},{48,64},{64,48},{80,96},{96,80},{17,33},{33,17},{4... | collective-permute-start | bytes 4718600 | tf_op jit(solution)/shard_map/ppermute | solution.py:394
  132.2 23.3 %collective-permute-done.8 = f32[16,96,128]{2,1,0:T(8,128)S(1)} collective-permute-done((f32[16,96,128]{2,1,0:T(8,128)S(1)}, f32[16,96,128]{2,1,0:T(8,128)S(1)}, u32[]{:S(2)}, u32[]{:S(2)}) %collective-permute-start.8) | collective-permute-done | bytes 786464 | tf_op jit(solution)/shard_map/ppermute | solution.py:384
  156.8 45.3 %collective-permute-done.6.early = f32[16,96,128]{2,1,0:T(8,128)S(1)} collective-permute-done((f32[16,96,128]{2,1,0:T(8,128)S(1)}, f32[16,96,128]{2,1,0:T(8,128)S(1)}, u32[]{:S(2)}, u32[]{:S(2)}) %collective-permute-start.6) | collective-permute-done | bytes 786464 | tf_op jit(solution)/shard_map/ppermute | solution.py:386
  202.8 14.8 %collective-permute-done.13.r2 = f32[16,96,128]{2,1,0:T(8,128)S(1)} collective-permute-done((f32[16,96,128]{2,1,0:T(8,128)S(1)}, f32[16,96,128]{2,1,0:T(8,128)S(1)}, u32[]{:S(2)}, u32[]{:S(2)}) %collective-permute-start.13) | collective-permute-done | bytes 786464 | tf_op jit(solution)/shard_map/ppermute | solution.py:388
  217.6 18.2 %collective-permute-done.7.late = f32[32,96,128]{2,1,0:T(8,128)S(1)} collective-permute-done((f32[32,96,128]{2,1,0:T(8,128)S(1)}, f32[32,96,128]{2,1,0:T(8,128)S(1)}, u32[]{:S(2)}, u32[]{:S(2)}) %collective-permute-start.7) | collective-permute-done | bytes 1572896 | tf_op jit(solution)/shard_map/ppermute | solution.py:394
  239.0 5.9 %collective-permute-start.22 = (f32[3,32,128]{2,1,0:T(8,128)S(1)}, f32[3,32,128]{2,1,0:T(8,128)S(1)}, u32[]{:S(2)}, u32[]{:S(2)}) collective-permute-start(f32[3,32,128]{2,1,0:T(8,128)S(1)} %get-tuple-element.113), channel_id=1, source_target_pairs={{1,3},{2,0},{5,7},{6,4},{9,11},{10,8},{13,15},{14,12},{17,19},{18,... | collective-permute-start | bytes 147464 | tf_op jit(solution)/shard_map/ppermute | solution.py:378
  245.0 2.6 collective-permute-start.18
  250.8 5.0 collective-permute-done.21.refs_16_
  257.2 5.0 collective-permute-done.23.refs_17_
  264.1 5.1 collective-permute-start.34
  269.3 11.2 %partial_step.4 = (f32[64,96,128]{2,1,0:T(8,128)S(1)}, f32[64,96,128]{2,1,0:T(8,128)S(1)}, f32[2,64,96,128]{3,2,1,0:T(8,128)S(1)}, f32[2,96,128]{2,1,0:T(8,128)S...) custom-call(s32[2]{0:T(128)S(1)} %pad_add_fusion.odd_ref, ...), custom_call_target="tpu_custom_call" | custom-call | flops 60000000 | bytes 40000000 | tf_op jit(solution)/shard_map/partial_step/pallas_call | solution.py:151
  282.7 8.7 %collective-permute-start.24 = (f32[16,96,128]{2,1,0:T(8,128)S(1)}, f32[16,96,128]{2,1,0:T(8,128)S(1)}, u32[]{:S(2)}, u32[]{:S(2)}) collective-permute-start(f32[16,96,128]{2,1,0:T(8,128)S(1)} %get-tuple-element.77), channel_id=1, source_target_pairs={{16,32},{32,16},{48,64},{64,48},{80,96},{96,80},{17,33},{33,17},{4... | collective-permute-start | bytes 2359304 | tf_op jit(solution)/shard_map/ppermute | solution.py:386
  294.8 76.5 %collective-permute-done.24.early = f32[16,96,128]{2,1,0:T(8,128)S(1)} collective-permute-done((f32[16,96,128]{2,1,0:T(8,128)S(1)}, f32[16,96,128]{2,1,0:T(8,128)S(1)}, u32[]{:S(2)}, u32[]{:S(2)}) %collective-permute-start.24) | collective-permute-done | bytes 786464 | tf_op jit(solution)/shard_map/ppermute | solution.py:386
  372.6 31.5 %collective-permute-done.31.r2 = f32[16,96,128]{2,1,0:T(8,128)S(1)} collective-permute-done((f32[16,96,128]{2,1,0:T(8,128)S(1)}, f32[16,96,128]{2,1,0:T(8,128)S(1)}, u32[]{:S(2)}, u32[]{:S(2)}) %collective-permute-start.31) | collective-permute-done | bytes 786464 | tf_op jit(solution)/shard_map/ppermute | solution.py:388
  413.2 4.0 collective-permute-done.38.refs_16_
  417.1 2.3 collective-permute-start.49
  427.5 12.9 %collective-permute-done.49.refs_1_ = f32[16,96,128]{2,1,0:T(8,128)S(1)} collective-permute-done((f32[16,96,128]{2,1,0:T(8,128)S(1)}, f32[16,96,128]{2,1,0:T(8,128)S(1)}, u32[]{:S(2)}, u32[]{:S(2)}) %collective-permute-start.49) | collective-permute-done | bytes 786464 | tf_op jit(solution)/shard_map/ppermute | solution.py:394
  442.3 4.6 collective-permute-start.48
  446.9 3.6 collective-permute-start.41
  453.3 14.3 %partial_step.5 = (f32[64,96,128]{2,1,0:T(8,128)S(1)}, f32[64,96,128]{2,1,0:T(8,128)S(1)}, f32[4,64,96,128]{3,2,1,0:T(8,128)}) custom-call(s32[2]{0:T(128)S(1)} %pad_add_fusion.odd_ref, f32[64,96,128]{2,1,0:T(8,128)S(1)} %get-tuple-element.88.refs_0_.refs_1_.refs_2_, f32[64,96,128]{2,1,0:T(8,128)S(1)} %get-tuple-element.88.refs_0_.refs_1_.refs_2_, ...), custom_call_target="tpu_custom_call" | custom-call | flops 60000000 | bytes 40000000 | tf_op jit(solution)/shard_map/partial_step/pallas_call | solution.py:151
  470.8 10.6 %collective-permute-done.41.refs_0_ = f32[16,96,128]{2,1,0:T(8,128)S(1)} collective-permute-done((f32[16,96,128]{2,1,0:T(8,128)S(1)}, f32[16,96,128]{2,1,0:T(8,128)S(1)}, u32[]{:S(2)}, u32[]{:S(2)}) %collective-permute-start.41) | collective-permute-done | bytes 786464 | tf_op jit(solution)/shard_map/ppermute | solution.py:395
  481.4 65.2 %collective-permute-done.47.refs_3_ = f32[16,96,128]{2,1,0:T(8,128)S(1)} collective-permute-done((f32[16,96,128]{2,1,0:T(8,128)S(1)}, f32[16,96,128]{2,1,0:T(8,128)S(1)}, u32[]{:S(2)}, u32[]{:S(2)}) %collective-permute-start.47) | collective-permute-done | bytes 786464 | tf_op jit(solution)/shard_map/ppermute | solution.py:388
  (111 shorter events, 68.1 us)
Async XLA Ops:
  5.1 77.3 %collective-permute-start.15 = (f32[48,96,128]{2,1,0:T(8,128)}, f32[48,96,128]{2,1,0:T(8,128)}, u32[]{:S(2)}, u32[]{:S(2)}) collective-permute-start(f32[48,96,128]{2,1,0:T(8,128)} %get-tuple-element.65), channel_id=1, source_target_pairs={{0,16},{16,0},{32,48},{48,32},{64,80},{80,64},{96,112},{112,96},{1... | collective-permute-start | bytes 7077896 | tf_op jit(solution)/shard_map/ppermute | solution.py:366
  7.7 70.3 %collective-permute-start.14 = (f32[16,96,128]{2,1,0:T(8,128)S(1)}, f32[16,96,128]{2,1,0:T(8,128)}, u32[]{:S(2)}, u32[]{:S(2)}) collective-permute-start(f32[16,96,128]{2,1,0:T(8,128)S(1)} %shard_map.30), channel_id=1, source_target_pairs={{0,16},{16,0},{32,48},{48,32},{64,80},{80,64},{96,112},{112,96},{1... | collective-permute-start | bytes 2359304 | tf_op jit(solution)/shard_map/ppermute | solution.py:364
  12.4 68.8 %collective-permute-start.4 = (f32[3,32,128]{2,1,0:T(8,128)S(1)}, f32[3,32,128]{2,1,0:T(8,128)S(1)}, u32[]{:S(2)}, u32[]{:S(2)}) collective-permute-start(f32[3,32,128]{2,1,0:T(8,128)S(1)} %get-tuple-element.115), channel_id=1, source_target_pairs={{1,3},{2,0},{5,7},{6,4},{9,11},{10,8},{13,15},{14,12},{17,19},{18,... | collective-permute-start | bytes 147464 | tf_op jit(solution)/shard_map/ppermute | solution.py:378
  15.9 70.4 %collective-permute-start.3 = (f32[3,32,128]{2,1,0:T(8,128)S(1)}, f32[3,32,128]{2,1,0:T(8,128)S(1)}, u32[]{:S(2)}, u32[]{:S(2)}) collective-permute-start(f32[3,32,128]{2,1,0:T(8,128)S(1)} %get-tuple-element.116), channel_id=1, source_target_pairs={{1,2},{2,1},{5,6},{6,5},{9,10},{10,9},{13,14},{14,13},{17,18},{18,... | collective-permute-start | bytes 147464 | tf_op jit(solution)/shard_map/ppermute | solution.py:380
  18.5 80.1 %collective-permute-start.2 = (f32[3,64,128]{2,1,0:T(8,128)}, f32[3,64,128]{2,1,0:T(8,128)}, u32[]{:S(2)}, u32[]{:S(2)}) collective-permute-start(f32[3,64,128]{2,1,0:T(8,128)} %get-tuple-element.110), channel_id=1, source_target_pairs={{0,1},{1,0},{2,3},{3,2},{4,5},{5,4},{6,7},{7,6},{8,9},{9,8},{10,11... | collective-permute-start | bytes 294920 | tf_op jit(solution)/shard_map/ppermute | solution.py:379
  86.3 25.4 %collective-permute-start.16 = (f32[64,128]{1,0:T(8,128)}, f32[64,128]{1,0:T(8,128)}, u32[]{:S(2)}, u32[]{:S(2)}) collective-permute-start(f32[64,128]{1,0:T(8,128)} %get-tuple-element.66), channel_id=1, source_target_pairs={{0,17},{1,18},{2,19},{16,1},{17,2},{18,3},{32,49},{33,50},{34,51},... | collective-permute-start | bytes 98312 | tf_op jit(solution)/shard_map/ppermute | solution.py:392
  90.3 21.4 %collective-permute-start.17 = (f32[64,128]{1,0:T(8,128)}, f32[64,128]{1,0:T(8,128)}, u32[]{:S(2)}, u32[]{:S(2)}) collective-permute-start(f32[64,128]{1,0:T(8,128)} %get-tuple-element.67), channel_id=1, source_target_pairs={{1,16},{2,17},{3,18},{17,0},{18,1},{19,2},{33,48},{34,49},{35,50},... | collective-permute-start | bytes 98312 | tf_op jit(solution)/shard_map/ppermute | solution.py:392
  113.7 142.1 %collective-permute-start.32 = (f32[64,96,128]{2,1,0:T(8,128)S(1)}, f32[64,96,128]{2,1,0:T(8,128)S(1)}, u32[]{:S(2)}, u32[]{:S(2)}) collective-permute-start(f32[64,96,128]{2,1,0:T(8,128)S(1)} %get-tuple-element.71.refs_9_.refs_10_.refs_11_), channel_id=1, source_target_pairs={{0,16},{16,0},{32,48},{48,32},{64,80},{80,64},{96,112},{112,96},{1... | collective-permute-start | bytes 9437192 | tf_op jit(solution)/shard_map/ppermute | solution.py:401
  116.1 39.5 %collective-permute-start.8 = (f32[16,96,128]{2,1,0:T(8,128)S(1)}, f32[16,96,128]{2,1,0:T(8,128)S(1)}, u32[]{:S(2)}, u32[]{:S(2)}) collective-permute-start(f32[16,96,128]{2,1,0:T(8,128)S(1)} %copy-done.4), channel_id=1, source_target_pairs={{96,0},{16,112},{97,1},{17,113},{98,2},{18,114},{99,3},{19,115},{1... | collective-permute-start | bytes 2359304 | tf_op jit(solution)/shard_map/ppermute | solution.py:384
  123.2 78.9 %collective-permute-start.6 = (f32[16,96,128]{2,1,0:T(8,128)S(1)}, f32[16,96,128]{2,1,0:T(8,128)S(1)}, u32[]{:S(2)}, u32[]{:S(2)}) collective-permute-start(f32[16,96,128]{2,1,0:T(8,128)S(1)} %get-tuple-element.57), channel_id=1, source_target_pairs={{16,32},{32,16},{48,64},{64,48},{80,96},{96,80},{17,33},{33,17},{4... | collective-permute-start | bytes 2359304 | tf_op jit(solution)/shard_map/ppermute | solution.py:386
  125.2 110.7 %collective-permute-start.7 = (f32[32,96,128]{2,1,0:T(8,128)S(1)}, f32[32,96,128]{2,1,0:T(8,128)S(1)}, u32[]{:S(2)}, u32[]{:S(2)}) collective-permute-start(f32[32,96,128]{2,1,0:T(8,128)S(1)} %get-tuple-element.58), channel_id=1, source_target_pairs={{16,32},{32,16},{48,64},{64,48},{80,96},{96,80},{17,33},{33,17},{4... | collective-permute-start | bytes 4718600 | tf_op jit(solution)/shard_map/ppermute | solution.py:394
  131.5 71.3 %collective-permute-start.11 = (f32[16,96,128]{2,1,0:T(8,128)S(1)}, f32[16,96,128]{2,1,0:T(8,128)S(1)}, u32[]{:S(2)}, u32[]{:S(2)}) collective-permute-start(f32[16,96,128]{2,1,0:T(8,128)S(1)} %collective-permute-done.10), channel_id=1, source_target_pairs={{0,48},{112,64},{1,49},{113,65},{2,50},{114,66},{3,51},{115,67},{4... | collective-permute-start | bytes 2359304 | tf_op jit(solution)/shard_map/ppermute | solution.py:388
  155.6 62.1 %collective-permute-start.13 = (f32[16,96,128]{2,1,0:T(8,128)S(1)}, f32[16,96,128]{2,1,0:T(8,128)S(1)}, u32[]{:S(2)}, u32[]{:S(2)}) collective-permute-start(f32[16,96,128]{2,1,0:T(8,128)S(1)} %collective-permute-done.12), channel_id=1, source_target_pairs={{0,16},{112,96},{1,17},{113,97},{2,18},{114,98},{3,19},{115,99},{4... | collective-permute-start | bytes 2359304 | tf_op jit(solution)/shard_map/ppermute | solution.py:388
  237.5 54.0 %collective-permute-start.26 = (f32[16,96,128]{2,1,0:T(8,128)S(1)}, f32[16,96,128]{2,1,0:T(8,128)S(1)}, u32[]{:S(2)}, u32[]{:S(2)}) collective-permute-start(f32[16,96,128]{2,1,0:T(8,128)S(1)} %get-tuple-element.79), channel_id=1, source_target_pairs={{96,0},{16,112},{97,1},{17,113},{98,2},{18,114},{99,3},{19,115},{1... | collective-permute-start | bytes 2359304 | tf_op jit(solution)/shard_map/ppermute | solution.py:384
  245.0 24.3 %collective-permute-start.18 = (f32[4,96,128]{2,1,0:T(8,128)S(1)}, f32[4,96,128]{2,1,0:T(8,128)S(1)}, u32[]{:S(2)}, u32[]{:S(2)}) collective-permute-start(f32[4,96,128]{2,1,0:T(8,128)S(1)} %get-tuple-element.72), channel_id=1, source_target_pairs={{0,4},{4,8},{8,12},{1,5},{5,9},{9,13},{2,6},{6,10},{10,14},{3,7},{... | collective-permute-start | bytes 589832 | tf_op jit(solution)/shard_map/ppermute | solution.py:385
  247.6 21.7 %collective-permute-start.19 = (f32[4,96,128]{2,1,0:T(8,128)S(1)}, f32[4,96,128]{2,1,0:T(8,128)S(1)}, u32[]{:S(2)}, u32[]{:S(2)}) collective-permute-start(f32[4,96,128]{2,1,0:T(8,128)S(1)} %get-tuple-element.73), channel_id=1, source_target_pairs={{4,0},{8,4},{12,8},{5,1},{9,5},{13,9},{6,2},{10,6},{14,10},{7,3},{... | collective-permute-start | bytes 589832 | tf_op jit(solution)/shard_map/ppermute | solution.py:385
  281.2 141.0 %collective-permute-start.50 = (f32[64,96,128]{2,1,0:T(8,128)S(1)}, f32[64,96,128]{2,1,0:T(8,128)S(1)}, u32[]{:S(2)}, u32[]{:S(2)}) collective-permute-start(f32[64,96,128]{2,1,0:T(8,128)S(1)} %get-tuple-element.90.refs_9_.refs_10_.refs_11_), channel_id=1, source_target_pairs={{0,16},{16,0},{32,48},{48,32},{64,80},{80,64},{96,112},{112,96},{1... | collective-permute-start | bytes 9437192 | tf_op jit(solution)/shard_map/ppermute | solution.py:401
  282.7 88.6 %collective-permute-start.24 = (f32[16,96,128]{2,1,0:T(8,128)S(1)}, f32[16,96,128]{2,1,0:T(8,128)S(1)}, u32[]{:S(2)}, u32[]{:S(2)}) collective-permute-start(f32[16,96,128]{2,1,0:T(8,128)S(1)} %get-tuple-element.77), channel_id=1, source_target_pairs={{16,32},{32,16},{48,64},{64,48},{80,96},{96,80},{17,33},{33,17},{4... | collective-permute-start | bytes 2359304 | tf_op jit(solution)/shard_map/ppermute | solution.py:386
  291.4 113.4 %collective-permute-start.25 = (f32[32,96,128]{2,1,0:T(8,128)S(1)}, f32[32,96,128]{2,1,0:T(8,128)S(1)}, u32[]{:S(2)}, u32[]{:S(2)}) collective-permute-start(f32[32,96,128]{2,1,0:T(8,128)S(1)} %get-tuple-element.78), channel_id=1, source_target_pairs={{16,32},{32,16},{48,64},{64,48},{80,96},{96,80},{17,33},{33,17},{4... | collective-permute-start | bytes 4718600 | tf_op jit(solution)/shard_map/ppermute | solution.py:394
  293.4 79.2 %collective-permute-start.27 = (f32[16,96,128]{2,1,0:T(8,128)S(1)}, f32[16,96,128]{2,1,0:T(8,128)S(1)}, u32[]{:S(2)}, u32[]{:S(2)}) collective-permute-start(f32[16,96,128]{2,1,0:T(8,128)S(1)} %collective-permute-done.26), channel_id=1, source_target_pairs={{0,80},{112,32},{1,81},{113,33},{2,82},{114,34},{3,83},{115,35},{4... | collective-permute-start | bytes 2359304 | tf_op jit(solution)/shard_map/ppermute | solution.py:388
  294.1 78.5 %collective-permute-start.29 = (f32[16,96,128]{2,1,0:T(8,128)S(1)}, f32[16,96,128]{2,1,0:T(8,128)S(1)}, u32[]{:S(2)}, u32[]{:S(2)}) collective-permute-start(f32[16,96,128]{2,1,0:T(8,128)S(1)} %collective-permute-done.28), channel_id=1, source_target_pairs={{0,48},{112,64},{1,49},{113,65},{2,50},{114,66},{3,51},{115,67},{4... | collective-permute-start | bytes 2359304 | tf_op jit(solution)/shard_map/ppermute | solution.py:388
  371.3 32.8 %collective-permute-start.31 = (f32[16,96,128]{2,1,0:T(8,128)S(1)}, f32[16,96,128]{2,1,0:T(8,128)S(1)}, u32[]{:S(2)}, u32[]{:S(2)}) collective-permute-start(f32[16,96,128]{2,1,0:T(8,128)S(1)} %collective-permute-done.30), channel_id=1, source_target_pairs={{0,16},{112,96},{1,17},{113,97},{2,18},{114,98},{3,19},{115,99},{4... | collective-permute-start | bytes 2359304 | tf_op jit(solution)/shard_map/ppermute | solution.py:388
  417.1 23.2 %collective-permute-start.49 = (f32[16,96,128]{2,1,0:T(8,128)S(1)}, f32[16,96,128]{2,1,0:T(8,128)S(1)}, u32[]{:S(2)}, u32[]{:S(2)}) collective-permute-start(f32[16,96,128]{2,1,0:T(8,128)S(1)} %get-tuple-element.107), channel_id=1, source_target_pairs={{16,32},{32,16},{48,64},{64,48},{80,96},{96,80},{17,33},{33,17},{4... | collective-permute-start | bytes 2359304 | tf_op jit(solution)/shard_map/ppermute | solution.py:394
  419.4 22.9 %collective-permute-start.42 = (f32[16,96,128]{2,1,0:T(8,128)S(1)}, f32[16,96,128]{2,1,0:T(8,128)S(1)}, u32[]{:S(2)}, u32[]{:S(2)}) collective-permute-start(f32[16,96,128]{2,1,0:T(8,128)S(1)} %get-tuple-element.97), channel_id=1, source_target_pairs={{96,0},{16,112},{97,1},{17,113},{98,2},{18,114},{99,3},{19,115},{1... | collective-permute-start | bytes 2359304 | tf_op jit(solution)/shard_map/ppermute | solution.py:384
  420.8 26.2 %collective-permute-start.44 = (f32[16,96,128]{2,1,0:T(8,128)S(1)}, f32[16,96,128]{2,1,0:T(8,128)S(1)}, u32[]{:S(2)}, u32[]{:S(2)}) collective-permute-start(f32[16,96,128]{2,1,0:T(8,128)S(1)} %get-tuple-element.97), channel_id=1, source_target_pairs={{64,0},{48,112},{65,1},{49,113},{66,2},{50,114},{67,3},{51,115},{6... | collective-permute-start | bytes 2359304 | tf_op jit(solution)/shard_map/ppermute | solution.py:384
  421.5 29.1 %collective-permute-start.46 = (f32[16,96,128]{2,1,0:T(8,128)S(1)}, f32[16,96,128]{2,1,0:T(8,128)S(1)}, u32[]{:S(2)}, u32[]{:S(2)}) collective-permute-start(f32[16,96,128]{2,1,0:T(8,128)S(1)} %get-tuple-element.97), channel_id=1, source_target_pairs={{32,0},{80,112},{33,1},{81,113},{34,2},{82,114},{35,3},{83,115},{3... | collective-permute-start | bytes 2359304 | tf_op jit(solution)/shard_map/ppermute | solution.py:384
  425.6 25.7 %collective-permute-start.51 = (f32[64,128]{1,0:T(8,128)S(1)}, f32[64,128]{1,0:T(8,128)S(1)}, u32[]{:S(2)}, u32[]{:S(2)}) collective-permute-start(f32[64,128]{1,0:T(8,128)S(1)} %get-tuple-element.100), channel_id=1, source_target_pairs={{0,17},{1,18},{2,19},{16,1},{17,2},{18,3},{32,49},{33,50},{34,51},... | collective-permute-start | bytes 98312 | tf_op jit(solution)/shard_map/ppermute | solution.py:392
  442.3 27.2 %collective-permute-start.48 = (f32[16,96,128]{2,1,0:T(8,128)S(1)}, f32[16,96,128]{2,1,0:T(8,128)S(1)}, u32[]{:S(2)}, u32[]{:S(2)}) collective-permute-start(f32[16,96,128]{2,1,0:T(8,128)S(1)} %get-tuple-element.98), channel_id=1, source_target_pairs={{16,32},{32,16},{48,64},{64,48},{80,96},{96,80},{17,33},{33,17},{4... | collective-permute-start | bytes 2359304 | tf_op jit(solution)/shard_map/ppermute | solution.py:386
  446.9 34.5 %collective-permute-start.41 = (f32[16,96,128]{2,1,0:T(8,128)S(1)}, f32[16,96,128]{2,1,0:T(8,128)S(1)}, u32[]{:S(2)}, u32[]{:S(2)}) collective-permute-start(f32[16,96,128]{2,1,0:T(8,128)S(1)} %get-tuple-element.108), channel_id=1, source_target_pairs={{16,32},{32,16},{48,64},{64,48},{80,96},{96,80},{17,33},{33,17},{4... | collective-permute-start | bytes 2359304 | tf_op jit(solution)/shard_map/ppermute | solution.py:395
  450.6 30.8 %collective-permute-start.43 = (f32[16,96,128]{2,1,0:T(8,128)S(1)}, f32[16,96,128]{2,1,0:T(8,128)S(1)}, u32[]{:S(2)}, u32[]{:S(2)}) collective-permute-start(f32[16,96,128]{2,1,0:T(8,128)S(1)} %collective-permute-done.42), channel_id=1, source_target_pairs={{0,80},{112,32},{1,81},{113,33},{2,82},{114,34},{3,83},{115,35},{4... | collective-permute-start | bytes 2359304 | tf_op jit(solution)/shard_map/ppermute | solution.py:388
  451.3 30.1 %collective-permute-start.45 = (f32[16,96,128]{2,1,0:T(8,128)S(1)}, f32[16,96,128]{2,1,0:T(8,128)S(1)}, u32[]{:S(2)}, u32[]{:S(2)}) collective-permute-start(f32[16,96,128]{2,1,0:T(8,128)S(1)} %collective-permute-done.44), channel_id=1, source_target_pairs={{0,48},{112,64},{1,49},{113,65},{2,50},{114,66},{3,51},{115,67},{4... | collective-permute-start | bytes 2359304 | tf_op jit(solution)/shard_map/ppermute | solution.py:388
  452.0 94.6 %collective-permute-start.47 = (f32[16,96,128]{2,1,0:T(8,128)S(1)}, f32[16,96,128]{2,1,0:T(8,128)S(1)}, u32[]{:S(2)}, u32[]{:S(2)}) collective-permute-start(f32[16,96,128]{2,1,0:T(8,128)S(1)} %collective-permute-done.46), channel_id=1, source_target_pairs={{0,16},{112,96},{1,17},{113,97},{2,18},{114,98},{3,19},{115,99},{4... | collective-permute-start | bytes 2359304 | tf_op jit(solution)/shard_map/ppermute | solution.py:388
  (26 other events, 248.2 us)

commit v6 on v5

--- a/solution.py
+++ b/solution.py
@@ -25,6 +25,7 @@
 CORNERS_DOWN = [(4 * a + k + 1, 4 * b + k) for a, b in EVEN_CUTS for k in range(3)]
 VMEM = 20 * 1024 * 1024
 PART_VMEM = 24 * 1024 * 1024
+FIRST_VMEM = 32 * 1024 * 1024
 
 
 def struct(*shape):
@@ -113,7 +114,7 @@
 
 def partial_step(step, odd, o, mid, e, inverse, halo_ends):
     first, last = step == 0, step == STEPS - 1
-    rows, depth, levels = o.shape
+    rows, depth, levels = mid.shape[1:]
 
     def specs(plane):
         if plane is None:
@@ -144,7 +145,7 @@
     ]
     face = pl.BlockSpec((ROWS, depth, levels), lambda i, odd_ref: (i, 0, 0))
     out_specs = [face, face, block(4 if last else 2)]
-    out_shape = [struct(*o.shape), struct(*o.shape), struct(4 if last else 2, *o.shape)]
+    out_shape = [struct(rows, depth, levels)] * 2 + [struct(4 if last else 2, rows, depth, levels)]
     if not last:
         out_specs += [fixed(2, depth, levels)] * 2 + [ends(2)] * 2
         out_shape += [struct(2, depth, levels)] * 2 + [struct(2, rows, levels)] * 2
@@ -153,15 +154,15 @@
         grid_spec=pltpu.PrefetchScalarGridSpec(
             num_scalar_prefetch=1,
             grid=(rows // ROWS,),
-            in_specs=specs(None)
+            in_specs=specs(middle(0) if first else None)
             + specs(middle(1))
             + specs(middle(2))
-            + specs(None)
+            + specs(middle(3) if first else None)
             + [block(4), fixed(4, depth, levels), fixed(4, depth, levels), ends(3), *half_ends],
             out_specs=out_specs,
         ),
         out_shape=out_shape,
-        compiler_params=pltpu.CompilerParams(vmem_limit_bytes=PART_VMEM),
+        compiler_params=pltpu.CompilerParams(vmem_limit_bytes=FIRST_VMEM if first else PART_VMEM),
         cost_estimate=pl.CostEstimate(flops=60_000_000, bytes_accessed=40_000_000, transcendentals=0),
         name="partial_step",
     )(odd, *([o] * 3), *([mid] * 6), *([e] * 3), inverse, *halo_ends)
@@ -362,12 +363,12 @@
     rows = density.shape[1]
     (e_first,) = pick(density, e_plane, [(0, TILE)], 52)
     first_halo = lax.ppermute(e_first, "py", EVEN_CUTS)
-    e, e_rest = pick(density, e_plane, [(0, rows), (TILE, rows)], 50)
+    (e_rest,) = pick(density, e_plane, [(TILE, rows)], 50)
     e_halo = lax.ppermute(e_rest, "py", EVEN_CUTS)
-    spans = [(0, rows), (0, EARLY), (EARLY, DIRECT), (DIRECT, rows)]
-    o, early, late, rest = pick(density, o_plane, spans, 46)
-    mid = density
-    rows, depth, _ = o.shape
+    spans = [(0, EARLY), (EARLY, DIRECT), (DIRECT, rows)]
+    early, late, rest = pick(density, o_plane, spans, 46)
+    o = mid = e = density
+    depth = density.shape[2]
     x_low, x_high = density[:, 0], density[:, rows - 1]
     z_low, z_high = (lax.dynamic_slice_in_dim(density[:, :, k], odd, 3, 0) for k in (0, depth - 1))
     z_even, z_odd = jnp.where(pz_odd == 1, z_low, z_high), jnp.where(pz_odd == 1, z_high, z_low)

time: 549 us -> 547 us (level)
    ppermute x3, waiting for transfers between devices: 0.01 us -> 25.3 us  [local(): lax.ppermute(low, ('py', 'pz'), CORNERS_DOWN)]
    ppermute x9, waiting for transfers between devices: 112 us -> 96.6 us  [local(): relayed[k] = lax.ppermute(relayed[k], 'py', on)]
    ppermute x1, waiting for transfers between devices: 10.6 us -> 0.01 us  [local(): lax.ppermute(late[cut:], 'py', ODD_CUTS)]
  transfers between devices with their start and end apart: 53 -> 53, of which waited for: 15 -> 15; matrix products, arithmetic and copies ran while one was open for 1% -> 1% of each run, Pallas kernels for 9% -> 10%
where the time goes in v6:
time: 547 us; the launch traced here: 545 us
  waiting for transfers between devices  369 us (67%)
  starting transfers between devices  106 us (19%)
  Pallas kernels  59.1 us (11%)
  local copies, waits for them, and re-layouts  10.4 us (2%)
    ppermute x3, waiting for transfers between devices, local(): o_early = lax.ppermute(early, 'py', ODD_CUTS)  119 us
    ppermute x9, waiting for transfers between devices, local(): relayed[k] = lax.ppermute(relayed[k], 'py', on)  96.6 us
    ppermute x1, waiting for transfers between devices, local(): first_halo = lax.ppermute(e_first, 'py', EVEN_CUTS)  58.7 us
    pallas_call x3, Pallas kernels, partial_step(): pl.pallas_call(functools.partial(partial_kernel, first, last), grid_spec=...  40.2 us
    ppermute x3, waiting for transfers between devices, local(): o_halos = [o_early, lax.ppermute(late[:cut], 'py', ODD_CUTS)]  32.1 us
    ppermute x3, waiting for transfers between devices, local(): lax.ppermute(low, ('py', 'pz'), CORNERS_DOWN)  25.3 us
    ppermute x9, waiting for transfers between devices, local(): relayed.append(lax.ppermute(rest, 'py', to))  23.3 us
    ppermute x3, starting transfers between devices, local(): o_early = lax.ppermute(early, 'py', ODD_CUTS)  15.1 us
  transfers between devices with their start and end apart: 53, of which 15 were waited for; matrix products, arithmetic and copies ran while one was open for 1% of the time, Pallas kernels for 10%

profile of v6, /device:TPU:6, one launch (start us, length us, event | category | flops | bytes accessed | tf_op | source)
XLA Modules:
  0.0 545.5 jit_solution(194441192312779531)
XLA Ops:
  4.3 2.2 collective-permute-start.14
  8.3 3.5 collective-permute-start.4
  11.8 2.6 collective-permute-start.3
  15.6 58.7 %collective-permute-done.14 = f32[16,96,128]{2,1,0:T(8,128)} collective-permute-done((f32[16,96,128]{2,1,0:T(8,128)S(1)}, f32[16,96,128]{2,1,0:T(8,128)}, u32[]{:S(2)}, u32[]{:S(2)}) %collective-permute-start.14) | collective-permute-done | bytes 786464 | tf_op jit(solution)/shard_map/ppermute | solution.py:365
  81.4 3.4 collective-permute-start.16
  84.8 3.7 collective-permute-start.17
  88.5 14.6 %partial_step.3 = (f32[64,96,128]{2,1,0:T(8,128)S(1)}, f32[64,96,128]{2,1,0:T(8,128)S(1)}, f32[2,64,96,128]{3,2,1,0:T(8,128)S(1)}, f32[2,96,128]{2,1,0:T(8,128)S...) custom-call(s32[2]{0:T(128)S(1)} %pad_add_fusion.odd_ref, ...), custom_call_target="tpu_custom_call" | custom-call | flops 60000000 | bytes 40000000 | tf_op jit(solution)/shard_map/partial_step/pallas_call | solution.py:152
  112.5 7.2 %collective-permute-start.8 = (f32[16,96,128]{2,1,0:T(8,128)S(1)}, f32[16,96,128]{2,1,0:T(8,128)S(1)}, u32[]{:S(2)}, u32[]{:S(2)}) collective-permute-start(f32[16,96,128]{2,1,0:T(8,128)S(1)} %get-tuple-element.54), channel_id=1, source_target_pairs={{96,0},{16,112},{97,1},{17,113},{98,2},{18,114},{99,3},{19,115},{1... | collective-permute-start | bytes 2359304 | tf_op jit(solution)/shard_map/ppermute | solution.py:385
  121.6 6.3 %collective-permute-start.7 = (f32[32,96,128]{2,1,0:T(8,128)S(1)}, f32[32,96,128]{2,1,0:T(8,128)S(1)}, u32[]{:S(2)}, u32[]{:S(2)}) collective-permute-start(f32[32,96,128]{2,1,0:T(8,128)S(1)} %get-tuple-element.53), channel_id=1, source_target_pairs={{16,32},{32,16},{48,64},{64,48},{80,96},{96,80},{17,33},{33,17},{4... | collective-permute-start | bytes 4718600 | tf_op jit(solution)/shard_map/ppermute | solution.py:395
  128.6 23.3 %collective-permute-done.8 = f32[16,96,128]{2,1,0:T(8,128)S(1)} collective-permute-done((f32[16,96,128]{2,1,0:T(8,128)S(1)}, f32[16,96,128]{2,1,0:T(8,128)S(1)}, u32[]{:S(2)}, u32[]{:S(2)}) %collective-permute-start.8) | collective-permute-done | bytes 786464 | tf_op jit(solution)/shard_map/ppermute | solution.py:385
  153.2 42.6 %collective-permute-done.6.early = f32[16,96,128]{2,1,0:T(8,128)S(1)} collective-permute-done((f32[16,96,128]{2,1,0:T(8,128)S(1)}, f32[16,96,128]{2,1,0:T(8,128)S(1)}, u32[]{:S(2)}, u32[]{:S(2)}) %collective-permute-start.6) | collective-permute-done | bytes 786464 | tf_op jit(solution)/shard_map/ppermute | solution.py:387
  196.5 14.8 %collective-permute-done.13.r2 = f32[16,96,128]{2,1,0:T(8,128)S(1)} collective-permute-done((f32[16,96,128]{2,1,0:T(8,128)S(1)}, f32[16,96,128]{2,1,0:T(8,128)S(1)}, u32[]{:S(2)}, u32[]{:S(2)}) %collective-permute-start.13) | collective-permute-done | bytes 786464 | tf_op jit(solution)/shard_map/ppermute | solution.py:389
  211.3 18.2 %collective-permute-done.7.late = f32[32,96,128]{2,1,0:T(8,128)S(1)} collective-permute-done((f32[32,96,128]{2,1,0:T(8,128)S(1)}, f32[32,96,128]{2,1,0:T(8,128)S(1)}, u32[]{:S(2)}, u32[]{:S(2)}) %collective-permute-start.7) | collective-permute-done | bytes 1572896 | tf_op jit(solution)/shard_map/ppermute | solution.py:395
  229.5 2.5 finish_odd.2
  233.6 5.9 %collective-permute-start.22 = (f32[3,32,128]{2,1,0:T(8,128)S(1)}, f32[3,32,128]{2,1,0:T(8,128)S(1)}, u32[]{:S(2)}, u32[]{:S(2)}) collective-permute-start(f32[3,32,128]{2,1,0:T(8,128)S(1)} %get-tuple-element.107), channel_id=1, source_target_pairs={{1,3},{2,0},{5,7},{6,4},{9,11},{10,8},{13,15},{14,12},{17,19},{18,... | collective-permute-start | bytes 147464 | tf_op jit(solution)/shard_map/ppermute | solution.py:379
  239.5 3.3 collective-permute-start.18
  246.0 5.0 collective-permute-done.21.refs_16_
  254.2 3.2 collective-permute-done.23.refs_17_
  259.3 5.1 collective-permute-start.34
  264.5 11.2 %partial_step.4 = (f32[64,96,128]{2,1,0:T(8,128)S(1)}, f32[64,96,128]{2,1,0:T(8,128)S(1)}, f32[2,64,96,128]{3,2,1,0:T(8,128)S(1)}, f32[2,96,128]{2,1,0:T(8,128)S...) custom-call(s32[2]{0:T(128)S(1)} %pad_add_fusion.odd_ref, ...), custom_call_target="tpu_custom_call" | custom-call | flops 60000000 | bytes 40000000 | tf_op jit(solution)/shard_map/partial_step/pallas_call | solution.py:152
  275.8 3.0 finish_even.3
  280.3 8.7 %collective-permute-start.24 = (f32[16,96,128]{2,1,0:T(8,128)S(1)}, f32[16,96,128]{2,1,0:T(8,128)S(1)}, u32[]{:S(2)}, u32[]{:S(2)}) collective-permute-start(f32[16,96,128]{2,1,0:T(8,128)S(1)} %get-tuple-element.71), channel_id=1, source_target_pairs={{16,32},{32,16},{48,64},{64,48},{80,96},{96,80},{17,33},{33,17},{4... | collective-permute-start | bytes 2359304 | tf_op jit(solution)/shard_map/ppermute | solution.py:387
  292.4 76.5 %collective-permute-done.24.early = f32[16,96,128]{2,1,0:T(8,128)S(1)} collective-permute-done((f32[16,96,128]{2,1,0:T(8,128)S(1)}, f32[16,96,128]{2,1,0:T(8,128)S(1)}, u32[]{:S(2)}, u32[]{:S(2)}) %collective-permute-start.24) | collective-permute-done | bytes 786464 | tf_op jit(solution)/shard_map/ppermute | solution.py:387
  370.2 31.5 %collective-permute-done.31.r2 = f32[16,96,128]{2,1,0:T(8,128)S(1)} collective-permute-done((f32[16,96,128]{2,1,0:T(8,128)S(1)}, f32[16,96,128]{2,1,0:T(8,128)S(1)}, u32[]{:S(2)}, u32[]{:S(2)}) %collective-permute-start.31) | collective-permute-done | bytes 786464 | tf_op jit(solution)/shard_map/ppermute | solution.py:389
  410.7 4.0 collective-permute-done.38.refs_16_
  414.7 2.3 collective-permute-start.49
  425.0 13.2 %collective-permute-done.49.refs_1_ = f32[16,96,128]{2,1,0:T(8,128)S(1)} collective-permute-done((f32[16,96,128]{2,1,0:T(8,128)S(1)}, f32[16,96,128]{2,1,0:T(8,128)S(1)}, u32[]{:S(2)}, u32[]{:S(2)}) %collective-permute-start.49) | collective-permute-done | bytes 786464 | tf_op jit(solution)/shard_map/ppermute | solution.py:395
  440.1 4.5 collective-permute-start.48
  444.6 3.8 collective-permute-start.41
  449.8 25.3 %collective-permute-done.52.refs_2_ = f32[64,128]{1,0:T(8,128)S(1)} collective-permute-done((f32[64,128]{1,0:T(8,128)S(1)}, f32[64,128]{1,0:T(8,128)S(1)}, u32[]{:S(2)}, u32[]{:S(2)}) %collective-permute-start.52) | collective-permute-done | bytes 32800 | tf_op jit(solution)/shard_map/ppermute | solution.py:393
  476.4 14.4 %partial_step.5 = (f32[64,96,128]{2,1,0:T(8,128)S(1)}, f32[64,96,128]{2,1,0:T(8,128)S(1)}, f32[4,64,96,128]{3,2,1,0:T(8,128)}) custom-call(s32[2]{0:T(128)S(1)} %pad_add_fusion.odd_ref, f32[64,96,128]{2,1,0:T(8,128)S(1)} %get-tuple-element.82.refs_0_.refs_1_.refs_2_, f32[64,96,128]{2,1,0:T(8,128)S(1)} %get-tuple-element.82.refs_0_.refs_1_.refs_2_, ...), custom_call_target="tpu_custom_call" | custom-call | flops 60000000 | bytes 40000000 | tf_op jit(solution)/shard_map/partial_step/pallas_call | solution.py:152
  493.9 50.3 %collective-permute-done.47.refs_3_ = f32[16,96,128]{2,1,0:T(8,128)S(1)} collective-permute-done((f32[16,96,128]{2,1,0:T(8,128)S(1)}, f32[16,96,128]{2,1,0:T(8,128)S(1)}, u32[]{:S(2)}, u32[]{:S(2)}) %collective-permute-start.47) | collective-permute-done | bytes 786464 | tf_op jit(solution)/shard_map/ppermute | solution.py:389
  (120 shorter events, 70.1 us)
Async XLA Ops:
  1.7 76.5 %collective-permute-start.15 = (f32[48,96,128]{2,1,0:T(8,128)S(1)}, f32[48,96,128]{2,1,0:T(8,128)}, u32[]{:S(2)}, u32[]{:S(2)}) collective-permute-start(f32[48,96,128]{2,1,0:T(8,128)S(1)} %shard_map.30), channel_id=1, source_target_pairs={{0,16},{16,0},{32,48},{48,32},{64,80},{80,64},{96,112},{112,96},{1... | collective-permute-start | bytes 7077896 | tf_op jit(solution)/shard_map/ppermute | solution.py:367
  4.3 70.0 %collective-permute-start.14 = (f32[16,96,128]{2,1,0:T(8,128)S(1)}, f32[16,96,128]{2,1,0:T(8,128)}, u32[]{:S(2)}, u32[]{:S(2)}) collective-permute-start(f32[16,96,128]{2,1,0:T(8,128)S(1)} %shard_map.29), channel_id=1, source_target_pairs={{0,16},{16,0},{32,48},{48,32},{64,80},{80,64},{96,112},{112,96},{1... | collective-permute-start | bytes 2359304 | tf_op jit(solution)/shard_map/ppermute | solution.py:365
  8.3 68.5 %collective-permute-start.4 = (f32[3,32,128]{2,1,0:T(8,128)S(1)}, f32[3,32,128]{2,1,0:T(8,128)S(1)}, u32[]{:S(2)}, u32[]{:S(2)}) collective-permute-start(f32[3,32,128]{2,1,0:T(8,128)S(1)} %get-tuple-element.109), channel_id=1, source_target_pairs={{1,3},{2,0},{5,7},{6,4},{9,11},{10,8},{13,15},{14,12},{17,19},{18,... | collective-permute-start | bytes 147464 | tf_op jit(solution)/shard_map/ppermute | solution.py:379
  11.8 69.5 %collective-permute-start.3 = (f32[3,32,128]{2,1,0:T(8,128)S(1)}, f32[3,32,128]{2,1,0:T(8,128)S(1)}, u32[]{:S(2)}, u32[]{:S(2)}) collective-permute-start(f32[3,32,128]{2,1,0:T(8,128)S(1)} %get-tuple-element.110), channel_id=1, source_target_pairs={{1,2},{2,1},{5,6},{6,5},{9,10},{10,9},{13,14},{14,13},{17,18},{18,... | collective-permute-start | bytes 147464 | tf_op jit(solution)/shard_map/ppermute | solution.py:381
  14.5 74.1 %collective-permute-start.2 = (f32[3,64,128]{2,1,0:T(8,128)S(1)}, f32[3,64,128]{2,1,0:T(8,128)S(1)}, u32[]{:S(2)}, u32[]{:S(2)}) collective-permute-start(f32[3,64,128]{2,1,0:T(8,128)S(1)} %get-tuple-element.104), channel_id=1, source_target_pairs={{0,1},{1,0},{2,3},{3,2},{4,5},{5,4},{6,7},{7,6},{8,9},{9,8},{10,11... | collective-permute-start | bytes 294920 | tf_op jit(solution)/shard_map/ppermute | solution.py:380
  81.4 24.1 %collective-permute-start.16 = (f32[64,128]{1,0:T(8,128)S(1)}, f32[64,128]{1,0:T(8,128)S(1)}, u32[]{:S(2)}, u32[]{:S(2)}) collective-permute-start(f32[64,128]{1,0:T(8,128)S(1)} %get-tuple-element.60), channel_id=1, source_target_pairs={{0,17},{1,18},{2,19},{16,1},{17,2},{18,3},{32,49},{33,50},{34,51},... | collective-permute-start | bytes 98312 | tf_op jit(solution)/shard_map/ppermute | solution.py:393
  108.2 142.8 %collective-permute-start.32 = (f32[64,96,128]{2,1,0:T(8,128)S(1)}, f32[64,96,128]{2,1,0:T(8,128)}, u32[]{:S(2)}, u32[]{:S(2)}) collective-permute-start(f32[64,96,128]{2,1,0:T(8,128)S(1)} %get-tuple-element.65.refs_9_.refs_10_.refs_11_), channel_id=1, source_target_pairs={{0,16},{16,0},{32,48},{48,32},{64,80},{80,64},{96,112},{112,96},{1... | collective-permute-start | bytes 9437192 | tf_op jit(solution)/shard_map/ppermute | solution.py:402
  112.5 39.5 %collective-permute-start.8 = (f32[16,96,128]{2,1,0:T(8,128)S(1)}, f32[16,96,128]{2,1,0:T(8,128)S(1)}, u32[]{:S(2)}, u32[]{:S(2)}) collective-permute-start(f32[16,96,128]{2,1,0:T(8,128)S(1)} %get-tuple-element.54), channel_id=1, source_target_pairs={{96,0},{16,112},{97,1},{17,113},{98,2},{18,114},{99,3},{19,115},{1... | collective-permute-start | bytes 2359304 | tf_op jit(solution)/shard_map/ppermute | solution.py:385
  119.6 76.2 %collective-permute-start.6 = (f32[16,96,128]{2,1,0:T(8,128)S(1)}, f32[16,96,128]{2,1,0:T(8,128)S(1)}, u32[]{:S(2)}, u32[]{:S(2)}) collective-permute-start(f32[16,96,128]{2,1,0:T(8,128)S(1)} %get-tuple-element.52), channel_id=1, source_target_pairs={{16,32},{32,16},{48,64},{64,48},{80,96},{96,80},{17,33},{33,17},{4... | collective-permute-start | bytes 2359304 | tf_op jit(solution)/shard_map/ppermute | solution.py:387
  121.6 108.0 %collective-permute-start.7 = (f32[32,96,128]{2,1,0:T(8,128)S(1)}, f32[32,96,128]{2,1,0:T(8,128)S(1)}, u32[]{:S(2)}, u32[]{:S(2)}) collective-permute-start(f32[32,96,128]{2,1,0:T(8,128)S(1)} %get-tuple-element.53), channel_id=1, source_target_pairs={{16,32},{32,16},{48,64},{64,48},{80,96},{96,80},{17,33},{33,17},{4... | collective-permute-start | bytes 4718600 | tf_op jit(solution)/shard_map/ppermute | solution.py:395
  127.9 68.6 %collective-permute-start.11 = (f32[16,96,128]{2,1,0:T(8,128)S(1)}, f32[16,96,128]{2,1,0:T(8,128)S(1)}, u32[]{:S(2)}, u32[]{:S(2)}) collective-permute-start(f32[16,96,128]{2,1,0:T(8,128)S(1)} %collective-permute-done.10), channel_id=1, source_target_pairs={{0,48},{112,64},{1,49},{113,65},{2,50},{114,66},{3,51},{115,67},{4... | collective-permute-start | bytes 2359304 | tf_op jit(solution)/shard_map/ppermute | solution.py:389
  152.0 59.4 %collective-permute-start.13 = (f32[16,96,128]{2,1,0:T(8,128)S(1)}, f32[16,96,128]{2,1,0:T(8,128)S(1)}, u32[]{:S(2)}, u32[]{:S(2)}) collective-permute-start(f32[16,96,128]{2,1,0:T(8,128)S(1)} %collective-permute-done.12), channel_id=1, source_target_pairs={{0,16},{112,96},{1,17},{113,97},{2,18},{114,98},{3,19},{115,99},{4... | collective-permute-start | bytes 2359304 | tf_op jit(solution)/shard_map/ppermute | solution.py:389
  232.0 57.0 %collective-permute-start.26 = (f32[16,96,128]{2,1,0:T(8,128)}, f32[16,96,128]{2,1,0:T(8,128)S(1)}, u32[]{:S(2)}, u32[]{:S(2)}) collective-permute-start(f32[16,96,128]{2,1,0:T(8,128)} %get-tuple-element.73), channel_id=1, source_target_pairs={{96,0},{16,112},{97,1},{17,113},{98,2},{18,114},{99,3},{19,115},{1... | collective-permute-start | bytes 2359304 | tf_op jit(solution)/shard_map/ppermute | solution.py:385
  239.5 25.0 %collective-permute-start.18 = (f32[4,96,128]{2,1,0:T(8,128)S(1)}, f32[4,96,128]{2,1,0:T(8,128)S(1)}, u32[]{:S(2)}, u32[]{:S(2)}) collective-permute-start(f32[4,96,128]{2,1,0:T(8,128)S(1)} %get-tuple-element.66), channel_id=1, source_target_pairs={{0,4},{4,8},{8,12},{1,5},{5,9},{9,13},{2,6},{6,10},{10,14},{3,7},{... | collective-permute-start | bytes 589832 | tf_op jit(solution)/shard_map/ppermute | solution.py:386
  242.8 21.7 %collective-permute-start.19 = (f32[4,96,128]{2,1,0:T(8,128)S(1)}, f32[4,96,128]{2,1,0:T(8,128)S(1)}, u32[]{:S(2)}, u32[]{:S(2)}) collective-permute-start(f32[4,96,128]{2,1,0:T(8,128)S(1)} %get-tuple-element.67), channel_id=1, source_target_pairs={{4,0},{8,4},{12,8},{5,1},{9,5},{13,9},{6,2},{10,6},{14,10},{7,3},{... | collective-permute-start | bytes 589832 | tf_op jit(solution)/shard_map/ppermute | solution.py:386
  278.8 141.0 %collective-permute-start.50 = (f32[64,96,128]{2,1,0:T(8,128)S(1)}, f32[64,96,128]{2,1,0:T(8,128)S(1)}, u32[]{:S(2)}, u32[]{:S(2)}) collective-permute-start(f32[64,96,128]{2,1,0:T(8,128)S(1)} %get-tuple-element.84.refs_9_.refs_10_.refs_11_), channel_id=1, source_target_pairs={{0,16},{16,0},{32,48},{48,32},{64,80},{80,64},{96,112},{112,96},{1... | collective-permute-start | bytes 9437192 | tf_op jit(solution)/shard_map/ppermute | solution.py:402
  280.3 88.6 %collective-permute-start.24 = (f32[16,96,128]{2,1,0:T(8,128)S(1)}, f32[16,96,128]{2,1,0:T(8,128)S(1)}, u32[]{:S(2)}, u32[]{:S(2)}) collective-permute-start(f32[16,96,128]{2,1,0:T(8,128)S(1)} %get-tuple-element.71), channel_id=1, source_target_pairs={{16,32},{32,16},{48,64},{64,48},{80,96},{96,80},{17,33},{33,17},{4... | collective-permute-start | bytes 2359304 | tf_op jit(solution)/shard_map/ppermute | solution.py:387
  289.0 113.4 %collective-permute-start.25 = (f32[32,96,128]{2,1,0:T(8,128)S(1)}, f32[32,96,128]{2,1,0:T(8,128)S(1)}, u32[]{:S(2)}, u32[]{:S(2)}) collective-permute-start(f32[32,96,128]{2,1,0:T(8,128)S(1)} %copy-done.6), channel_id=1, source_target_pairs={{16,32},{32,16},{48,64},{64,48},{80,96},{96,80},{17,33},{33,17},{4... | collective-permute-start | bytes 4718600 | tf_op jit(solution)/shard_map/ppermute | solution.py:395
  291.0 79.2 %collective-permute-start.27 = (f32[16,96,128]{2,1,0:T(8,128)S(1)}, f32[16,96,128]{2,1,0:T(8,128)S(1)}, u32[]{:S(2)}, u32[]{:S(2)}) collective-permute-start(f32[16,96,128]{2,1,0:T(8,128)S(1)} %collective-permute-done.26), channel_id=1, source_target_pairs={{0,80},{112,32},{1,81},{113,33},{2,82},{114,34},{3,83},{115,35},{4... | collective-permute-start | bytes 2359304 | tf_op jit(solution)/shard_map/ppermute | solution.py:389
  291.7 78.5 %collective-permute-start.29 = (f32[16,96,128]{2,1,0:T(8,128)S(1)}, f32[16,96,128]{2,1,0:T(8,128)S(1)}, u32[]{:S(2)}, u32[]{:S(2)}) collective-permute-start(f32[16,96,128]{2,1,0:T(8,128)S(1)} %collective-permute-done.28), channel_id=1, source_target_pairs={{0,48},{112,64},{1,49},{113,65},{2,50},{114,66},{3,51},{115,67},{4... | collective-permute-start | bytes 2359304 | tf_op jit(solution)/shard_map/ppermute | solution.py:389
  368.9 32.8 %collective-permute-start.31 = (f32[16,96,128]{2,1,0:T(8,128)S(1)}, f32[16,96,128]{2,1,0:T(8,128)S(1)}, u32[]{:S(2)}, u32[]{:S(2)}) collective-permute-start(f32[16,96,128]{2,1,0:T(8,128)S(1)} %collective-permute-done.30), channel_id=1, source_target_pairs={{0,16},{112,96},{1,17},{113,97},{2,18},{114,98},{3,19},{115,99},{4... | collective-permute-start | bytes 2359304 | tf_op jit(solution)/shard_map/ppermute | solution.py:389
  414.7 23.5 %collective-permute-start.49 = (f32[16,96,128]{2,1,0:T(8,128)S(1)}, f32[16,96,128]{2,1,0:T(8,128)S(1)}, u32[]{:S(2)}, u32[]{:S(2)}) collective-permute-start(f32[16,96,128]{2,1,0:T(8,128)S(1)} %get-tuple-element.101), channel_id=1, source_target_pairs={{16,32},{32,16},{48,64},{64,48},{80,96},{96,80},{17,33},{33,17},{4... | collective-permute-start | bytes 2359304 | tf_op jit(solution)/shard_map/ppermute | solution.py:395
  416.9 23.2 %collective-permute-start.42 = (f32[16,96,128]{2,1,0:T(8,128)S(1)}, f32[16,96,128]{2,1,0:T(8,128)S(1)}, u32[]{:S(2)}, u32[]{:S(2)}) collective-permute-start(f32[16,96,128]{2,1,0:T(8,128)S(1)} %get-tuple-element.91), channel_id=1, source_target_pairs={{96,0},{16,112},{97,1},{17,113},{98,2},{18,114},{99,3},{19,115},{1... | collective-permute-start | bytes 2359304 | tf_op jit(solution)/shard_map/ppermute | solution.py:385
  418.3 26.3 %collective-permute-start.44 = (f32[16,96,128]{2,1,0:T(8,128)S(1)}, f32[16,96,128]{2,1,0:T(8,128)S(1)}, u32[]{:S(2)}, u32[]{:S(2)}) collective-permute-start(f32[16,96,128]{2,1,0:T(8,128)S(1)} %get-tuple-element.91), channel_id=1, source_target_pairs={{64,0},{48,112},{65,1},{49,113},{66,2},{50,114},{67,3},{51,115},{6... | collective-permute-start | bytes 2359304 | tf_op jit(solution)/shard_map/ppermute | solution.py:385
  419.0 29.4 %collective-permute-start.46 = (f32[16,96,128]{2,1,0:T(8,128)S(1)}, f32[16,96,128]{2,1,0:T(8,128)S(1)}, u32[]{:S(2)}, u32[]{:S(2)}) collective-permute-start(f32[16,96,128]{2,1,0:T(8,128)S(1)} %get-tuple-element.91), channel_id=1, source_target_pairs={{32,0},{80,112},{33,1},{81,113},{34,2},{82,114},{35,3},{83,115},{3... | collective-permute-start | bytes 2359304 | tf_op jit(solution)/shard_map/ppermute | solution.py:385
  423.1 26.0 %collective-permute-start.51 = (f32[64,128]{1,0:T(8,128)S(1)}, f32[64,128]{1,0:T(8,128)S(1)}, u32[]{:S(2)}, u32[]{:S(2)}) collective-permute-start(f32[64,128]{1,0:T(8,128)S(1)} %get-tuple-element.94), channel_id=1, source_target_pairs={{0,17},{1,18},{2,19},{16,1},{17,2},{18,3},{32,49},{33,50},{34,51},... | collective-permute-start | bytes 98312 | tf_op jit(solution)/shard_map/ppermute | solution.py:393
  438.2 36.9 %collective-permute-start.52 = (f32[64,128]{1,0:T(8,128)S(1)}, f32[64,128]{1,0:T(8,128)S(1)}, u32[]{:S(2)}, u32[]{:S(2)}) collective-permute-start(f32[64,128]{1,0:T(8,128)S(1)} %get-tuple-element.95), channel_id=1, source_target_pairs={{1,16},{2,17},{3,18},{17,0},{18,1},{19,2},{33,48},{34,49},{35,50},... | collective-permute-start | bytes 98312 | tf_op jit(solution)/shard_map/ppermute | solution.py:393
  440.1 52.5 %collective-permute-start.48 = (f32[16,96,128]{2,1,0:T(8,128)S(1)}, f32[16,96,128]{2,1,0:T(8,128)S(1)}, u32[]{:S(2)}, u32[]{:S(2)}) collective-permute-start(f32[16,96,128]{2,1,0:T(8,128)S(1)} %get-tuple-element.92), channel_id=1, source_target_pairs={{16,32},{32,16},{48,64},{64,48},{80,96},{96,80},{17,33},{33,17},{4... | collective-permute-start | bytes 2359304 | tf_op jit(solution)/shard_map/ppermute | solution.py:387
  444.6 49.3 %collective-permute-start.41 = (f32[16,96,128]{2,1,0:T(8,128)S(1)}, f32[16,96,128]{2,1,0:T(8,128)S(1)}, u32[]{:S(2)}, u32[]{:S(2)}) collective-permute-start(f32[16,96,128]{2,1,0:T(8,128)S(1)} %get-tuple-element.102), channel_id=1, source_target_pairs={{16,32},{32,16},{48,64},{64,48},{80,96},{96,80},{17,33},{33,17},{4... | collective-permute-start | bytes 2359304 | tf_op jit(solution)/shard_map/ppermute | solution.py:396
  448.4 45.5 %collective-permute-start.43 = (f32[16,96,128]{2,1,0:T(8,128)S(1)}, f32[16,96,128]{2,1,0:T(8,128)S(1)}, u32[]{:S(2)}, u32[]{:S(2)}) collective-permute-start(f32[16,96,128]{2,1,0:T(8,128)S(1)} %collective-permute-done.42), channel_id=1, source_target_pairs={{0,80},{112,32},{1,81},{113,33},{2,82},{114,34},{3,83},{115,35},{4... | collective-permute-start | bytes 2359304 | tf_op jit(solution)/shard_map/ppermute | solution.py:389
  449.1 44.8 %collective-permute-start.45 = (f32[16,96,128]{2,1,0:T(8,128)S(1)}, f32[16,96,128]{2,1,0:T(8,128)S(1)}, u32[]{:S(2)}, u32[]{:S(2)}) collective-permute-start(f32[16,96,128]{2,1,0:T(8,128)S(1)} %collective-permute-done.44), channel_id=1, source_target_pairs={{0,48},{112,64},{1,49},{113,65},{2,50},{114,66},{3,51},{115,67},{4... | collective-permute-start | bytes 2359304 | tf_op jit(solution)/shard_map/ppermute | solution.py:389
  475.1 69.1 %collective-permute-start.47 = (f32[16,96,128]{2,1,0:T(8,128)S(1)}, f32[16,96,128]{2,1,0:T(8,128)S(1)}, u32[]{:S(2)}, u32[]{:S(2)}) collective-permute-start(f32[16,96,128]{2,1,0:T(8,128)S(1)} %collective-permute-done.46), channel_id=1, source_target_pairs={{0,16},{112,96},{1,17},{113,97},{2,18},{114,98},{3,19},{115,99},{4... | collective-permute-start | bytes 2359304 | tf_op jit(solution)/shard_map/ppermute | solution.py:389
  (30 other events, 605.8 us)

commit v7 on v6

--- a/solution.py
+++ b/solution.py
@@ -300,9 +300,9 @@
     copies = []
     for start, count in pieces:
         own_halos, halos = halos[:count], halos[count:]
-        for at in range(0, own_halos[0].shape[0], TILE):
-            rows = pl.ds(at, TILE)
-            own = pl.ds(start + at, TILE)
+        for at in range(0, own_halos[0].shape[0], ROWS):
+            rows = pl.ds(at, ROWS)
+            own = pl.ds(start + at, ROWS)
             done[own] = part[own] + 0.1 * sum((h[rows] for h in own_halos[1:]), own_halos[0][rows])
             if len(pieces) == 1 and halos:
                 for column, z in zip(halos, (0, part.shape[1] - 1)):
@@ -323,7 +323,7 @@
         + [pl.BlockSpec(memory_space=pltpu.HBM)],
         out_specs=pl.BlockSpec(memory_space=pltpu.HBM),
         out_shape=struct(*whole.shape),
-        scratch_shapes=[pltpu.VMEM(part.shape, jnp.float32), pltpu.SemaphoreType.DMA((part.shape[0] // TILE,))],
+        scratch_shapes=[pltpu.VMEM(part.shape, jnp.float32), pltpu.SemaphoreType.DMA((part.shape[0] // ROWS,))],
         input_output_aliases={2 + len(halos): 0},
         compiler_params=pltpu.CompilerParams(vmem_limit_bytes=VMEM),
         cost_estimate=pl.CostEstimate(flops=6_000_000, bytes_accessed=9_500_000, transcendentals=0),
@@ -391,7 +391,7 @@
             e_halo = jnp.concatenate([first_halo, e_halo])
         low, high = columns(e_halo)
         low, high = lax.ppermute(high, ("py", "pz"), CORNERS_UP), lax.ppermute(low, ("py", "pz"), CORNERS_DOWN)
-        cut = late.shape[0] if step < STEPS - 1 else late.shape[0] // 2
+        cut = late.shape[0] if step < STEPS - 1 else late.shape[0] - ROWS
         o_halos = [o_early, lax.ppermute(late[:cut], "py", ODD_CUTS)]
         o_final = lax.ppermute(late[cut:], "py", ODD_CUTS) if step == STEPS - 1 else None
         ends = [*px, z_even, z_odd, z_by]

time: 547 us -> 564 us (1.031)
  the two profiles are of different devices: /device:TPU:6 before, /device:TPU:34 now
where the time goes in v7:
time: 564 us; the launch traced here: 563 us
  waiting for transfers between devices  297 us (53%)
  starting transfers between devices  195 us (35%)
  Pallas kernels  59 us (10%)
  local copies, waits for them, and re-layouts  10.4 us (2%)
    ppermute x3, waiting for transfers between devices, local(): o_early = lax.ppermute(early, 'py', ODD_CUTS)  130 us
    ppermute x1, waiting for transfers between devices, local(): first_halo = lax.ppermute(e_first, 'py', EVEN_CUTS)  59 us
    ppermute x1, starting transfers between devices, local(): lax.ppermute(late[cut:], 'py', ODD_CUTS)  47.4 us
    ppermute x3, starting transfers between devices, local(): lax.ppermute(high, ('py', 'pz'), CORNERS_UP)  44 us
    pallas_call x3, Pallas kernels, partial_step(): pl.pallas_call(functools.partial(partial_kernel, first, last), grid_spec=...  40.2 us
    ppermute x9, waiting for transfers between devices, local(): relayed[k] = lax.ppermute(relayed[k], 'py', on)  35.3 us
    ppermute x3, waiting for transfers between devices, local(): o_halos = [o_early, lax.ppermute(late[:cut], 'py', ODD_CUTS)]  33 us
    ppermute x3, starting transfers between devices, local(): o_halos = [o_early, lax.ppermute(late[:cut], 'py', ODD_CUTS)]  18.2 us
  transfers between devices with their start and end apart: 53, of which 15 were waited for; matrix products, arithmetic and copies ran while one was open for 1% of the time, Pallas kernels for 10%

profile of v7, /device:TPU:34, one launch (start us, length us, event | category | flops | bytes accessed | tf_op | source)
XLA Modules:
  0.0 562.6 jit_solution(9545266433423626303)
XLA Ops:
  8.3 3.5 collective-permute-start.4
  15.3 59.0 %collective-permute-done.14 = f32[16,96,128]{2,1,0:T(8,128)} collective-permute-done((f32[16,96,128]{2,1,0:T(8,128)S(1)}, f32[16,96,128]{2,1,0:T(8,128)}, u32[]{:S(2)}, u32[]{:S(2)}) %collective-permute-start.14) | collective-permute-done | bytes 786464 | tf_op jit(solution)/shard_map/ppermute | solution.py:365
  81.4 4.4 collective-permute-start.16
  88.0 14.6 %partial_step.3 = (f32[64,96,128]{2,1,0:T(8,128)S(1)}, f32[64,96,128]{2,1,0:T(8,128)S(1)}, f32[2,64,96,128]{3,2,1,0:T(8,128)S(1)}, f32[2,96,128]{2,1,0:T(8,128)S...) custom-call(s32[2]{0:T(128)S(1)} %pad_add_fusion.odd_ref, ...), custom_call_target="tpu_custom_call" | custom-call | flops 60000000 | bytes 40000000 | tf_op jit(solution)/shard_map/partial_step/pallas_call | solution.py:152
  116.4 6.8 %collective-permute-start.6 = (f32[16,96,128]{2,1,0:T(8,128)S(1)}, f32[16,96,128]{2,1,0:T(8,128)S(1)}, u32[]{:S(2)}, u32[]{:S(2)}) collective-permute-start(f32[16,96,128]{2,1,0:T(8,128)S(1)} %get-tuple-element.52), channel_id=1, source_target_pairs={{16,32},{32,16},{48,64},{64,48},{80,96},{96,80},{17,33},{33,17},{4... | collective-permute-start | bytes 2359304 | tf_op jit(solution)/shard_map/ppermute | solution.py:387
  125.1 5.6 %collective-permute-done.12 = f32[16,96,128]{2,1,0:T(8,128)S(1)} collective-permute-done((f32[16,96,128]{2,1,0:T(8,128)S(1)}, f32[16,96,128]{2,1,0:T(8,128)S(1)}, u32[]{:S(2)}, u32[]{:S(2)}) %collective-permute-start.12) | collective-permute-done | bytes 786464 | tf_op jit(solution)/shard_map/ppermute | solution.py:385
  132.2 61.2 %collective-permute-done.6.early = f32[16,96,128]{2,1,0:T(8,128)S(1)} collective-permute-done((f32[16,96,128]{2,1,0:T(8,128)S(1)}, f32[16,96,128]{2,1,0:T(8,128)S(1)}, u32[]{:S(2)}, u32[]{:S(2)}) %collective-permute-start.6) | collective-permute-done | bytes 786464 | tf_op jit(solution)/shard_map/ppermute | solution.py:387
  194.8 35.3 %collective-permute-done.9.r0 = f32[16,96,128]{2,1,0:T(8,128)S(1)} collective-permute-done((f32[16,96,128]{2,1,0:T(8,128)S(1)}, f32[16,96,128]{2,1,0:T(8,128)S(1)}, u32[]{:S(2)}, u32[]{:S(2)}) %collective-permute-start.9) | collective-permute-done | bytes 786464 | tf_op jit(solution)/shard_map/ppermute | solution.py:389
  233.3 5.0 collective-permute-start.22
  238.3 3.6 collective-permute-start.18
  245.6 4.4 collective-permute-done.21.refs_16_
  253.3 2.7 collective-permute-done.23.refs_17_
  256.0 3.1 collective-permute-start.33
  259.1 2.7 collective-permute-start.34
  261.9 11.2 %partial_step.4 = (f32[64,96,128]{2,1,0:T(8,128)S(1)}, f32[64,96,128]{2,1,0:T(8,128)S(1)}, f32[2,64,96,128]{3,2,1,0:T(8,128)S(1)}, f32[2,96,128]{2,1,0:T(8,128)S...) custom-call(s32[2]{0:T(128)S(1)} %pad_add_fusion.odd_ref, ...), custom_call_target="tpu_custom_call" | custom-call | flops 60000000 | bytes 40000000 | tf_op jit(solution)/shard_map/partial_step/pallas_call | solution.py:152
  273.2 3.0 finish_even.3
  276.2 4.2 collective-permute-start.50
  281.0 3.3 collective-permute-start.30
  286.3 6.3 %collective-permute-start.25 = (f32[32,96,128]{2,1,0:T(8,128)S(1)}, f32[32,96,128]{2,1,0:T(8,128)S(1)}, u32[]{:S(2)}, u32[]{:S(2)}) collective-permute-start(f32[32,96,128]{2,1,0:T(8,128)S(1)} %copy-done.6), channel_id=1, source_target_pairs={{16,32},{32,16},{48,64},{64,48},{80,96},{96,80},{17,33},{33,17},{4... | collective-permute-start | bytes 4718600 | tf_op jit(solution)/shard_map/ppermute | solution.py:395
  293.9 8.2 %collective-permute-done.30 = f32[16,96,128]{2,1,0:T(8,128)S(1)} collective-permute-done((f32[16,96,128]{2,1,0:T(8,128)}, f32[16,96,128]{2,1,0:T(8,128)S(1)}, u32[]{:S(2)}, u32[]{:S(2)}) %collective-permute-start.30) | collective-permute-done | bytes 786464 | tf_op jit(solution)/shard_map/ppermute | solution.py:385
  302.8 63.4 %collective-permute-done.24.early = f32[16,96,128]{2,1,0:T(8,128)S(1)} collective-permute-done((f32[16,96,128]{2,1,0:T(8,128)S(1)}, f32[16,96,128]{2,1,0:T(8,128)S(1)}, u32[]{:S(2)}, u32[]{:S(2)}) %collective-permute-start.24) | collective-permute-done | bytes 786464 | tf_op jit(solution)/shard_map/ppermute | solution.py:387
  366.9 33.0 %collective-permute-done.25.late = f32[32,96,128]{2,1,0:T(8,128)S(1)} collective-permute-done((f32[32,96,128]{2,1,0:T(8,128)S(1)}, f32[32,96,128]{2,1,0:T(8,128)S(1)}, u32[]{:S(2)}, u32[]{:S(2)}) %collective-permute-start.25) | collective-permute-done | bytes 1572896 | tf_op jit(solution)/shard_map/ppermute | solution.py:395
  403.5 4.8 collective-permute-start.38
  412.2 4.7 collective-permute-done.40.refs_17_
  417.6 3.2 collective-permute-start.46
  424.2 4.3 collective-permute-start.48
  428.5 10.0 %collective-permute-start.49 = (f32[24,96,128]{2,1,0:T(8,128)S(1)}, f32[24,96,128]{2,1,0:T(8,128)S(1)}, u32[]{:S(2)}, u32[]{:S(2)}) collective-permute-start(f32[24,96,128]{2,1,0:T(8,128)S(1)} %slice.47), channel_id=1, source_target_pairs={{16,32},{32,16},{48,64},{64,48},{80,96},{96,80},{17,33},{33,17},{4... | collective-permute-start | bytes 3538952 | tf_op jit(solution)/shard_map/ppermute | solution.py:395
  441.4 5.9 %collective-permute-done.48.refs_0_ = f32[16,96,128]{2,1,0:T(8,128)S(1)} collective-permute-done((f32[16,96,128]{2,1,0:T(8,128)S(1)}, f32[16,96,128]{2,1,0:T(8,128)S(1)}, u32[]{:S(2)}, u32[]{:S(2)}) %collective-permute-start.48) | collective-permute-done | bytes 786464 | tf_op jit(solution)/shard_map/ppermute | solution.py:387
  447.2 36.4 %collective-permute-start.51 = (f32[64,128]{1,0:T(8,128)S(1)}, f32[64,128]{1,0:T(8,128)S(1)}, u32[]{:S(2)}, u32[]{:S(2)}) collective-permute-start(f32[64,128]{1,0:T(8,128)S(1)} %get-tuple-element.94), channel_id=1, source_target_pairs={{0,17},{1,18},{2,19},{16,1},{17,2},{18,3},{32,49},{33,50},{34,51},... | collective-permute-start | bytes 98312 | tf_op jit(solution)/shard_map/ppermute | solution.py:393
  487.2 9.2 %collective-permute-done.52.refs_2_ = f32[64,128]{1,0:T(8,128)S(1)} collective-permute-done((f32[64,128]{1,0:T(8,128)S(1)}, f32[64,128]{1,0:T(8,128)S(1)}, u32[]{:S(2)}, u32[]{:S(2)}) %collective-permute-start.52) | collective-permute-done | bytes 32800 | tf_op jit(solution)/shard_map/ppermute | solution.py:393
  496.5 47.4 %collective-permute-start.41 = (f32[8,96,128]{2,1,0:T(8,128)S(1)}, f32[8,96,128]{2,1,0:T(8,128)S(1)}, u32[]{:S(2)}, u32[]{:S(2)}) collective-permute-start(f32[8,96,128]{2,1,0:T(8,128)S(1)} %slice.46), channel_id=1, source_target_pairs={{16,32},{32,16},{48,64},{64,48},{80,96},{96,80},{17,33},{33,17},{4... | collective-permute-start | bytes 1179656 | tf_op jit(solution)/shard_map/ppermute | solution.py:396
  543.8 14.4 %partial_step.5 = (f32[64,96,128]{2,1,0:T(8,128)S(1)}, f32[64,96,128]{2,1,0:T(8,128)S(1)}, f32[4,64,96,128]{3,2,1,0:T(8,128)}) custom-call(s32[2]{0:T(128)S(1)} %pad_add_fusion.odd_ref, f32[64,96,128]{2,1,0:T(8,128)S(1)} %get-tuple-element.82.refs_0_.refs_1_.refs_2_, f32[64,96,128]{2,1,0:T(8,128)S(1)} %get-tuple-element.82.refs_0_.refs_1_.refs_2_, ...), custom_call_target="tpu_custom_call" | custom-call | flops 60000000 | bytes 40000000 | tf_op jit(solution)/shard_map/partial_step/pallas_call | solution.py:152
  (121 shorter events, 77.0 us)
Async XLA Ops:
  1.7 76.5 %collective-permute-start.15 = (f32[48,96,128]{2,1,0:T(8,128)S(1)}, f32[48,96,128]{2,1,0:T(8,128)}, u32[]{:S(2)}, u32[]{:S(2)}) collective-permute-start(f32[48,96,128]{2,1,0:T(8,128)S(1)} %shard_map.30), channel_id=1, source_target_pairs={{0,16},{16,0},{32,48},{48,32},{64,80},{80,64},{96,112},{112,96},{1... | collective-permute-start | bytes 7077896 | tf_op jit(solution)/shard_map/ppermute | solution.py:367
  5.0 69.3 %collective-permute-start.14 = (f32[16,96,128]{2,1,0:T(8,128)S(1)}, f32[16,96,128]{2,1,0:T(8,128)}, u32[]{:S(2)}, u32[]{:S(2)}) collective-permute-start(f32[16,96,128]{2,1,0:T(8,128)S(1)} %shard_map.29), channel_id=1, source_target_pairs={{0,16},{16,0},{32,48},{48,32},{64,80},{80,64},{96,112},{112,96},{1... | collective-permute-start | bytes 2359304 | tf_op jit(solution)/shard_map/ppermute | solution.py:365
  8.3 68.5 %collective-permute-start.4 = (f32[3,32,128]{2,1,0:T(8,128)S(1)}, f32[3,32,128]{2,1,0:T(8,128)S(1)}, u32[]{:S(2)}, u32[]{:S(2)}) collective-permute-start(f32[3,32,128]{2,1,0:T(8,128)S(1)} %get-tuple-element.107), channel_id=1, source_target_pairs={{1,3},{2,0},{5,7},{6,4},{9,11},{10,8},{13,15},{14,12},{17,19},{18,... | collective-permute-start | bytes 147464 | tf_op jit(solution)/shard_map/ppermute | solution.py:379
  11.8 69.5 %collective-permute-start.3 = (f32[3,32,128]{2,1,0:T(8,128)S(1)}, f32[3,32,128]{2,1,0:T(8,128)S(1)}, u32[]{:S(2)}, u32[]{:S(2)}) collective-permute-start(f32[3,32,128]{2,1,0:T(8,128)S(1)} %get-tuple-element.108), channel_id=1, source_target_pairs={{1,2},{2,1},{5,6},{6,5},{9,10},{10,9},{13,14},{14,13},{17,18},{18,... | collective-permute-start | bytes 147464 | tf_op jit(solution)/shard_map/ppermute | solution.py:381
  14.2 73.8 %collective-permute-start.2 = (f32[3,64,128]{2,1,0:T(8,128)S(1)}, f32[3,64,128]{2,1,0:T(8,128)S(1)}, u32[]{:S(2)}, u32[]{:S(2)}) collective-permute-start(f32[3,64,128]{2,1,0:T(8,128)S(1)} %get-tuple-element.102), channel_id=1, source_target_pairs={{0,1},{1,0},{2,3},{3,2},{4,5},{5,4},{6,7},{7,6},{8,9},{9,8},{10,11... | collective-permute-start | bytes 294920 | tf_op jit(solution)/shard_map/ppermute | solution.py:380
  81.4 23.5 %collective-permute-start.16 = (f32[64,128]{1,0:T(8,128)S(1)}, f32[64,128]{1,0:T(8,128)S(1)}, u32[]{:S(2)}, u32[]{:S(2)}) collective-permute-start(f32[64,128]{1,0:T(8,128)S(1)} %get-tuple-element.60), channel_id=1, source_target_pairs={{0,17},{1,18},{2,19},{16,1},{17,2},{18,3},{32,49},{33,50},{34,51},... | collective-permute-start | bytes 98312 | tf_op jit(solution)/shard_map/ppermute | solution.py:393
  85.8 19.1 %collective-permute-start.17 = (f32[64,128]{1,0:T(8,128)S(1)}, f32[64,128]{1,0:T(8,128)S(1)}, u32[]{:S(2)}, u32[]{:S(2)}) collective-permute-start(f32[64,128]{1,0:T(8,128)S(1)} %get-tuple-element.61), channel_id=1, source_target_pairs={{1,16},{2,17},{3,18},{17,0},{18,1},{19,2},{33,48},{34,49},{35,50},... | collective-permute-start | bytes 98312 | tf_op jit(solution)/shard_map/ppermute | solution.py:393
  107.6 142.4 %collective-permute-start.32 = (f32[64,96,128]{2,1,0:T(8,128)S(1)}, f32[64,96,128]{2,1,0:T(8,128)}, u32[]{:S(2)}, u32[]{:S(2)}) collective-permute-start(f32[64,96,128]{2,1,0:T(8,128)S(1)} %get-tuple-element.65.refs_9_.refs_10_.refs_11_), channel_id=1, source_target_pairs={{0,16},{16,0},{32,48},{48,32},{64,80},{80,64},{96,112},{112,96},{1... | collective-permute-start | bytes 9437192 | tf_op jit(solution)/shard_map/ppermute | solution.py:402
  116.4 77.1 %collective-permute-start.6 = (f32[16,96,128]{2,1,0:T(8,128)S(1)}, f32[16,96,128]{2,1,0:T(8,128)S(1)}, u32[]{:S(2)}, u32[]{:S(2)}) collective-permute-start(f32[16,96,128]{2,1,0:T(8,128)S(1)} %get-tuple-element.52), channel_id=1, source_target_pairs={{16,32},{32,16},{48,64},{64,48},{80,96},{96,80},{17,33},{33,17},{4... | collective-permute-start | bytes 2359304 | tf_op jit(solution)/shard_map/ppermute | solution.py:387
  123.2 106.8 %collective-permute-start.7 = (f32[32,96,128]{2,1,0:T(8,128)S(1)}, f32[32,96,128]{2,1,0:T(8,128)S(1)}, u32[]{:S(2)}, u32[]{:S(2)}) collective-permute-start(f32[32,96,128]{2,1,0:T(8,128)S(1)} %get-tuple-element.53), channel_id=1, source_target_pairs={{16,32},{32,16},{48,64},{64,48},{80,96},{96,80},{17,33},{33,17},{4... | collective-permute-start | bytes 4718600 | tf_op jit(solution)/shard_map/ppermute | solution.py:395
  130.8 63.9 %collective-permute-start.11 = (f32[16,96,128]{2,1,0:T(8,128)S(1)}, f32[16,96,128]{2,1,0:T(8,128)S(1)}, u32[]{:S(2)}, u32[]{:S(2)}) collective-permute-start(f32[16,96,128]{2,1,0:T(8,128)S(1)} %collective-permute-done.10), channel_id=1, source_target_pairs={{0,48},{112,64},{1,49},{113,65},{2,50},{114,66},{3,51},{115,67},{4... | collective-permute-start | bytes 2359304 | tf_op jit(solution)/shard_map/ppermute | solution.py:389
  131.5 63.2 %collective-permute-start.13 = (f32[16,96,128]{2,1,0:T(8,128)S(1)}, f32[16,96,128]{2,1,0:T(8,128)S(1)}, u32[]{:S(2)}, u32[]{:S(2)}) collective-permute-start(f32[16,96,128]{2,1,0:T(8,128)S(1)} %collective-permute-done.12), channel_id=1, source_target_pairs={{0,16},{112,96},{1,17},{113,97},{2,18},{114,98},{3,19},{115,99},{4... | collective-permute-start | bytes 2359304 | tf_op jit(solution)/shard_map/ppermute | solution.py:389
  193.4 36.6 %collective-permute-start.9 = (f32[16,96,128]{2,1,0:T(8,128)S(1)}, f32[16,96,128]{2,1,0:T(8,128)S(1)}, u32[]{:S(2)}, u32[]{:S(2)}) collective-permute-start(f32[16,96,128]{2,1,0:T(8,128)S(1)} %collective-permute-done.8), channel_id=1, source_target_pairs={{0,80},{112,32},{1,81},{113,33},{2,82},{114,34},{3,83},{115,35},{4... | collective-permute-start | bytes 2359304 | tf_op jit(solution)/shard_map/ppermute | solution.py:389
  232.5 53.7 %collective-permute-start.26 = (f32[16,96,128]{2,1,0:T(8,128)}, f32[16,96,128]{2,1,0:T(8,128)S(1)}, u32[]{:S(2)}, u32[]{:S(2)}) collective-permute-start(f32[16,96,128]{2,1,0:T(8,128)} %get-tuple-element.73), channel_id=1, source_target_pairs={{96,0},{16,112},{97,1},{17,113},{98,2},{18,114},{99,3},{19,115},{1... | collective-permute-start | bytes 2359304 | tf_op jit(solution)/shard_map/ppermute | solution.py:385
  238.3 23.6 %collective-permute-start.18 = (f32[4,96,128]{2,1,0:T(8,128)S(1)}, f32[4,96,128]{2,1,0:T(8,128)S(1)}, u32[]{:S(2)}, u32[]{:S(2)}) collective-permute-start(f32[4,96,128]{2,1,0:T(8,128)S(1)} %get-tuple-element.66), channel_id=1, source_target_pairs={{0,4},{4,8},{8,12},{1,5},{5,9},{9,13},{2,6},{6,10},{10,14},{3,7},{... | collective-permute-start | bytes 589832 | tf_op jit(solution)/shard_map/ppermute | solution.py:386
  241.8 20.0 %collective-permute-start.19 = (f32[4,96,128]{2,1,0:T(8,128)S(1)}, f32[4,96,128]{2,1,0:T(8,128)S(1)}, u32[]{:S(2)}, u32[]{:S(2)}) collective-permute-start(f32[4,96,128]{2,1,0:T(8,128)S(1)} %get-tuple-element.67), channel_id=1, source_target_pairs={{4,0},{8,4},{12,8},{5,1},{9,5},{13,9},{6,2},{10,6},{14,10},{7,3},{... | collective-permute-start | bytes 589832 | tf_op jit(solution)/shard_map/ppermute | solution.py:386
  276.2 164.4 %collective-permute-start.50 = (f32[64,96,128]{2,1,0:T(8,128)S(1)}, f32[64,96,128]{2,1,0:T(8,128)S(1)}, u32[]{:S(2)}, u32[]{:S(2)}) collective-permute-start(f32[64,96,128]{2,1,0:T(8,128)S(1)} %get-tuple-element.84.refs_9_.refs_10_.refs_11_), channel_id=1, source_target_pairs={{0,16},{16,0},{32,48},{48,32},{64,80},{80,64},{96,112},{112,96},{1... | collective-permute-start | bytes 9437192 | tf_op jit(solution)/shard_map/ppermute | solution.py:402
  281.0 21.0 %collective-permute-start.30 = (f32[16,96,128]{2,1,0:T(8,128)}, f32[16,96,128]{2,1,0:T(8,128)S(1)}, u32[]{:S(2)}, u32[]{:S(2)}) collective-permute-start(f32[16,96,128]{2,1,0:T(8,128)} %get-tuple-element.73), channel_id=1, source_target_pairs={{32,0},{80,112},{33,1},{81,113},{34,2},{82,114},{35,3},{83,115},{3... | collective-permute-start | bytes 2359304 | tf_op jit(solution)/shard_map/ppermute | solution.py:385
  284.3 81.9 %collective-permute-start.24 = (f32[16,96,128]{2,1,0:T(8,128)S(1)}, f32[16,96,128]{2,1,0:T(8,128)S(1)}, u32[]{:S(2)}, u32[]{:S(2)}) collective-permute-start(f32[16,96,128]{2,1,0:T(8,128)S(1)} %get-tuple-element.71), channel_id=1, source_target_pairs={{16,32},{32,16},{48,64},{64,48},{80,96},{96,80},{17,33},{33,17},{4... | collective-permute-start | bytes 2359304 | tf_op jit(solution)/shard_map/ppermute | solution.py:387
  286.3 113.6 %collective-permute-start.25 = (f32[32,96,128]{2,1,0:T(8,128)S(1)}, f32[32,96,128]{2,1,0:T(8,128)S(1)}, u32[]{:S(2)}, u32[]{:S(2)}) collective-permute-start(f32[32,96,128]{2,1,0:T(8,128)S(1)} %copy-done.6), channel_id=1, source_target_pairs={{16,32},{32,16},{48,64},{64,48},{80,96},{96,80},{17,33},{33,17},{4... | collective-permute-start | bytes 4718600 | tf_op jit(solution)/shard_map/ppermute | solution.py:395
  292.6 74.3 %collective-permute-start.27 = (f32[16,96,128]{2,1,0:T(8,128)S(1)}, f32[16,96,128]{2,1,0:T(8,128)S(1)}, u32[]{:S(2)}, u32[]{:S(2)}) collective-permute-start(f32[16,96,128]{2,1,0:T(8,128)S(1)} %collective-permute-done.26), channel_id=1, source_target_pairs={{0,80},{112,32},{1,81},{113,33},{2,82},{114,34},{3,83},{115,35},{4... | collective-permute-start | bytes 2359304 | tf_op jit(solution)/shard_map/ppermute | solution.py:389
  302.1 64.8 %collective-permute-start.29 = (f32[16,96,128]{2,1,0:T(8,128)S(1)}, f32[16,96,128]{2,1,0:T(8,128)S(1)}, u32[]{:S(2)}, u32[]{:S(2)}) collective-permute-start(f32[16,96,128]{2,1,0:T(8,128)S(1)} %collective-permute-done.28), channel_id=1, source_target_pairs={{0,48},{112,64},{1,49},{113,65},{2,50},{114,66},{3,51},{115,67},{4... | collective-permute-start | bytes 2359304 | tf_op jit(solution)/shard_map/ppermute | solution.py:389
  401.5 27.0 %collective-permute-start.42 = (f32[16,96,128]{2,1,0:T(8,128)S(1)}, f32[16,96,128]{2,1,0:T(8,128)S(1)}, u32[]{:S(2)}, u32[]{:S(2)}) collective-permute-start(f32[16,96,128]{2,1,0:T(8,128)S(1)} %get-tuple-element.91), channel_id=1, source_target_pairs={{96,0},{16,112},{97,1},{17,113},{98,2},{18,114},{99,3},{19,115},{1... | collective-permute-start | bytes 2359304 | tf_op jit(solution)/shard_map/ppermute | solution.py:385
  416.9 21.6 %collective-permute-start.44 = (f32[16,96,128]{2,1,0:T(8,128)S(1)}, f32[16,96,128]{2,1,0:T(8,128)S(1)}, u32[]{:S(2)}, u32[]{:S(2)}) collective-permute-start(f32[16,96,128]{2,1,0:T(8,128)S(1)} %get-tuple-element.91), channel_id=1, source_target_pairs={{64,0},{48,112},{65,1},{49,113},{66,2},{50,114},{67,3},{51,115},{6... | collective-permute-start | bytes 2359304 | tf_op jit(solution)/shard_map/ppermute | solution.py:385
  417.6 22.2 %collective-permute-start.46 = (f32[16,96,128]{2,1,0:T(8,128)S(1)}, f32[16,96,128]{2,1,0:T(8,128)S(1)}, u32[]{:S(2)}, u32[]{:S(2)}) collective-permute-start(f32[16,96,128]{2,1,0:T(8,128)S(1)} %get-tuple-element.91), channel_id=1, source_target_pairs={{32,0},{80,112},{33,1},{81,113},{34,2},{82,114},{35,3},{83,115},{3... | collective-permute-start | bytes 2359304 | tf_op jit(solution)/shard_map/ppermute | solution.py:385
  424.2 23.1 %collective-permute-start.48 = (f32[16,96,128]{2,1,0:T(8,128)S(1)}, f32[16,96,128]{2,1,0:T(8,128)S(1)}, u32[]{:S(2)}, u32[]{:S(2)}) collective-permute-start(f32[16,96,128]{2,1,0:T(8,128)S(1)} %get-tuple-element.92), channel_id=1, source_target_pairs={{16,32},{32,16},{48,64},{64,48},{80,96},{96,80},{17,33},{33,17},{4... | collective-permute-start | bytes 2359304 | tf_op jit(solution)/shard_map/ppermute | solution.py:387
  428.5 131.5 %collective-permute-start.49 = (f32[24,96,128]{2,1,0:T(8,128)S(1)}, f32[24,96,128]{2,1,0:T(8,128)S(1)}, u32[]{:S(2)}, u32[]{:S(2)}) collective-permute-start(f32[24,96,128]{2,1,0:T(8,128)S(1)} %slice.47), channel_id=1, source_target_pairs={{16,32},{32,16},{48,64},{64,48},{80,96},{96,80},{17,33},{33,17},{4... | collective-permute-start | bytes 3538952 | tf_op jit(solution)/shard_map/ppermute | solution.py:395
  438.6 122.9 %collective-permute-start.43 = (f32[16,96,128]{2,1,0:T(8,128)S(1)}, f32[16,96,128]{2,1,0:T(8,128)S(1)}, u32[]{:S(2)}, u32[]{:S(2)}) collective-permute-start(f32[16,96,128]{2,1,0:T(8,128)S(1)} %collective-permute-done.42), channel_id=1, source_target_pairs={{0,80},{112,32},{1,81},{113,33},{2,82},{114,34},{3,83},{115,35},{4... | collective-permute-start | bytes 2359304 | tf_op jit(solution)/shard_map/ppermute | solution.py:389
  439.9 121.6 %collective-permute-start.45 = (f32[16,96,128]{2,1,0:T(8,128)S(1)}, f32[16,96,128]{2,1,0:T(8,128)S(1)}, u32[]{:S(2)}, u32[]{:S(2)}) collective-permute-start(f32[16,96,128]{2,1,0:T(8,128)S(1)} %collective-permute-done.44), channel_id=1, source_target_pairs={{0,48},{112,64},{1,49},{113,65},{2,50},{114,66},{3,51},{115,67},{4... | collective-permute-start | bytes 2359304 | tf_op jit(solution)/shard_map/ppermute | solution.py:389
  440.6 120.9 %collective-permute-start.47 = (f32[16,96,128]{2,1,0:T(8,128)S(1)}, f32[16,96,128]{2,1,0:T(8,128)S(1)}, u32[]{:S(2)}, u32[]{:S(2)}) collective-permute-start(f32[16,96,128]{2,1,0:T(8,128)S(1)} %collective-permute-done.46), channel_id=1, source_target_pairs={{0,16},{112,96},{1,17},{113,97},{2,18},{114,98},{3,19},{115,99},{4... | collective-permute-start | bytes 2359304 | tf_op jit(solution)/shard_map/ppermute | solution.py:389
  447.2 38.0 %collective-permute-start.51 = (f32[64,128]{1,0:T(8,128)S(1)}, f32[64,128]{1,0:T(8,128)S(1)}, u32[]{:S(2)}, u32[]{:S(2)}) collective-permute-start(f32[64,128]{1,0:T(8,128)S(1)} %get-tuple-element.94), channel_id=1, source_target_pairs={{0,17},{1,18},{2,19},{16,1},{17,2},{18,3},{32,49},{33,50},{34,51},... | collective-permute-start | bytes 98312 | tf_op jit(solution)/shard_map/ppermute | solution.py:393
  496.5 65.0 %collective-permute-start.41 = (f32[8,96,128]{2,1,0:T(8,128)S(1)}, f32[8,96,128]{2,1,0:T(8,128)S(1)}, u32[]{:S(2)}, u32[]{:S(2)}) collective-permute-start(f32[8,96,128]{2,1,0:T(8,128)S(1)} %slice.46), channel_id=1, source_target_pairs={{16,32},{32,16},{48,64},{64,48},{80,96},{96,80},{17,33},{33,17},{4... | collective-permute-start | bytes 1179656 | tf_op jit(solution)/shard_map/ppermute | solution.py:396
  (30 other events, 570.7 us)

commit v8 on v7

--- a/solution.py
+++ b/solution.py
@@ -361,9 +361,9 @@
     odd_ref = jnp.stack([odd, pz_odd]).astype(jnp.int32)
     e_plane, o_plane = 3 * (1 - odd), 3 * odd
     rows = density.shape[1]
-    (e_first,) = pick(density, e_plane, [(0, TILE)], 52)
+    (e_first,) = pick(density, e_plane, [(0, ROWS)], 52)
     first_halo = lax.ppermute(e_first, "py", EVEN_CUTS)
-    (e_rest,) = pick(density, e_plane, [(TILE, rows)], 50)
+    (e_rest,) = pick(density, e_plane, [(ROWS, rows)], 50)
     e_halo = lax.ppermute(e_rest, "py", EVEN_CUTS)
     spans = [(0, EARLY), (EARLY, DIRECT), (DIRECT, rows)]
     early, late, rest = pick(density, o_plane, spans, 46)
@@ -404,7 +404,8 @@
         o, early, late, rest, x_low, x_high, z_even, z_odd = outs
     out = place(e_plane, e_part, [(0, [e_halo])], (low, high), mid)
     out = place(o_plane, o_part, [(0, o_halos[:1]), (EARLY, o_halos[1:])], (), out)
-    return place(o_plane, o_part, [(EARLY + cut, [o_final]), (DIRECT, relayed)], (), out)
+    out = place(o_plane, o_part, [(DIRECT, relayed)], (), out)
+    return place(o_plane, o_part, [(EARLY + cut, [o_final])], (), out)
 
 
 def solution(mesh):

time: 564 us -> 564 us (level)
  no operation moved by 1% of the time
where the time goes in v8:
time: 564 us; the launch traced here: 562 us
  waiting for transfers between devices  297 us (53%)
  starting transfers between devices  195 us (35%)
  Pallas kernels  59.8 us (11%)
  local copies, waits for them, and re-layouts  9.35 us (2%)
    ppermute x3, waiting for transfers between devices, local(): o_early = lax.ppermute(early, 'py', ODD_CUTS)  130 us
    ppermute x1, waiting for transfers between devices, local(): first_halo = lax.ppermute(e_first, 'py', EVEN_CUTS)  59.1 us
    ppermute x1, starting transfers between devices, local(): lax.ppermute(late[cut:], 'py', ODD_CUTS)  47.4 us
    ppermute x3, starting transfers between devices, local(): lax.ppermute(high, ('py', 'pz'), CORNERS_UP)  44 us
    pallas_call x3, Pallas kernels, partial_step(): pl.pallas_call(functools.partial(partial_kernel, first, last), grid_spec=...  40.2 us
    ppermute x9, waiting for transfers between devices, local(): relayed[k] = lax.ppermute(relayed[k], 'py', on)  35.3 us
    ppermute x3, waiting for transfers between devices, local(): o_halos = [o_early, lax.ppermute(late[:cut], 'py', ODD_CUTS)]  33 us
    ppermute x3, starting transfers between devices, local(): o_halos = [o_early, lax.ppermute(late[:cut], 'py', ODD_CUTS)]  18.2 us
  transfers between devices with their start and end apart: 53, of which 15 were waited for; matrix products, arithmetic and copies ran while one was open for 1% of the time, Pallas kernels for 10%

profile of v8, /device:TPU:34, one launch (start us, length us, event | category | flops | bytes accessed | tf_op | source)
XLA Modules:
  0.0 562.4 jit_solution(10948119858573200975)
XLA Ops:
  8.3 3.5 collective-permute-start.4
  15.3 59.1 %collective-permute-done.14 = f32[8,96,128]{2,1,0:T(8,128)S(1)} collective-permute-done((f32[8,96,128]{2,1,0:T(8,128)S(1)}, f32[8,96,128]{2,1,0:T(8,128)S(1)}, u32[]{:S(2)}, u32[]{:S(2)}) %collective-permute-start.14) | collective-permute-done | bytes 393248 | tf_op jit(solution)/shard_map/ppermute | solution.py:365
  80.3 4.4 collective-permute-start.16
  87.0 14.6 %partial_step.3 = (f32[64,96,128]{2,1,0:T(8,128)S(1)}, f32[64,96,128]{2,1,0:T(8,128)S(1)}, f32[2,64,96,128]{3,2,1,0:T(8,128)S(1)}, f32[2,96,128]{2,1,0:T(8,128)S...) custom-call(s32[2]{0:T(128)S(1)} %pad_add_fusion.odd_ref, ...), custom_call_target="tpu_custom_call" | custom-call | flops 60000000 | bytes 40000000 | tf_op jit(solution)/shard_map/partial_step/pallas_call | solution.py:152
  115.4 6.8 %collective-permute-start.6 = (f32[16,96,128]{2,1,0:T(8,128)S(1)}, f32[16,96,128]{2,1,0:T(8,128)S(1)}, u32[]{:S(2)}, u32[]{:S(2)}) collective-permute-start(f32[16,96,128]{2,1,0:T(8,128)S(1)} %get-tuple-element.52), channel_id=1, source_target_pairs={{16,32},{32,16},{48,64},{64,48},{80,96},{96,80},{17,33},{33,17},{4... | collective-permute-start | bytes 2359304 | tf_op jit(solution)/shard_map/ppermute | solution.py:387
  124.1 5.6 %collective-permute-done.12 = f32[16,96,128]{2,1,0:T(8,128)S(1)} collective-permute-done((f32[16,96,128]{2,1,0:T(8,128)S(1)}, f32[16,96,128]{2,1,0:T(8,128)S(1)}, u32[]{:S(2)}, u32[]{:S(2)}) %collective-permute-start.12) | collective-permute-done | bytes 786464 | tf_op jit(solution)/shard_map/ppermute | solution.py:385
  131.2 61.2 %collective-permute-done.6.early = f32[16,96,128]{2,1,0:T(8,128)S(1)} collective-permute-done((f32[16,96,128]{2,1,0:T(8,128)S(1)}, f32[16,96,128]{2,1,0:T(8,128)S(1)}, u32[]{:S(2)}, u32[]{:S(2)}) %collective-permute-start.6) | collective-permute-done | bytes 786464 | tf_op jit(solution)/shard_map/ppermute | solution.py:387
  193.7 35.3 %collective-permute-done.9.r0 = f32[16,96,128]{2,1,0:T(8,128)S(1)} collective-permute-done((f32[16,96,128]{2,1,0:T(8,128)S(1)}, f32[16,96,128]{2,1,0:T(8,128)S(1)}, u32[]{:S(2)}, u32[]{:S(2)}) %collective-permute-start.9) | collective-permute-done | bytes 786464 | tf_op jit(solution)/shard_map/ppermute | solution.py:389
  232.3 5.0 collective-permute-start.22
  237.2 3.6 collective-permute-start.18
  244.6 4.4 collective-permute-done.21.refs_16_
  252.3 2.7 collective-permute-done.23.refs_17_
  255.0 3.1 collective-permute-start.33
  258.1 2.7 collective-permute-start.34
  260.9 11.2 %partial_step.4 = (f32[64,96,128]{2,1,0:T(8,128)S(1)}, f32[64,96,128]{2,1,0:T(8,128)S(1)}, f32[2,64,96,128]{3,2,1,0:T(8,128)S(1)}, f32[2,96,128]{2,1,0:T(8,128)S...) custom-call(s32[2]{0:T(128)S(1)} %pad_add_fusion.odd_ref, ...), custom_call_target="tpu_custom_call" | custom-call | flops 60000000 | bytes 40000000 | tf_op jit(solution)/shard_map/partial_step/pallas_call | solution.py:152
  272.2 3.0 finish_even.3
  275.2 4.2 collective-permute-start.50
  280.0 3.3 collective-permute-start.30
  285.3 6.3 %collective-permute-start.25 = (f32[32,96,128]{2,1,0:T(8,128)S(1)}, f32[32,96,128]{2,1,0:T(8,128)S(1)}, u32[]{:S(2)}, u32[]{:S(2)}) collective-permute-start(f32[32,96,128]{2,1,0:T(8,128)S(1)} %copy-done.6), channel_id=1, source_target_pairs={{16,32},{32,16},{48,64},{64,48},{80,96},{96,80},{17,33},{33,17},{4... | collective-permute-start | bytes 4718600 | tf_op jit(solution)/shard_map/ppermute | solution.py:395
  292.9 8.2 %collective-permute-done.30 = f32[16,96,128]{2,1,0:T(8,128)S(1)} collective-permute-done((f32[16,96,128]{2,1,0:T(8,128)}, f32[16,96,128]{2,1,0:T(8,128)S(1)}, u32[]{:S(2)}, u32[]{:S(2)}) %collective-permute-start.30) | collective-permute-done | bytes 786464 | tf_op jit(solution)/shard_map/ppermute | solution.py:385
  301.8 63.4 %collective-permute-done.24.early = f32[16,96,128]{2,1,0:T(8,128)S(1)} collective-permute-done((f32[16,96,128]{2,1,0:T(8,128)S(1)}, f32[16,96,128]{2,1,0:T(8,128)S(1)}, u32[]{:S(2)}, u32[]{:S(2)}) %collective-permute-start.24) | collective-permute-done | bytes 786464 | tf_op jit(solution)/shard_map/ppermute | solution.py:387
  365.9 33.0 %collective-permute-done.25.late = f32[32,96,128]{2,1,0:T(8,128)S(1)} collective-permute-done((f32[32,96,128]{2,1,0:T(8,128)S(1)}, f32[32,96,128]{2,1,0:T(8,128)S(1)}, u32[]{:S(2)}, u32[]{:S(2)}) %collective-permute-start.25) | collective-permute-done | bytes 1572896 | tf_op jit(solution)/shard_map/ppermute | solution.py:395
  402.5 4.8 collective-permute-start.38
  411.2 4.7 collective-permute-done.40.refs_17_
  416.6 3.2 collective-permute-start.46
  423.2 4.3 collective-permute-start.48
  427.5 10.0 %collective-permute-start.49 = (f32[24,96,128]{2,1,0:T(8,128)S(1)}, f32[24,96,128]{2,1,0:T(8,128)S(1)}, u32[]{:S(2)}, u32[]{:S(2)}) collective-permute-start(f32[24,96,128]{2,1,0:T(8,128)S(1)} %slice.47), channel_id=1, source_target_pairs={{16,32},{32,16},{48,64},{64,48},{80,96},{96,80},{17,33},{33,17},{4... | collective-permute-start | bytes 3538952 | tf_op jit(solution)/shard_map/ppermute | solution.py:395
  440.4 5.9 %collective-permute-done.48.refs_0_ = f32[16,96,128]{2,1,0:T(8,128)S(1)} collective-permute-done((f32[16,96,128]{2,1,0:T(8,128)S(1)}, f32[16,96,128]{2,1,0:T(8,128)S(1)}, u32[]{:S(2)}, u32[]{:S(2)}) %collective-permute-start.48) | collective-permute-done | bytes 786464 | tf_op jit(solution)/shard_map/ppermute | solution.py:387
  446.2 36.4 %collective-permute-start.51 = (f32[64,128]{1,0:T(8,128)S(1)}, f32[64,128]{1,0:T(8,128)S(1)}, u32[]{:S(2)}, u32[]{:S(2)}) collective-permute-start(f32[64,128]{1,0:T(8,128)S(1)} %get-tuple-element.94), channel_id=1, source_target_pairs={{0,17},{1,18},{2,19},{16,1},{17,2},{18,3},{32,49},{33,50},{34,51},... | collective-permute-start | bytes 98312 | tf_op jit(solution)/shard_map/ppermute | solution.py:393
  486.2 9.2 %collective-permute-done.52.refs_2_ = f32[64,128]{1,0:T(8,128)S(1)} collective-permute-done((f32[64,128]{1,0:T(8,128)S(1)}, f32[64,128]{1,0:T(8,128)S(1)}, u32[]{:S(2)}, u32[]{:S(2)}) %collective-permute-start.52) | collective-permute-done | bytes 32800 | tf_op jit(solution)/shard_map/ppermute | solution.py:393
  495.4 47.4 %collective-permute-start.41 = (f32[8,96,128]{2,1,0:T(8,128)S(1)}, f32[8,96,128]{2,1,0:T(8,128)S(1)}, u32[]{:S(2)}, u32[]{:S(2)}) collective-permute-start(f32[8,96,128]{2,1,0:T(8,128)S(1)} %slice.46), channel_id=1, source_target_pairs={{16,32},{32,16},{48,64},{64,48},{80,96},{96,80},{17,33},{33,17},{4... | collective-permute-start | bytes 1179656 | tf_op jit(solution)/shard_map/ppermute | solution.py:396
  542.8 14.4 %partial_step.5 = (f32[64,96,128]{2,1,0:T(8,128)S(1)}, f32[64,96,128]{2,1,0:T(8,128)S(1)}, f32[4,64,96,128]{3,2,1,0:T(8,128)}) custom-call(s32[2]{0:T(128)S(1)} %pad_add_fusion.odd_ref, f32[64,96,128]{2,1,0:T(8,128)S(1)} %get-tuple-element.82.refs_0_.refs_1_.refs_2_, f32[64,96,128]{2,1,0:T(8,128)S(1)} %get-tuple-element.82.refs_0_.refs_1_.refs_2_, ...), custom_call_target="tpu_custom_call" | custom-call | flops 60000000 | bytes 40000000 | tf_op jit(solution)/shard_map/partial_step/pallas_call | solution.py:152
  (122 shorter events, 76.7 us)
Async XLA Ops:
  1.8 75.2 %collective-permute-start.15 = (f32[56,96,128]{2,1,0:T(8,128)S(1)}, f32[56,96,128]{2,1,0:T(8,128)}, u32[]{:S(2)}, u32[]{:S(2)}) collective-permute-start(f32[56,96,128]{2,1,0:T(8,128)S(1)} %shard_map.30), channel_id=1, source_target_pairs={{0,16},{16,0},{32,48},{48,32},{64,80},{80,64},{96,112},{112,96},{1... | collective-permute-start | bytes 8257544 | tf_op jit(solution)/shard_map/ppermute | solution.py:367
  5.0 69.3 %collective-permute-start.14 = (f32[8,96,128]{2,1,0:T(8,128)S(1)}, f32[8,96,128]{2,1,0:T(8,128)S(1)}, u32[]{:S(2)}, u32[]{:S(2)}) collective-permute-start(f32[8,96,128]{2,1,0:T(8,128)S(1)} %shard_map.29), channel_id=1, source_target_pairs={{0,16},{16,0},{32,48},{48,32},{64,80},{80,64},{96,112},{112,96},{1... | collective-permute-start | bytes 1179656 | tf_op jit(solution)/shard_map/ppermute | solution.py:365
  8.3 67.4 %collective-permute-start.4 = (f32[3,32,128]{2,1,0:T(8,128)S(1)}, f32[3,32,128]{2,1,0:T(8,128)S(1)}, u32[]{:S(2)}, u32[]{:S(2)}) collective-permute-start(f32[3,32,128]{2,1,0:T(8,128)S(1)} %get-tuple-element.107), channel_id=1, source_target_pairs={{1,3},{2,0},{5,7},{6,4},{9,11},{10,8},{13,15},{14,12},{17,19},{18,... | collective-permute-start | bytes 147464 | tf_op jit(solution)/shard_map/ppermute | solution.py:379
  11.8 68.5 %collective-permute-start.3 = (f32[3,32,128]{2,1,0:T(8,128)S(1)}, f32[3,32,128]{2,1,0:T(8,128)S(1)}, u32[]{:S(2)}, u32[]{:S(2)}) collective-permute-start(f32[3,32,128]{2,1,0:T(8,128)S(1)} %get-tuple-element.108), channel_id=1, source_target_pairs={{1,2},{2,1},{5,6},{6,5},{9,10},{10,9},{13,14},{14,13},{17,18},{18,... | collective-permute-start | bytes 147464 | tf_op jit(solution)/shard_map/ppermute | solution.py:381
  14.1 72.8 %collective-permute-start.2 = (f32[3,64,128]{2,1,0:T(8,128)S(1)}, f32[3,64,128]{2,1,0:T(8,128)S(1)}, u32[]{:S(2)}, u32[]{:S(2)}) collective-permute-start(f32[3,64,128]{2,1,0:T(8,128)S(1)} %get-tuple-element.102), channel_id=1, source_target_pairs={{0,1},{1,0},{2,3},{3,2},{4,5},{5,4},{6,7},{7,6},{8,9},{9,8},{10,11... | collective-permute-start | bytes 294920 | tf_op jit(solution)/shard_map/ppermute | solution.py:380
  80.3 23.5 %collective-permute-start.16 = (f32[64,128]{1,0:T(8,128)S(1)}, f32[64,128]{1,0:T(8,128)S(1)}, u32[]{:S(2)}, u32[]{:S(2)}) collective-permute-start(f32[64,128]{1,0:T(8,128)S(1)} %get-tuple-element.60), channel_id=1, source_target_pairs={{0,17},{1,18},{2,19},{16,1},{17,2},{18,3},{32,49},{33,50},{34,51},... | collective-permute-start | bytes 98312 | tf_op jit(solution)/shard_map/ppermute | solution.py:393
  84.8 19.1 %collective-permute-start.17 = (f32[64,128]{1,0:T(8,128)S(1)}, f32[64,128]{1,0:T(8,128)S(1)}, u32[]{:S(2)}, u32[]{:S(2)}) collective-permute-start(f32[64,128]{1,0:T(8,128)S(1)} %get-tuple-element.61), channel_id=1, source_target_pairs={{1,16},{2,17},{3,18},{17,0},{18,1},{19,2},{33,48},{34,49},{35,50},... | collective-permute-start | bytes 98312 | tf_op jit(solution)/shard_map/ppermute | solution.py:393
  106.6 142.4 %collective-permute-start.32 = (f32[64,96,128]{2,1,0:T(8,128)S(1)}, f32[64,96,128]{2,1,0:T(8,128)}, u32[]{:S(2)}, u32[]{:S(2)}) collective-permute-start(f32[64,96,128]{2,1,0:T(8,128)S(1)} %get-tuple-element.65.refs_9_.refs_10_.refs_11_), channel_id=1, source_target_pairs={{0,16},{16,0},{32,48},{48,32},{64,80},{80,64},{96,112},{112,96},{1... | collective-permute-start | bytes 9437192 | tf_op jit(solution)/shard_map/ppermute | solution.py:402
  115.4 77.1 %collective-permute-start.6 = (f32[16,96,128]{2,1,0:T(8,128)S(1)}, f32[16,96,128]{2,1,0:T(8,128)S(1)}, u32[]{:S(2)}, u32[]{:S(2)}) collective-permute-start(f32[16,96,128]{2,1,0:T(8,128)S(1)} %get-tuple-element.52), channel_id=1, source_target_pairs={{16,32},{32,16},{48,64},{64,48},{80,96},{96,80},{17,33},{33,17},{4... | collective-permute-start | bytes 2359304 | tf_op jit(solution)/shard_map/ppermute | solution.py:387
  122.2 106.8 %collective-permute-start.7 = (f32[32,96,128]{2,1,0:T(8,128)S(1)}, f32[32,96,128]{2,1,0:T(8,128)S(1)}, u32[]{:S(2)}, u32[]{:S(2)}) collective-permute-start(f32[32,96,128]{2,1,0:T(8,128)S(1)} %get-tuple-element.53), channel_id=1, source_target_pairs={{16,32},{32,16},{48,64},{64,48},{80,96},{96,80},{17,33},{33,17},{4... | collective-permute-start | bytes 4718600 | tf_op jit(solution)/shard_map/ppermute | solution.py:395
  129.8 63.9 %collective-permute-start.11 = (f32[16,96,128]{2,1,0:T(8,128)S(1)}, f32[16,96,128]{2,1,0:T(8,128)S(1)}, u32[]{:S(2)}, u32[]{:S(2)}) collective-permute-start(f32[16,96,128]{2,1,0:T(8,128)S(1)} %collective-permute-done.10), channel_id=1, source_target_pairs={{0,48},{112,64},{1,49},{113,65},{2,50},{114,66},{3,51},{115,67},{4... | collective-permute-start | bytes 2359304 | tf_op jit(solution)/shard_map/ppermute | solution.py:389
  130.5 63.2 %collective-permute-start.13 = (f32[16,96,128]{2,1,0:T(8,128)S(1)}, f32[16,96,128]{2,1,0:T(8,128)S(1)}, u32[]{:S(2)}, u32[]{:S(2)}) collective-permute-start(f32[16,96,128]{2,1,0:T(8,128)S(1)} %collective-permute-done.12), channel_id=1, source_target_pairs={{0,16},{112,96},{1,17},{113,97},{2,18},{114,98},{3,19},{115,99},{4... | collective-permute-start | bytes 2359304 | tf_op jit(solution)/shard_map/ppermute | solution.py:389
  192.4 36.6 %collective-permute-start.9 = (f32[16,96,128]{2,1,0:T(8,128)S(1)}, f32[16,96,128]{2,1,0:T(8,128)S(1)}, u32[]{:S(2)}, u32[]{:S(2)}) collective-permute-start(f32[16,96,128]{2,1,0:T(8,128)S(1)} %collective-permute-done.8), channel_id=1, source_target_pairs={{0,80},{112,32},{1,81},{113,33},{2,82},{114,34},{3,83},{115,35},{4... | collective-permute-start | bytes 2359304 | tf_op jit(solution)/shard_map/ppermute | solution.py:389
  231.5 53.7 %collective-permute-start.26 = (f32[16,96,128]{2,1,0:T(8,128)}, f32[16,96,128]{2,1,0:T(8,128)S(1)}, u32[]{:S(2)}, u32[]{:S(2)}) collective-permute-start(f32[16,96,128]{2,1,0:T(8,128)} %get-tuple-element.73), channel_id=1, source_target_pairs={{96,0},{16,112},{97,1},{17,113},{98,2},{18,114},{99,3},{19,115},{1... | collective-permute-start | bytes 2359304 | tf_op jit(solution)/shard_map/ppermute | solution.py:385
  237.2 23.6 %collective-permute-start.18 = (f32[4,96,128]{2,1,0:T(8,128)S(1)}, f32[4,96,128]{2,1,0:T(8,128)S(1)}, u32[]{:S(2)}, u32[]{:S(2)}) collective-permute-start(f32[4,96,128]{2,1,0:T(8,128)S(1)} %get-tuple-element.66), channel_id=1, source_target_pairs={{0,4},{4,8},{8,12},{1,5},{5,9},{9,13},{2,6},{6,10},{10,14},{3,7},{... | collective-permute-start | bytes 589832 | tf_op jit(solution)/shard_map/ppermute | solution.py:386
  240.8 20.0 %collective-permute-start.19 = (f32[4,96,128]{2,1,0:T(8,128)S(1)}, f32[4,96,128]{2,1,0:T(8,128)S(1)}, u32[]{:S(2)}, u32[]{:S(2)}) collective-permute-start(f32[4,96,128]{2,1,0:T(8,128)S(1)} %get-tuple-element.67), channel_id=1, source_target_pairs={{4,0},{8,4},{12,8},{5,1},{9,5},{13,9},{6,2},{10,6},{14,10},{7,3},{... | collective-permute-start | bytes 589832 | tf_op jit(solution)/shard_map/ppermute | solution.py:386
  275.2 164.4 %collective-permute-start.50 = (f32[64,96,128]{2,1,0:T(8,128)S(1)}, f32[64,96,128]{2,1,0:T(8,128)S(1)}, u32[]{:S(2)}, u32[]{:S(2)}) collective-permute-start(f32[64,96,128]{2,1,0:T(8,128)S(1)} %get-tuple-element.84.refs_9_.refs_10_.refs_11_), channel_id=1, source_target_pairs={{0,16},{16,0},{32,48},{48,32},{64,80},{80,64},{96,112},{112,96},{1... | collective-permute-start | bytes 9437192 | tf_op jit(solution)/shard_map/ppermute | solution.py:402
  280.0 21.0 %collective-permute-start.30 = (f32[16,96,128]{2,1,0:T(8,128)}, f32[16,96,128]{2,1,0:T(8,128)S(1)}, u32[]{:S(2)}, u32[]{:S(2)}) collective-permute-start(f32[16,96,128]{2,1,0:T(8,128)} %get-tuple-element.73), channel_id=1, source_target_pairs={{32,0},{80,112},{33,1},{81,113},{34,2},{82,114},{35,3},{83,115},{3... | collective-permute-start | bytes 2359304 | tf_op jit(solution)/shard_map/ppermute | solution.py:385
  283.3 81.9 %collective-permute-start.24 = (f32[16,96,128]{2,1,0:T(8,128)S(1)}, f32[16,96,128]{2,1,0:T(8,128)S(1)}, u32[]{:S(2)}, u32[]{:S(2)}) collective-permute-start(f32[16,96,128]{2,1,0:T(8,128)S(1)} %get-tuple-element.71), channel_id=1, source_target_pairs={{16,32},{32,16},{48,64},{64,48},{80,96},{96,80},{17,33},{33,17},{4... | collective-permute-start | bytes 2359304 | tf_op jit(solution)/shard_map/ppermute | solution.py:387
  285.3 113.6 %collective-permute-start.25 = (f32[32,96,128]{2,1,0:T(8,128)S(1)}, f32[32,96,128]{2,1,0:T(8,128)S(1)}, u32[]{:S(2)}, u32[]{:S(2)}) collective-permute-start(f32[32,96,128]{2,1,0:T(8,128)S(1)} %copy-done.6), channel_id=1, source_target_pairs={{16,32},{32,16},{48,64},{64,48},{80,96},{96,80},{17,33},{33,17},{4... | collective-permute-start | bytes 4718600 | tf_op jit(solution)/shard_map/ppermute | solution.py:395
  291.6 74.3 %collective-permute-start.27 = (f32[16,96,128]{2,1,0:T(8,128)S(1)}, f32[16,96,128]{2,1,0:T(8,128)S(1)}, u32[]{:S(2)}, u32[]{:S(2)}) collective-permute-start(f32[16,96,128]{2,1,0:T(8,128)S(1)} %collective-permute-done.26), channel_id=1, source_target_pairs={{0,80},{112,32},{1,81},{113,33},{2,82},{114,34},{3,83},{115,35},{4... | collective-permute-start | bytes 2359304 | tf_op jit(solution)/shard_map/ppermute | solution.py:389
  301.1 64.8 %collective-permute-start.29 = (f32[16,96,128]{2,1,0:T(8,128)S(1)}, f32[16,96,128]{2,1,0:T(8,128)S(1)}, u32[]{:S(2)}, u32[]{:S(2)}) collective-permute-start(f32[16,96,128]{2,1,0:T(8,128)S(1)} %collective-permute-done.28), channel_id=1, source_target_pairs={{0,48},{112,64},{1,49},{113,65},{2,50},{114,66},{3,51},{115,67},{4... | collective-permute-start | bytes 2359304 | tf_op jit(solution)/shard_map/ppermute | solution.py:389
  400.5 27.0 %collective-permute-start.42 = (f32[16,96,128]{2,1,0:T(8,128)S(1)}, f32[16,96,128]{2,1,0:T(8,128)S(1)}, u32[]{:S(2)}, u32[]{:S(2)}) collective-permute-start(f32[16,96,128]{2,1,0:T(8,128)S(1)} %get-tuple-element.91), channel_id=1, source_target_pairs={{96,0},{16,112},{97,1},{17,113},{98,2},{18,114},{99,3},{19,115},{1... | collective-permute-start | bytes 2359304 | tf_op jit(solution)/shard_map/ppermute | solution.py:385
  415.9 21.6 %collective-permute-start.44 = (f32[16,96,128]{2,1,0:T(8,128)S(1)}, f32[16,96,128]{2,1,0:T(8,128)S(1)}, u32[]{:S(2)}, u32[]{:S(2)}) collective-permute-start(f32[16,96,128]{2,1,0:T(8,128)S(1)} %get-tuple-element.91), channel_id=1, source_target_pairs={{64,0},{48,112},{65,1},{49,113},{66,2},{50,114},{67,3},{51,115},{6... | collective-permute-start | bytes 2359304 | tf_op jit(solution)/shard_map/ppermute | solution.py:385
  416.6 22.2 %collective-permute-start.46 = (f32[16,96,128]{2,1,0:T(8,128)S(1)}, f32[16,96,128]{2,1,0:T(8,128)S(1)}, u32[]{:S(2)}, u32[]{:S(2)}) collective-permute-start(f32[16,96,128]{2,1,0:T(8,128)S(1)} %get-tuple-element.91), channel_id=1, source_target_pairs={{32,0},{80,112},{33,1},{81,113},{34,2},{82,114},{35,3},{83,115},{3... | collective-permute-start | bytes 2359304 | tf_op jit(solution)/shard_map/ppermute | solution.py:385
  423.2 23.1 %collective-permute-start.48 = (f32[16,96,128]{2,1,0:T(8,128)S(1)}, f32[16,96,128]{2,1,0:T(8,128)S(1)}, u32[]{:S(2)}, u32[]{:S(2)}) collective-permute-start(f32[16,96,128]{2,1,0:T(8,128)S(1)} %get-tuple-element.92), channel_id=1, source_target_pairs={{16,32},{32,16},{48,64},{64,48},{80,96},{96,80},{17,33},{33,17},{4... | collective-permute-start | bytes 2359304 | tf_op jit(solution)/shard_map/ppermute | solution.py:387
  427.5 131.5 %collective-permute-start.49 = (f32[24,96,128]{2,1,0:T(8,128)S(1)}, f32[24,96,128]{2,1,0:T(8,128)S(1)}, u32[]{:S(2)}, u32[]{:S(2)}) collective-permute-start(f32[24,96,128]{2,1,0:T(8,128)S(1)} %slice.47), channel_id=1, source_target_pairs={{16,32},{32,16},{48,64},{64,48},{80,96},{96,80},{17,33},{33,17},{4... | collective-permute-start | bytes 3538952 | tf_op jit(solution)/shard_map/ppermute | solution.py:395
  437.5 122.9 %collective-permute-start.43 = (f32[16,96,128]{2,1,0:T(8,128)S(1)}, f32[16,96,128]{2,1,0:T(8,128)S(1)}, u32[]{:S(2)}, u32[]{:S(2)}) collective-permute-start(f32[16,96,128]{2,1,0:T(8,128)S(1)} %collective-permute-done.42), channel_id=1, source_target_pairs={{0,80},{112,32},{1,81},{113,33},{2,82},{114,34},{3,83},{115,35},{4... | collective-permute-start | bytes 2359304 | tf_op jit(solution)/shard_map/ppermute | solution.py:389
  438.9 121.6 %collective-permute-start.45 = (f32[16,96,128]{2,1,0:T(8,128)S(1)}, f32[16,96,128]{2,1,0:T(8,128)S(1)}, u32[]{:S(2)}, u32[]{:S(2)}) collective-permute-start(f32[16,96,128]{2,1,0:T(8,128)S(1)} %collective-permute-done.44), channel_id=1, source_target_pairs={{0,48},{112,64},{1,49},{113,65},{2,50},{114,66},{3,51},{115,67},{4... | collective-permute-start | bytes 2359304 | tf_op jit(solution)/shard_map/ppermute | solution.py:389
  439.6 120.8 %collective-permute-start.47 = (f32[16,96,128]{2,1,0:T(8,128)S(1)}, f32[16,96,128]{2,1,0:T(8,128)S(1)}, u32[]{:S(2)}, u32[]{:S(2)}) collective-permute-start(f32[16,96,128]{2,1,0:T(8,128)S(1)} %collective-permute-done.46), channel_id=1, source_target_pairs={{0,16},{112,96},{1,17},{113,97},{2,18},{114,98},{3,19},{115,99},{4... | collective-permute-start | bytes 2359304 | tf_op jit(solution)/shard_map/ppermute | solution.py:389
  446.2 38.0 %collective-permute-start.51 = (f32[64,128]{1,0:T(8,128)S(1)}, f32[64,128]{1,0:T(8,128)S(1)}, u32[]{:S(2)}, u32[]{:S(2)}) collective-permute-start(f32[64,128]{1,0:T(8,128)S(1)} %get-tuple-element.94), channel_id=1, source_target_pairs={{0,17},{1,18},{2,19},{16,1},{17,2},{18,3},{32,49},{33,50},{34,51},... | collective-permute-start | bytes 98312 | tf_op jit(solution)/shard_map/ppermute | solution.py:393
  495.4 66.0 %collective-permute-start.41 = (f32[8,96,128]{2,1,0:T(8,128)S(1)}, f32[8,96,128]{2,1,0:T(8,128)S(1)}, u32[]{:S(2)}, u32[]{:S(2)}) collective-permute-start(f32[8,96,128]{2,1,0:T(8,128)S(1)} %slice.46), channel_id=1, source_target_pairs={{16,32},{32,16},{48,64},{64,48},{80,96},{96,80},{17,33},{33,17},{4... | collective-permute-start | bytes 1179656 | tf_op jit(solution)/shard_map/ppermute | solution.py:396
  (30 other events, 569.9 us)
